TPU v7x, 32 devices: a whole 2x2x4 slice. The times are simulated.
32 devices in a mesh: items: 8 (over y, x, core), heads: 4 (over z).
Axes of the slice: x: 2, y: 2, z: 4, core: 2. Of those that a mesh axis runs over, the one named last changes fastest.
Arguments:
- latents: bfloat16 [16384, 1024], P(('items', 'heads')), may hold values from -6 to 6
- pixels: bfloat16 [261, 131072], P(None, 'items'), may hold values from -6 to 6
- pixel_item: int32 [8, 16384], P('items'), may hold values from 0 to 3, never falling along the last dimension, each value on 1 to 6144 neighbouring positions
- cotangent: bfloat16 [16384, 1024], P(('items', 'heads')), may hold values from -6 to 6
- cross_query: float32 [1024, 1024], P(('items', 'heads')), may hold values from -0.1875 to 0.1875
- cross_key: float32 [261, 1024], P(None, ('items', 'heads')), may hold values from -0.375 to 0.375
- cross_value: float32 [261, 1024], P(None, ('items', 'heads')), may hold values from -0.375 to 0.375
- cross_out: float32 [1024, 1024], P(('items', 'heads')), may hold values from -4 to 4
- cross_up: float32 [1024, 1024], P('items', 'heads'), may hold values from -0.1875 to 0.1875
- cross_down: float32 [1024, 1024], P('heads', 'items'), may hold values from -0.1875 to 0.1875
- self_query: float32 [1024, 1024], P('items', 'heads'), may hold values from -0.1875 to 0.1875
- self_key: float32 [1024, 1024], P('items', 'heads'), may hold values from -0.1875 to 0.1875
- self_value: float32 [1024, 1024], P('items', 'heads'), may hold values from -0.1875 to 0.1875
- self_out: float32 [1024, 1024], P('heads', 'items'), may hold values from -3 to 3
- self_up: float32 [1024, 1024], P('items', 'heads'), may hold values from -0.1875 to 0.1875
- self_down: float32 [1024, 1024], P('heads', 'items'), may hold values from -0.1875 to 0.1875
- gain_cross: float32 [1024], P(('items', 'heads')), may hold values from 0.1 to 1.9
- gain_cross_mlp: float32 [1024], P(('items', 'heads')), may hold values from 0.1 to 1.9
- gain_self: float32 [1024], P(('items', 'heads')), may hold values from 0.1 to 1.9
- gain_self_mlp: float32 [1024], P(('items', 'heads')), may hold values from 0.1 to 1.9
Outputs:
- layer_out: bfloat16 [16384, 1024], P(('items', 'heads'))
- latents_grad: float32 [16384, 1024], P(('items', 'heads'))
- grad_cross_query: float32 [1024, 1024], P(('items', 'heads'))
- grad_cross_key: float32 [261, 1024], P(None, ('items', 'heads'))
- grad_cross_value: float32 [261, 1024], P(None, ('items', 'heads'))
- grad_cross_out: float32 [1024, 1024], P(('items', 'heads'))
- grad_cross_up: float32 [1024, 1024], P('items', 'heads')
- grad_cross_down: float32 [1024, 1024], P('heads', 'items')
- grad_self_query: float32 [1024, 1024], P('items', 'heads')
- grad_self_key: float32 [1024, 1024], P('items', 'heads')
- grad_self_value: float32 [1024, 1024], P('items', 'heads')
- grad_self_out: float32 [1024, 1024], P('heads', 'items')
- grad_self_up: float32 [1024, 1024], P('items', 'heads')
- grad_self_down: float32 [1024, 1024], P('heads', 'items')
- grad_gain_cross: float32 [1024], P(('items', 'heads'))
- grad_gain_cross_mlp: float32 [1024], P(('items', 'heads'))
- grad_gain_self: float32 [1024], P(('items', 'heads'))
- grad_gain_self_mlp: float32 [1024], P(('items', 'heads'))
Inputs may be any that keep to these rules, and one draw needn't show every extreme that they name: `pixel_item`: within each group the item numbers never fall along the pixel rows; every one of the 4 items has 1 to 6144 pixel rows, and some item has exactly 6144.
All inputs are finite; a program needn't handle non-finite values.
Results may differ from a plain program's by a relative error of at most 0.03.
Values may be sent and summed in bfloat16 or wider, within the bound.
A program may use at most 384 MiB of HBM per device.

v0:
```python
import math

import jax
import jax.numpy as jnp
from jax import lax
from jax.sharding import PartitionSpec as P

HEAD = 128
NLAT = 512


EPSILON = 1e-05
MASKED = -1e30
HIGHEST = lax.Precision.HIGHEST


def rounded(values):
    return values.astype(jnp.bfloat16)


def widened(values):
    return values.astype(jnp.float32)


def product(left_side, right_side):
    return jnp.dot(left_side, right_side, preferred_element_type=jnp.float32)


def product_tn(left_side, right_side):
    return lax.dot_general(
        left_side, right_side, (((0,), (0,)), ((), ())), preferred_element_type=jnp.float32
    )


def product_nt(left_side, right_side):
    return lax.dot_general(
        left_side, right_side, (((1,), (1,)), ((), ())), preferred_element_type=jnp.float32
    )


def norm_rows(values, gain_vec):
    centre = values - jnp.mean(values, axis=-1, keepdims=True)
    spread = jnp.mean(centre * centre, axis=-1, keepdims=True)
    return centre * lax.rsqrt(spread + EPSILON) * gain_vec


def norm_pixels(values):
    centre = values - jnp.mean(values, axis=0, keepdims=True)
    spread = jnp.mean(centre * centre, axis=0, keepdims=True)
    return centre * lax.rsqrt(spread + EPSILON)


def spread_rows(values):
    return lax.all_gather(values, "heads", axis=0, tiled=True)


def collect_rows(row_term, row_total):
    return lax.psum_scatter(
        row_term(jnp.int32(0), lax.axis_size("heads") * row_total).astype(jnp.bfloat16),
        "heads",
        scatter_dimension=0,
        tiled=True,
    ).astype(jnp.float32)


def norm_backward(residual, gain_vec, grad_normed):
    unused, norm_back = jax.vjp(norm_rows, residual, gain_vec)
    return norm_back(grad_normed)


def mlp_block(residual, gain_vec, up_part, down_part):
    own_rows = residual.shape[0]
    normed = rounded(norm_rows(residual, gain_vec))
    normed = spread_rows(normed)
    before = product(normed, up_part)
    hidden = rounded(jax.nn.gelu(before))

    def row_term(begin_row, row_count):
        return product(hidden, down_part)

    branch = collect_rows(row_term, own_rows)
    return (residual + branch, (normed, before, hidden))


def mlp_block_back(residual, gain_vec, up_part, down_part, saved, grad_out):
    normed, before, hidden = saved
    own_rows = residual.shape[0]
    grad_round = rounded(grad_out)
    grad_round = spread_rows(grad_round)
    grad_down = product_tn(hidden, grad_round)
    grad_hidden = product_nt(grad_round, down_part)
    unused, gelu_back = jax.vjp(jax.nn.gelu, before)
    grad_before = rounded(gelu_back(grad_hidden)[0])
    grad_up = product_tn(normed, grad_before)

    def row_term(begin_row, row_count):
        return product_nt(grad_before, up_part)

    grad_normed = collect_rows(row_term, own_rows)
    grad_residual, grad_gain = norm_backward(residual, gain_vec, grad_normed)
    return (grad_out + grad_residual, grad_up, grad_down, grad_gain)


def head_scores(query_rows, key_rows, scale_by):
    return (
        jnp.einsum("iqhd,ikhd->ihqk", query_rows, key_rows, preferred_element_type=jnp.float32)
        * scale_by
    )


def attention_block(residual, gain_vec, weight_set, scale_by):
    query_w, key_w, value_w, out_w = weight_set
    own_rows = residual.shape[0]
    normed = spread_rows(rounded(norm_rows(residual, gain_vec)))
    group_rows = normed.shape[0]
    shape_four = (group_rows // NLAT, NLAT, query_w.shape[1] // HEAD, HEAD)
    query_rows = rounded(product(normed, query_w)).reshape(shape_four)
    key_rows = rounded(product(normed, key_w)).reshape(shape_four)
    value_rows = rounded(product(normed, value_w)).reshape(shape_four)
    scores = head_scores(query_rows, key_rows, scale_by)
    row_top = jnp.max(scores, axis=-1, keepdims=True)
    raw_weights = jnp.exp(scores - row_top)
    row_total = jnp.sum(raw_weights, axis=-1, keepdims=True)
    weights = rounded(raw_weights / row_total)
    mixed_rows = jnp.einsum(
        "ihqk,ikhd->iqhd", weights, value_rows, preferred_element_type=jnp.float32
    )
    mixed_rows = rounded(mixed_rows.reshape(group_rows, query_w.shape[1]))

    def row_term(begin_row, row_count):
        return product(mixed_rows, out_w)

    branch = collect_rows(row_term, own_rows)
    saved = (normed, query_rows, key_rows, value_rows, row_top + jnp.log(row_total), mixed_rows)
    return (residual + branch, saved)


def attention_block_back(residual, gain_vec, weight_set, scale_by, saved, grad_out):
    query_w, key_w, value_w, out_w = weight_set
    normed, query_rows, key_rows, value_rows, log_total, mixed_rows = saved
    own_rows = residual.shape[0]
    group_rows = normed.shape[0]
    group_grad = spread_rows(rounded(grad_out))
    grad_out_w = product_tn(mixed_rows, group_grad)
    grad_mixed = rounded(product_nt(group_grad, out_w)).reshape(query_rows.shape)
    weights = jnp.exp(head_scores(query_rows, key_rows, scale_by) - log_total)
    grad_value = jnp.einsum(
        "ihqk,iqhd->ikhd", rounded(weights), grad_mixed, preferred_element_type=jnp.float32
    )
    grad_value = rounded(grad_value.reshape(group_rows, -1))
    grad_weights = jnp.einsum(
        "iqhd,ikhd->ihqk", grad_mixed, value_rows, preferred_element_type=jnp.float32
    )
    grad_scores = weights * (grad_weights - jnp.sum(grad_weights * weights, axis=-1, keepdims=True))
    grad_scores = rounded(grad_scores)
    grad_query = (
        jnp.einsum("ihqk,ikhd->iqhd", grad_scores, key_rows, preferred_element_type=jnp.float32)
        * scale_by
    )
    grad_query = rounded(grad_query.reshape(group_rows, -1))
    grad_key = (
        jnp.einsum("ihqk,iqhd->ikhd", grad_scores, query_rows, preferred_element_type=jnp.float32)
        * scale_by
    )
    grad_key = rounded(grad_key.reshape(group_rows, -1))
    grad_query_w = product_tn(normed, grad_query)
    grad_key_w = product_tn(normed, grad_key)
    grad_value_w = product_tn(normed, grad_value)

    def row_term(begin_row, row_count):
        from_query = product_nt(grad_query, query_w)
        from_key = product_nt(grad_key, key_w)
        from_value = product_nt(grad_value, value_w)
        return from_query + from_key + from_value

    grad_normed = collect_rows(row_term, own_rows)
    grad_residual, grad_gain = norm_backward(residual, gain_vec, grad_normed)
    return (grad_out + grad_residual, grad_query_w, grad_key_w, grad_value_w, grad_out_w, grad_gain)


def cross_block(residual, gain_vec, query_w, out_w, key_part, value_part, allowed, scale_by):
    normed = rounded(norm_rows(residual, gain_vec))
    query_rows = rounded(product(normed, query_w))
    scores = jnp.where(allowed, product_nt(query_rows, key_part) * scale_by, MASKED)
    row_top = jnp.max(scores, axis=-1, keepdims=True)
    raw_weights = jnp.exp(scores - row_top)
    row_total = jnp.sum(raw_weights, axis=-1, keepdims=True)
    weights = rounded(raw_weights / row_total)
    mixed_rows = rounded(product(weights, value_part))
    saved = (normed, query_rows, row_top + jnp.log(row_total), mixed_rows)
    return (residual + product(mixed_rows, out_w), saved)


def cross_block_back(
    residual,
    gain_vec,
    query_w,
    out_w,
    pixel_part,
    key_part,
    value_part,
    allowed,
    scale_by,
    saved,
    grad_out,
):
    normed, query_rows, log_total, mixed_rows = saved
    grad_round = rounded(grad_out)
    grad_out_w = product_tn(mixed_rows, grad_round)
    grad_mixed = rounded(product_nt(grad_round, out_w))
    weights = jnp.where(
        allowed, jnp.exp(product_nt(query_rows, key_part) * scale_by - log_total), 0.0
    )
    weights_low = rounded(weights)
    grad_weights = product_nt(grad_mixed, value_part)
    grad_scores = weights * (grad_weights - jnp.sum(grad_weights * weights, axis=-1, keepdims=True))
    grad_scores = rounded(grad_scores)
    grad_query = rounded(product(grad_scores, key_part) * scale_by)
    grad_query_w = product_tn(normed, grad_query)
    grad_normed = product_nt(grad_query, query_w)
    pixel_by_scores = product_nt(pixel_part, grad_scores)
    grad_key_w = jnp.dot(pixel_by_scores, widened(query_rows), precision=HIGHEST) * scale_by
    pixel_by_weights = product_nt(pixel_part, weights_low)
    grad_value_w = jnp.dot(pixel_by_weights, widened(grad_mixed), precision=HIGHEST)
    grad_residual, grad_gain = norm_backward(residual, gain_vec, grad_normed)
    return (grad_out + grad_residual, grad_query_w, grad_key_w, grad_value_w, grad_out_w, grad_gain)


def local(
    latents,
    pixels,
    pixel_item,
    cotangent,
    cross_query,
    cross_key,
    cross_value,
    cross_out,
    cross_up,
    cross_down,
    self_query,
    self_key,
    self_value,
    self_out,
    self_up,
    self_down,
    gain_cross,
    gain_cross_mlp,
    gain_self,
    gain_self_mlp,
):
    full_set = (
        lax.all_gather(rounded(cross_query), ("items", "heads"), axis=0, tiled=True),
        lax.all_gather(rounded(cross_key), ("items", "heads"), axis=1, tiled=True),
        lax.all_gather(rounded(cross_value), ("items", "heads"), axis=1, tiled=True),
        lax.all_gather(rounded(cross_out), ("items", "heads"), axis=0, tiled=True),
        lax.all_gather(rounded(gain_cross), ("items", "heads"), axis=0, tiled=True),
        lax.all_gather(rounded(gain_cross_mlp), ("items", "heads"), axis=0, tiled=True),
        lax.all_gather(rounded(gain_self), ("items", "heads"), axis=0, tiled=True),
        lax.all_gather(rounded(gain_self_mlp), ("items", "heads"), axis=0, tiled=True),
    )
    column_set = (
        lax.all_gather(rounded(self_query), "items", axis=0, tiled=True),
        lax.all_gather(rounded(self_key), "items", axis=0, tiled=True),
        lax.all_gather(rounded(self_value), "items", axis=0, tiled=True),
        lax.all_gather(rounded(self_out), "items", axis=1, tiled=True),
        lax.all_gather(rounded(cross_up), "items", axis=0, tiled=True),
        lax.all_gather(rounded(cross_down), "items", axis=1, tiled=True),
        lax.all_gather(rounded(self_up), "items", axis=0, tiled=True),
        lax.all_gather(rounded(self_down), "items", axis=1, tiled=True),
    )
    query_cross = full_set[0]
    key_cross = full_set[1]
    value_cross = full_set[2]
    out_cross = full_set[3]
    gain_list = [
        widened(full_set[4]),
        widened(full_set[5]),
        widened(full_set[6]),
        widened(full_set[7]),
    ]
    attention_set = (column_set[0], column_set[1], column_set[2], column_set[3])
    mlp_set = (column_set[4], column_set[5], column_set[6], column_set[7])
    own_rows = latents.shape[0]
    first_row = lax.axis_index("heads") * own_rows
    row_item = (first_row + jnp.arange(own_rows, dtype=jnp.int32)) // NLAT
    item_ids = pixel_item[0]
    pixel_part = rounded(norm_pixels(widened(pixels)))
    key_part = rounded(product_tn(pixel_part, key_cross))
    value_part = rounded(product_tn(pixel_part, value_cross))
    allowed = row_item[:, None] == item_ids[None, :]
    scale_cross = 1.0 / math.sqrt(key_cross.shape[1])
    scale_self = 1.0 / math.sqrt(HEAD)
    start_rows = widened(latents)
    after_cross, saved_cross = cross_block(
        start_rows, gain_list[0], query_cross, out_cross, key_part, value_part, allowed, scale_cross
    )
    after_mlp_one, saved_mlp_one = mlp_block(after_cross, gain_list[1], mlp_set[0], mlp_set[1])
    after_self, saved_self = attention_block(after_mlp_one, gain_list[2], attention_set, scale_self)
    final_rows, saved_mlp_two = mlp_block(after_self, gain_list[3], mlp_set[2], mlp_set[3])
    grad_final = widened(cotangent)
    grad_after_self, grad_self_up, grad_self_down, grad_gain_four = mlp_block_back(
        after_self, gain_list[3], mlp_set[2], mlp_set[3], saved_mlp_two, grad_final
    )
    (
        grad_after_mlp,
        grad_self_query,
        grad_self_key,
        grad_self_value,
        grad_self_out,
        grad_gain_three,
    ) = attention_block_back(
        after_mlp_one, gain_list[2], attention_set, scale_self, saved_self, grad_after_self
    )
    grad_after_cross, grad_cross_up, grad_cross_down, grad_gain_two = mlp_block_back(
        after_cross, gain_list[1], mlp_set[0], mlp_set[1], saved_mlp_one, grad_after_mlp
    )
    (
        latents_grad,
        grad_cross_query,
        grad_cross_key,
        grad_cross_value,
        grad_cross_out,
        grad_gain_one,
    ) = cross_block_back(
        start_rows,
        gain_list[0],
        query_cross,
        out_cross,
        pixel_part,
        key_part,
        value_part,
        allowed,
        scale_cross,
        saved_cross,
        grad_after_cross,
    )
    cross_grads = (
        lax.psum_scatter(grad_cross_query, ("items", "heads"), scatter_dimension=0, tiled=True),
        lax.psum_scatter(grad_cross_key, ("items", "heads"), scatter_dimension=1, tiled=True),
        lax.psum_scatter(grad_cross_value, ("items", "heads"), scatter_dimension=1, tiled=True),
        lax.psum_scatter(grad_cross_out, ("items", "heads"), scatter_dimension=0, tiled=True),
        lax.psum_scatter(grad_gain_one, ("items", "heads"), scatter_dimension=0, tiled=True),
        lax.psum_scatter(grad_gain_two, ("items", "heads"), scatter_dimension=0, tiled=True),
        lax.psum_scatter(grad_gain_three, ("items", "heads"), scatter_dimension=0, tiled=True),
        lax.psum_scatter(grad_gain_four, ("items", "heads"), scatter_dimension=0, tiled=True),
    )
    mlp_grads = (grad_cross_up, grad_cross_down, grad_self_up, grad_self_down)
    column_grads = (
        lax.psum_scatter(
            grad_self_query.astype(jnp.bfloat16), "items", scatter_dimension=0, tiled=True
        ).astype(jnp.float32),
        lax.psum_scatter(
            grad_self_key.astype(jnp.bfloat16), "items", scatter_dimension=0, tiled=True
        ).astype(jnp.float32),
        lax.psum_scatter(
            grad_self_value.astype(jnp.bfloat16), "items", scatter_dimension=0, tiled=True
        ).astype(jnp.float32),
        lax.psum_scatter(
            grad_self_out.astype(jnp.bfloat16), "items", scatter_dimension=1, tiled=True
        ).astype(jnp.float32),
        lax.psum_scatter(
            mlp_grads[0].astype(jnp.bfloat16), "items", scatter_dimension=0, tiled=True
        ).astype(jnp.float32),
        lax.psum_scatter(
            mlp_grads[1].astype(jnp.bfloat16), "items", scatter_dimension=1, tiled=True
        ).astype(jnp.float32),
        lax.psum_scatter(
            mlp_grads[2].astype(jnp.bfloat16), "items", scatter_dimension=0, tiled=True
        ).astype(jnp.float32),
        lax.psum_scatter(
            mlp_grads[3].astype(jnp.bfloat16), "items", scatter_dimension=1, tiled=True
        ).astype(jnp.float32),
    )
    return (
        rounded(final_rows),
        latents_grad,
        cross_grads[0],
        cross_grads[1],
        cross_grads[2],
        cross_grads[3],
        column_grads[4],
        column_grads[5],
        column_grads[0],
        column_grads[1],
        column_grads[2],
        column_grads[3],
        column_grads[6],
        column_grads[7],
        cross_grads[4],
        cross_grads[5],
        cross_grads[6],
        cross_grads[7],
    )


def solution(mesh):
    placed = (
        P(("items", "heads"), None),
        P(None, "items"),
        P("items", None),
        P(("items", "heads"), None),
        P(("items", "heads"), None),
        P(None, ("items", "heads")),
        P(None, ("items", "heads")),
        P(("items", "heads"), None),
        P("items", "heads"),
        P("heads", "items"),
        P("items", "heads"),
        P("items", "heads"),
        P("items", "heads"),
        P("heads", "items"),
        P("items", "heads"),
        P("heads", "items"),
        P(("items", "heads")),
        P(("items", "heads")),
        P(("items", "heads")),
        P(("items", "heads")),
    )
    return jax.shard_map(
        local,
        mesh=mesh,
        in_specs=placed,
        out_specs=(
            P(("items", "heads"), None),
            P(("items", "heads"), None),
            P(("items", "heads"), None),
            P(None, ("items", "heads")),
            P(None, ("items", "heads")),
            P(("items", "heads"), None),
            P("items", "heads"),
            P("heads", "items"),
            P("items", "heads"),
            P("items", "heads"),
            P("items", "heads"),
            P("heads", "items"),
            P("items", "heads"),
            P("heads", "items"),
            P(("items", "heads")),
            P(("items", "heads")),
            P(("items", "heads")),
            P(("items", "heads")),
        ),
        check_vma=False,
    )
```

profile of v0, /device:TPU:0, one launch (start us, length us, event | category | flops | bytes accessed | tf_op | source)
XLA Modules:
  0.0 2241.7 jit_solution(11751128950780707236)
XLA Ops:
  16.0 42.1 %all-reduce.9 = (bf16[1024]{0:T(1024)(128)(2,1)S(1)}, bf16[1024]{0:T(1024)(128)(2,1)S(1)}, bf16[1024]{0:T(1024)(128)(2,1)S(1)}, bf16[1024]{0:T(1024)(128)(2,1)}) all-reduce(bf16[1024]{0:T(1024)(128)(2,1)S(1)} %dynamic-update-slice, bf16[1024]{0:T(1024)(128)(2,1)S(1)} %dynamic-update-slice.1, ...), channel_id=1, replica_groups=mesh['items'=8,'heads'=4] {'items','heads'}, use_global_device_ids=true, to_apply=%add | all-reduce | flops 4096 | bytes 16384
  58.2 5.2 convert_reduce_fusion
  66.6 74.9 %all_gather.69 = bf16[261,1024]{0,1:T(8,128)(2,1)S(1)} all-gather(bf16[261,32]{0,1:T(8,128)(2,1)S(1)} %convert_element_type.290), channel_id=1, replica_groups=mesh['items'=8,'heads'=4] {'items','heads'}, dimensions={1}, use_global_device_ids=true | all-gather | bytes 551232 | tf_op jit(solution)/shard_map/all_gather | solution.py:254
  141.5 69.9 %all_gather.68 = bf16[261,1024]{0,1:T(8,128)(2,1)S(1)} all-gather(bf16[261,32]{0,1:T(8,128)(2,1)S(1)} %convert_element_type.287), channel_id=1, replica_groups=mesh['items'=8,'heads'=4] {'items','heads'}, dimensions={1}, use_global_device_ids=true | all-gather | bytes 551232 | tf_op jit(solution)/shard_map/all_gather | solution.py:253
  211.4 26.0 %convolution_convert_fusion = bf16[16384,1024]{1,0:T(8,128)(2,1)} fusion(bf16[261,1024]{0,1:T(8,128)(2,1)S(1)} %all_gather.68, bf16[261,16384]{1,0:T(8,128)(2,1)} %param.21, f32[16384]{0:T(1024)S(1)} %add_rsqrt_fusion, f32[16384]{0:T(1024)S(1)} %broadcast_multiply_fusion), kind=kOutput, calls=%fused_computation.7 | convolution fusion | flops 8791588864 | bytes 42772480 | tf_op jit(solution)/shard_map/dot_general | solution.py:30
  237.4 29.6 %fusion.30 = f32[16384,1024]{1,0:T(8,128)} fusion(bf16[261,1024]{0,1:T(8,128)(2,1)S(1)} %all_gather.69, bf16[261,16384]{1,0:T(8,128)(2,1)} %param.21, f32[16384]{0:T(1024)S(1)} %add_rsqrt_fusion, f32[16384]{0:T(1024)S(1)} %broadcast_multiply_fusion), kind=kOutput, calls=%fused_computation.68 | convolution fusion | flops 8774811648 | bytes 76326912 | tf_op jit(solution)/shard_map/dot_general | solution.py:30
  270.0 37.0 %fusion.109 = (f32[512]{0:T(512)}, f32[512,16384]{1,0:T(8,128)}, f32[512,16384]{1,0:T(8,128)}) fusion(s32[16384]{0:T(1024)S(1)} %bitcast.119, s32[512]{0:T(512)S(1)} %add_select_fusion, bf16[512,1024]{1,0:T(8,128)(2,1)S(1)} %convolution_convert_fusion.11, bf16[16384,1024]{1,0:T(8,128)(2,1)} %convolution_convert_fusion), kind=kOutput, calls=%fused_computation.194 | convolution fusion | flops 17213423616 | bytes 101781504 | tf_op jit(solution)/shard_map/dot_general | solution.py:36
  307.1 39.8 %online-softmax = f32[512,1024]{1,0:T(8,128)} custom-call(f32[512,16384]{1,0:T(8,128)} %get-tuple-element.35, f32[16384,1024]{1,0:T(8,128)} %fusion.30), custom_call_target="tpu_custom_call" | custom-call | tf_op online-softmax
  353.2 11.9 all_gather.74
  365.1 8.7 all_gather.73
  373.8 59.5 %all-gather.13.cloned.1.call-done = bf16[2048,1024]{1,0:T(8,128)(2,1)} async-done(((bf16[512,1024]{1,0:T(8,128)(2,1)}), bf16[2048,1024]{1,0:T(8,128)(2,1)}) %all-gather.13.cloned.1.call-update) | async-done | bytes 4194320 | tf_op jit(solution)/shard_map/all_gather | solution.py:54
  441.7 75.4 %reduce-scatter.25.cloned.1.call-done = bf16[512,1024]{1,0:T(8,128)(2,1)} async-done(((bf16[2048,1024]{1,0:T(8,128)(2,1)}), bf16[512,1024]{1,0:T(8,128)(2,1)}) %reduce-scatter.25.cloned.1.call-update) | async-done | bytes 1048592 | tf_op jit(solution)/shard_map/reduce_scatter | solution.py:58
  521.1 11.0 all_gather.80
  532.0 11.1 all_gather.77
  543.1 9.0 all_gather.79
  552.1 10.7 all_gather.78
  562.8 39.5 %all-gather.15.cloned.1.call-done = bf16[2048,1024]{1,0:T(8,128)(2,1)} async-done(((bf16[512,1024]{1,0:T(8,128)(2,1)}), bf16[2048,1024]{1,0:T(8,128)(2,1)}) %all-gather.15.cloned.1.call-update) | async-done | bytes 4194320 | tf_op jit(solution)/shard_map/all_gather | solution.py:54
  602.3 4.4 convolution_convert_fusion.7
  617.2 4.5 convolution_convert_fusion.9
  636.2 4.7 convolution_convert_fusion.4
  641.9 74.4 %reduce-scatter.27.cloned.1.call-done = bf16[512,1024]{1,0:T(8,128)(2,1)} async-done(((bf16[2048,1024]{1,0:T(8,128)(2,1)}), bf16[512,1024]{1,0:T(8,128)(2,1)}) %reduce-scatter.27.cloned.1.call-update) | async-done | bytes 1048592 | tf_op jit(solution)/shard_map/reduce_scatter | solution.py:58
  720.7 11.0 all_gather.84
  731.7 10.7 all_gather.83
  742.4 56.8 %all-gather.19.cloned.1.call-done = bf16[2048,1024]{1,0:T(8,128)(2,1)} async-done(((bf16[512,1024]{1,0:T(8,128)(2,1)}), bf16[2048,1024]{1,0:T(8,128)(2,1)}) %all-gather.19.cloned.1.call-update) | async-done | bytes 4194320 | tf_op jit(solution)/shard_map/all_gather | solution.py:54
  799.2 4.9 fusion.116
  804.1 76.5 %all-gather.17.cloned.1.call-done = bf16[2048,1024]{1,0:T(8,128)(2,1)} async-done(((bf16[512,1024]{1,0:T(8,128)(2,1)}), bf16[2048,1024]{1,0:T(8,128)(2,1)}) %all-gather.17.cloned.1.call-update) | async-done | bytes 4194320 | tf_op jit(solution)/shard_map/all_gather | solution.py:54
  880.6 6.7 fusion.54
  891.6 5.3 convolution_convert_fusion.3
  897.0 70.0 %reduce-scatter.31.cloned.1.call-done = bf16[512,1024]{1,0:T(8,128)(2,1)} async-done(((bf16[2048,1024]{1,0:T(8,128)(2,1)}), bf16[512,1024]{1,0:T(8,128)(2,1)}) %reduce-scatter.31.cloned.1.call-update) | async-done | bytes 1048592 | tf_op jit(solution)/shard_map/reduce_scatter | solution.py:58
  970.3 76.1 %reduce-scatter.29.cloned.1.call-done = bf16[512,1024]{1,0:T(8,128)(2,1)} async-done(((bf16[2048,1024]{1,0:T(8,128)(2,1)}), bf16[512,1024]{1,0:T(8,128)(2,1)}) %reduce-scatter.29.cloned.1.call-update) | async-done | bytes 1048592 | tf_op jit(solution)/shard_map/reduce_scatter | solution.py:58
  1046.4 4.1 fusion.111
  1053.5 81.1 %all-gather.21.cloned.1.call-done = bf16[2048,1024]{1,0:T(8,128)(2,1)} async-done(((bf16[512,1024]{1,0:T(8,128)(2,1)}), bf16[2048,1024]{1,0:T(8,128)(2,1)}) %all-gather.21.cloned.1.call-update) | async-done | bytes 4194320 | tf_op jit(solution)/shard_map/all_gather | solution.py:54
  1134.6 4.6 convolution_convert_fusion.6
  1141.3 3.7 copy.79
  1145.0 6.5 fusion.61
  1151.5 4.7 multiply_reduce_fusion.1
  1162.9 3.7 copy.81
  1166.7 3.7 copy.75
  1180.4 75.0 %reduce-scatter.33.cloned.1.call-done = bf16[512,1024]{1,0:T(8,128)(2,1)} async-done(((bf16[2048,1024]{1,0:T(8,128)(2,1)}), bf16[512,1024]{1,0:T(8,128)(2,1)}) %reduce-scatter.33.cloned.1.call-update) | async-done | bytes 1048592 | tf_op jit(solution)/shard_map/reduce_scatter | solution.py:58
  1261.4 81.3 %all-gather.23.cloned.1.call-done = bf16[2048,1024]{1,0:T(8,128)(2,1)} async-done(((bf16[512,1024]{1,0:T(8,128)(2,1)}), bf16[2048,1024]{1,0:T(8,128)(2,1)}) %all-gather.23.cloned.1.call-update) | async-done | bytes 4194320 | tf_op jit(solution)/shard_map/all_gather | solution.py:54
  1342.7 5.3 fusion.47
  1352.5 4.3 convolution_convert_fusion.12
  1357.9 4.4 convolution_convert_fusion.13
  1362.3 4.3 convolution_convert_fusion.14
  1368.8 4.3 convolution_convert_fusion.15
  1373.4 4.4 convolution_convert_fusion.16
  1377.8 4.5 convolution_convert_fusion.17
  1387.1 14.5 exponential_reduce_fusion
  1403.9 24.0 %reduce-scatter.35.cloned.1.call-done = bf16[512,1024]{1,0:T(8,128)(2,1)} async-done(((bf16[2048,1024]{1,0:T(8,128)(2,1)}), bf16[512,1024]{1,0:T(8,128)(2,1)}) %reduce-scatter.35.cloned.1.call-update) | async-done | bytes 1048592 | tf_op jit(solution)/shard_map/reduce_scatter | solution.py:58
  1434.2 44.7 %multiply_reduce_fusion = (f32[512]{0:T(512)S(1)}, f32[512,16384]{1,0:T(8,128)}) fusion(f32[512]{0:T(512)S(1)} %log_add_fusion.1, f32[512,16384]{1,0:T(8,128)} %get-tuple-element.45, s32[16384]{0:T(1024)S(1)} %bitcast.120, s32[512]{0:T(512)S(1)} %copy-done.40, bf16[512,1024]{1,0:T(8,128)(2,1)S(1)} %convolution_convert_fusion.10, f32[16384,1024]{1,0:T(8,128)} %fusion.30), kind=kOutput, calls=%fused_computation.3 | convolution fusion | flops 17246978048 | bytes 135337984 | tf_op jit(solution)/shard_map/dot_general | solution.py:36
  1478.9 28.0 %multiply_convert_fusion = bf16[512,16384]{1,0:T(8,128)(2,1)} fusion(f32[512,16384]{1,0:T(8,128)} %get-tuple-element.55, f32[512]{0:T(512)S(1)} %get-tuple-element.54, f32[512]{0:T(512)S(1)} %log_add_fusion.1, f32[512,16384]{1,0:T(8,128)} %get-tuple-element.45, s32[16384]{0:T(1024)S(1)} %bitcast.121, s32[512]{0:T(512)S(1)} %copy-done.40), kind=kLoop, calls=%fused_computation.2 | loop fusion | flops 58720256 | bytes 83957760 | tf_op jit(solution)/shard_map/convert_element_type | solution.py:18
  1507.0 12.4 fusion.28
  1522.5 17.0 fusion.6
  1542.6 4.9 fusion.89
  1547.6 24.9 %multiply_convert_fusion.2 = bf16[512,1024]{1,0:T(8,128)(2,1)S(1)} fusion(bf16[512,16384]{1,0:T(8,128)(2,1)} %multiply_convert_fusion, bf16[16384,1024]{1,0:T(8,128)(2,1)} %convolution_convert_fusion), kind=kOutput, calls=%fused_computation.94 | convolution fusion | flops 17180917760 | bytes 51380224 | tf_op jit(solution)/shard_map/dot_general | solution.py:26
  1583.3 30.7 %reduce-scatter.49.cloned.1.call-done = bf16[128,256]{1,0:T(8,128)(2,1)} async-done(((bf16[1024,256]{1,0:T(8,128)(2,1)}), bf16[128,256]{1,0:T(8,128)(2,1)}) %reduce-scatter.49.cloned.1.call-update) | async-done | bytes 65552 | tf_op jit(solution)/shard_map/reduce_scatter | solution.py:352
  1615.5 35.6 %reduce-scatter.47.cloned.1.call-done = bf16[128,256]{1,0:T(8,128)(2,1)} async-done(((bf16[1024,256]{1,0:T(8,128)(2,1)}), bf16[128,256]{1,0:T(8,128)(2,1)}) %reduce-scatter.47.cloned.1.call-update) | async-done | bytes 65552 | tf_op jit(solution)/shard_map/reduce_scatter | solution.py:349
  1652.5 35.7 %reduce-scatter.55.cloned.1.call-done = bf16[128,256]{1,0:T(8,128)(2,1)} async-done(((bf16[1024,256]{1,0:T(8,128)(2,1)}), bf16[128,256]{1,0:T(8,128)(2,1)}) %reduce-scatter.55.cloned.1.call-update) | async-done | bytes 65552
  1689.9 35.6 %reduce-scatter.45.cloned.1.call-done = bf16[128,256]{1,0:T(8,128)(2,1)} async-done(((bf16[1024,256]{1,0:T(8,128)(2,1)}), bf16[128,256]{1,0:T(8,128)(2,1)}) %reduce-scatter.45.cloned.1.call-update) | async-done | bytes 65552 | tf_op jit(solution)/shard_map/reduce_scatter | solution.py:361
  1732.7 39.6 %all-reduce.8 = (f32[1024]{0:T(1024)S(1)}, f32[1024]{0:T(1024)S(1)}, f32[1024]{0:T(1024)S(1)}, f32[1024]{0:T(1024)S(1)}) all-reduce(f32[1024]{0:T(1024)S(1)} %get-tuple-element.22, f32[1024]{0:T(1024)S(1)} %copy-done.76, f32[1024]{0:T(1024)S(1)} %copy-done.75, ...), channel_id=20, replica_groups=mesh['items'=8,'heads'=4] {'items','heads'}, use_global_device_ids=true, to_apply=%region_43.44.clone | all-reduce | flops 4096 | bytes 32768
  1778.2 51.1 %reduce-scatter.39.cloned.1.call-done = f32[261,32]{0,1:T(8,128)} async-done(((f32[261,1024]{0,1:T(8,128)}), f32[261,32]{0,1:T(8,128)}) %reduce-scatter.39.cloned.1.call-update) | async-done | bytes 33424 | tf_op jit(solution)/shard_map/reduce_scatter | solution.py:339
  1829.3 102.8 %reduce-scatter.41.cloned.1.call-done = f32[261,32]{0,1:T(8,128)} async-done(((f32[261,1024]{0,1:T(8,128)}), f32[261,32]{0,1:T(8,128)}) %reduce-scatter.41.cloned.1.call-update) | async-done | bytes 33424 | tf_op jit(solution)/shard_map/reduce_scatter | solution.py:340
  1932.1 151.2 %reduce-scatter.43.cloned.1.call-done = f32[32,1024]{1,0:T(8,128)} async-done(((f32[1024,1024]{1,0:T(8,128)}), f32[32,1024]{1,0:T(8,128)}) %reduce-scatter.43.cloned.1.call-update) | async-done | bytes 131088 | tf_op jit(solution)/shard_map/reduce_scatter | solution.py:341
  2083.3 151.4 %reduce-scatter.37.cloned.1.call-done = f32[32,1024]{1,0:T(8,128)} async-done(((f32[1024,1024]{1,0:T(8,128)}), f32[32,1024]{1,0:T(8,128)}) %reduce-scatter.37.cloned.1.call-update) | async-done | bytes 131088 | tf_op jit(solution)/shard_map/reduce_scatter | solution.py:338
  (350 shorter events, 154.8 us)
Async XLA Ops:
  7.2 7.5 copy-start.9
  7.2 50.9 %copy-start.60 = (f32[261,32]{0,1:T(8,128)S(1)}, f32[261,32]{0,1:T(8,128)}, u32[]{:S(2)}) copy-start(f32[261,32]{0,1:T(8,128)} %param.25) | copy-start | bytes 100228
  7.2 51.0 %copy-start.61 = (f32[261,32]{0,1:T(8,128)S(1)}, f32[261,32]{0,1:T(8,128)}, u32[]{:S(2)}) copy-start(f32[261,32]{0,1:T(8,128)} %param.26) | copy-start | bytes 100228
  7.2 259.8 %all-gather.9.cloned.1.call-start = ((), (), s32[]{:S(2)}) async-start(), calls=%async_computation.18 | async-start | bytes 2162688 | tf_op jit(solution)/shard_map/all_gather | solution.py:252
  8.9 338.0 %all-gather.11.cloned.1.call-start = ((), (), s32[]{:S(2)}) async-start(), calls=%async_computation.19 | async-start | bytes 2162688 | tf_op jit(solution)/shard_map/all_gather | solution.py:255
  10.5 422.8 %all-gather.13.cloned.1.call-start = ((), (), s32[]{:S(2)}) async-start(), calls=%async_computation.20 | async-start | bytes 5242880 | tf_op jit(solution)/shard_map/all_gather | solution.py:54
  13.2 256.8 %copy-start.39 = (s32[512]{0:T(512)}, s32[512]{0:T(512)S(1)}, u32[]{:S(2)}) copy-start(s32[512]{0:T(512)S(1)} %add_select_fusion) | copy-start | bytes 6148
  14.7 252.4 %copy-start.64 = (f32[512]{0:T(512)}, f32[512]{0:T(512)S(1)}, u32[]{:S(2)}) copy-start(f32[512]{0:T(512)S(1)} %broadcast_multiply_fusion.4) | copy-start | bytes 6148
  15.1 48.3 %copy-start.68 = (f32[512]{0:T(512)}, f32[512]{0:T(512)S(1)}, u32[]{:S(2)}) copy-start(f32[512]{0:T(512)S(1)} %fusion.55) | copy-start | bytes 6148
  15.1 251.9 %copy-start.72 = (f32[512]{0:T(512)}, f32[512]{0:T(512)S(1)}, u32[]{:S(2)}) copy-start(f32[512]{0:T(512)S(1)} %fusion.97) | copy-start | bytes 6148
  58.1 208.9 %copy-start.62 = (f32[1024]{0:T(1024)}, f32[1024]{0:T(1024)S(1)}, u32[]{:S(2)}) copy-start(f32[1024]{0:T(1024)S(1)} %convert_element_type.281) | copy-start | bytes 12292
  58.2 293.5 %copy-start.56 = (f32[1024]{0:T(1024)}, f32[1024]{0:T(1024)S(1)}, u32[]{:S(2)}) copy-start(f32[1024]{0:T(1024)S(1)} %convert_element_type.295) | copy-start | bytes 12292
  58.2 6.0 copy-start.1
  64.2 173.2 %copy-start.43 = (f32[16384]{0:T(1024)}, f32[16384]{0:T(1024)S(1)}, u32[]{:S(2)}) copy-start(f32[16384]{0:T(1024)S(1)} %broadcast_multiply_fusion) | copy-start | bytes 196612
  66.6 170.8 %copy-start.46 = (f32[16384]{0:T(1024)}, f32[16384]{0:T(1024)S(1)}, u32[]{:S(2)}) copy-start(f32[16384]{0:T(1024)S(1)} %add_rsqrt_fusion) | copy-start | bytes 196612
  270.0 37.1 %copy-start.41 = (bf16[512,1024]{1,0:T(8,128)(2,1)}, bf16[512,1024]{1,0:T(8,128)(2,1)S(1)}, u32[]{:S(2)}) copy-start(bf16[512,1024]{1,0:T(8,128)(2,1)S(1)} %convolution_convert_fusion.11) | copy-start | bytes 3145732
  353.1 163.9 %reduce-scatter.25.cloned.1.call-start = ((), (), s32[]{:S(2)}) async-start(), calls=%async_computation.21 | async-start | bytes 5242880 | tf_op jit(solution)/shard_map/reduce_scatter | solution.py:58
  365.1 71.6 %copy-start.45 = (bf16[256,1024]{1,0:T(8,128)(2,1)}, bf16[256,1024]{1,0:T(8,128)(2,1)S(1)}, u32[]{:S(2)}) copy-start(bf16[256,1024]{1,0:T(8,128)(2,1)S(1)} %all_gather.74) | copy-start | bytes 1572868
  373.8 62.9 %copy-start.33 = (bf16[1024,256]{1,0:T(8,128)(2,1)}, bf16[1024,256]{1,0:T(8,128)(2,1)S(1)}, u32[]{:S(2)}) copy-start(bf16[1024,256]{1,0:T(8,128)(2,1)S(1)} %all_gather.73) | copy-start | bytes 1572868
  441.6 160.7 %all-gather.15.cloned.1.call-start = ((), (), s32[]{:S(2)}) async-start(), calls=%async_computation.22 | async-start | bytes 5242880 | tf_op jit(solution)/shard_map/all_gather | solution.py:54
  520.9 195.4 %reduce-scatter.27.cloned.1.call-start = ((), (), s32[]{:S(2)}) async-start(), calls=%async_computation.23 | async-start | bytes 5242880 | tf_op jit(solution)/shard_map/reduce_scatter | solution.py:58
  552.1 50.2 %copy-start.36 = (bf16[1024,256]{1,0:T(8,128)(2,1)}, bf16[1024,256]{1,0:T(8,128)(2,1)S(1)}, u32[]{:S(2)}) copy-start(bf16[1024,256]{1,0:T(8,128)(2,1)S(1)} %all_gather.79) | copy-start | bytes 1572868
  640.9 158.3 %all-gather.19.cloned.1.call-start = ((), (), s32[]{:S(2)}) async-start(), calls=%async_computation.26 | async-start | bytes 5242880 | tf_op jit(solution)/shard_map/all_gather | solution.py:54
  641.6 238.9 %all-gather.17.cloned.1.call-start = ((), (), s32[]{:S(2)}) async-start(), calls=%async_computation.24 | async-start | bytes 5242880 | tf_op jit(solution)/shard_map/all_gather | solution.py:54
  720.6 246.4 %reduce-scatter.31.cloned.1.call-start = ((), (), s32[]{:S(2)}) async-start(), calls=%async_computation.27 | async-start | bytes 5242880 | tf_op jit(solution)/shard_map/reduce_scatter | solution.py:58
  880.6 7.7 copy-start.38
  891.5 154.9 %reduce-scatter.29.cloned.1.call-start = ((), (), s32[]{:S(2)}) async-start(), calls=%async_computation.25 | async-start | bytes 5242880 | tf_op jit(solution)/shard_map/reduce_scatter | solution.py:58
  896.9 237.7 %all-gather.21.cloned.1.call-start = ((), (), s32[]{:S(2)}) async-start(), calls=%async_computation.28 | async-start | bytes 5242880 | tf_op jit(solution)/shard_map/all_gather | solution.py:54
  1053.2 202.2 %reduce-scatter.33.cloned.1.call-start = ((), (), s32[]{:S(2)}) async-start(), calls=%async_computation.29 | async-start | bytes 5242880 | tf_op jit(solution)/shard_map/reduce_scatter | solution.py:58
  1145.0 6.5 copy-start.12
  1145.0 6.5 copy-start.24
  1145.0 11.2 slice-start
  1162.9 7.4 copy-start.20
  1180.0 162.7 %all-gather.23.cloned.1.call-start = ((), (), s32[]{:S(2)}) async-start(), calls=%async_computation.30 | async-start | bytes 5242880 | tf_op jit(solution)/shard_map/all_gather | solution.py:54
  1261.3 87.7 %copy-start.34 = (bf16[1024,256]{1,0:T(8,128)(2,1)S(1)}, bf16[1024,256]{1,0:T(8,128)(2,1)}, u32[]{:S(2)}) copy-start(bf16[1024,256]{1,0:T(8,128)(2,1)} %copy-done.33) | copy-start | bytes 1572868
  1261.3 166.5 %reduce-scatter.35.cloned.1.call-start = ((), (), s32[]{:S(2)}) async-start(), calls=%async_computation.31 | async-start | bytes 5242880 | tf_op jit(solution)/shard_map/reduce_scatter | solution.py:58
  1352.4 5.5 copy-start.28
  1352.4 224.6 %reduce-scatter.59.cloned.1.call-start = ((), (), s32[]{:S(2)}) async-start(), calls=%async_computation.43 | async-start | bytes 589824
  1357.8 220.8 %reduce-scatter.53.cloned.1.call-start = ((), (), s32[]{:S(2)}) async-start(), calls=%async_computation.40 | async-start | bytes 589824 | tf_op jit(solution)/shard_map/reduce_scatter | solution.py:367
  1362.3 6.6 copy-start.26
  1362.3 217.9 %reduce-scatter.57.cloned.1.call-start = ((), (), s32[]{:S(2)}) async-start(), calls=%async_computation.42 | async-start | bytes 589824
  1368.8 213.0 %reduce-scatter.51.cloned.1.call-start = ((), (), s32[]{:S(2)}) async-start(), calls=%async_computation.39 | async-start | bytes 589824 | tf_op jit(solution)/shard_map/reduce_scatter | solution.py:355
  1373.2 240.8 %reduce-scatter.49.cloned.1.call-start = ((), (), s32[]{:S(2)}) async-start(), calls=%async_computation.38 | async-start | bytes 589824 | tf_op jit(solution)/shard_map/reduce_scatter | solution.py:352
  1377.8 273.3 %reduce-scatter.47.cloned.1.call-start = ((), (), s32[]{:S(2)}) async-start(), calls=%async_computation.37 | async-start | bytes 589824 | tf_op jit(solution)/shard_map/reduce_scatter | solution.py:349
  1382.3 306.0 %reduce-scatter.55.cloned.1.call-start = ((), (), s32[]{:S(2)}) async-start(), calls=%async_computation.41 | async-start | bytes 589824
  1387.0 338.5 %reduce-scatter.45.cloned.1.call-start = ((), (), s32[]{:S(2)}) async-start(), calls=%async_computation.36 | async-start | bytes 589824 | tf_op jit(solution)/shard_map/reduce_scatter | solution.py:361
  1387.1 14.5 copy-start.30
  1387.1 14.5 copy-start.79
  1401.6 26.2 %copy-start.3 = (f32[512,1024]{1,0:T(8,128)S(1)}, f32[512,1024]{1,0:T(8,128)}, u32[]{:S(2)}) copy-start(f32[512,1024]{1,0:T(8,128)} %copy-done.2) | copy-start | bytes 6291460
  1401.6 26.2 %copy-start.57 = (f32[1024]{0:T(1024)S(1)}, f32[1024]{0:T(1024)}, u32[]{:S(2)}) copy-start(f32[1024]{0:T(1024)} %copy-done.56) | copy-start | bytes 12292
  1401.7 26.2 %copy-start.59 = (f32[512]{0:T(512)S(1)}, f32[512]{0:T(512)}, u32[]{:S(2)}) copy-start(f32[512]{0:T(512)} %copy-done.58) | copy-start | bytes 6148
  1403.8 25.9 %copy-start.71 = (f32[512]{0:T(512)S(1)}, f32[512]{0:T(512)}, u32[]{:S(2)}) copy-start(f32[512]{0:T(512)} %copy-done.70) | copy-start | bytes 6148
  1403.8 25.9 %copy-start.67 = (f32[512]{0:T(512)S(1)}, f32[512]{0:T(512)}, u32[]{:S(2)}) copy-start(f32[512]{0:T(512)} %copy-done.66) | copy-start | bytes 6148
  1403.8 425.5 %reduce-scatter.39.cloned.1.call-start = ((), (), s32[]{:S(2)}) async-start(), calls=%async_computation.33 | async-start | bytes 1622016 | tf_op jit(solution)/shard_map/reduce_scatter | solution.py:339
  1478.9 28.0 %copy-start.44 = (f32[16384]{0:T(1024)S(1)}, f32[16384]{0:T(1024)}, u32[]{:S(2)}) copy-start(f32[16384]{0:T(1024)} %copy-done.43) | copy-start | bytes 196612
  1478.9 28.0 %copy-start.47 = (f32[16384]{0:T(1024)S(1)}, f32[16384]{0:T(1024)}, u32[]{:S(2)}) copy-start(f32[16384]{0:T(1024)} %copy-done.46) | copy-start | bytes 196612
  1506.9 12.4 copy-start.42
  1522.5 409.6 %reduce-scatter.41.cloned.1.call-start = ((), (), s32[]{:S(2)}) async-start(), calls=%async_computation.34 | async-start | bytes 1622016 | tf_op jit(solution)/shard_map/reduce_scatter | solution.py:340
  1542.5 540.8 %reduce-scatter.43.cloned.1.call-start = ((), (), s32[]{:S(2)}) async-start(), calls=%async_computation.35 | async-start | bytes 4325376 | tf_op jit(solution)/shard_map/reduce_scatter | solution.py:341
  1547.5 26.0 %copy-start.10 = (bf16[512,1024]{1,0:T(8,128)(2,1)S(1)}, bf16[512,1024]{1,0:T(8,128)(2,1)}, u32[]{:S(2)}) copy-start(bf16[512,1024]{1,0:T(8,128)(2,1)} %param.20) | copy-start | bytes 3145732
  1547.5 26.0 %copy-start.63 = (f32[1024]{0:T(1024)S(1)}, f32[1024]{0:T(1024)}, u32[]{:S(2)}) copy-start(f32[1024]{0:T(1024)} %copy-done.62) | copy-start | bytes 12292
  1547.5 26.0 %copy-start.65 = (f32[512]{0:T(512)S(1)}, f32[512]{0:T(512)}, u32[]{:S(2)}) copy-start(f32[512]{0:T(512)} %copy-done.64) | copy-start | bytes 6148
  1547.5 26.0 %copy-start.73 = (f32[512]{0:T(512)S(1)}, f32[512]{0:T(512)}, u32[]{:S(2)}) copy-start(f32[512]{0:T(512)} %copy-done.72) | copy-start | bytes 6148
  1547.5 687.2 %reduce-scatter.37.cloned.1.call-start = ((), (), s32[]{:S(2)}) async-start(), calls=%async_computation.32 | async-start | bytes 4325376 | tf_op jit(solution)/shard_map/reduce_scatter | solution.py:338
  (48 other events, 103.8 us)
Sparse Core Ops, SparseCore 0:
  11.5 59.0 all-gather.8
  74.1 56.2 all-gather.10
  353.2 80.0 all-gather.12
  441.7 75.2 reduce-scatter.24
  521.0 81.2 all-gather.14
  641.0 75.2 reduce-scatter.26
  717.9 81.2 all-gather.18
  801.3 79.2 all-gather.16
  891.6 75.2 reduce-scatter.30
  969.1 77.2 reduce-scatter.28
  1053.3 81.2 all-gather.20
  1180.1 75.2 reduce-scatter.32
  1261.4 81.2 all-gather.22
  1352.5 75.2 reduce-scatter.34
  1430.8 34.5 reduce-scatter.58
  1468.3 34.1 reduce-scatter.52
  1505.5 34.1 reduce-scatter.56
  1542.5 34.1 reduce-scatter.50
  1579.8 34.1 reduce-scatter.48
  1616.9 34.1 reduce-scatter.46
  1654.1 34.1 reduce-scatter.54
  1691.4 34.1 reduce-scatter.44
  1731.3 97.9 reduce-scatter.38
  1835.0 97.0 reduce-scatter.40
  1934.9 148.3 reduce-scatter.42
  2086.0 148.6 reduce-scatter.36
where the time goes:
time: 2250 us; the launch traced here: 2240 us
  waiting for transfers between devices  1380 us (61%)
  matrix products  335 us (15%)
  blocking collectives  310 us (14%)
  other arithmetic  103 us (5%)
  local copies, waits for them, and re-layouts  51 us (2%)
  Pallas kernels  39.8 us (2%)
    reduce_scatter x6, waiting for transfers between devices, collect_rows(): lax.psum_scatter(row_term(jnp.int32(0), lax.axis_size('heads') * row_tota...  395 us
    all_gather x6, waiting for transfers between devices, spread_rows(): return lax.all_gather(values, 'heads', axis=0, tiled=True)  395 us
    reduce_scatter x1, waiting for transfers between devices, local(): lax.psum_scatter(grad_cross_query, ('items', 'heads'), scatter_dimension=...  151 us
    reduce_scatter x1, waiting for transfers between devices, local(): lax.psum_scatter(grad_cross_out, ('items', 'heads'), scatter_dimension=0,...  151 us
    dot_general x14, matrix products, product_nt(): lax.dot_general(left_side, right_side, (((1,), (1,)), ((), ())), preferre...  145 us
    reduce_scatter x1, waiting for transfers between devices, local(): lax.psum_scatter(grad_cross_value, ('items', 'heads'), scatter_dimension=...  103 us
    dot_general x12, matrix products, product_tn(): lax.dot_general(left_side, right_side, (((0,), (0,)), ((), ())), preferre...  95.7 us
    unnamed x2, blocking collectives  81.7 us
  transfers between devices with their start and end apart: 26, of which 20 were waited for; matrix products, arithmetic and copies ran while one was open for 15% of the time, Pallas kernels for 2%

commit v1 on v0

v1 whole, which is shorter than its diff:
```python
import math

import jax
import jax.numpy as jnp
from jax import lax
from jax.sharding import PartitionSpec as P

HEAD = 128
NLAT = 512
PIX_MOST = 6144
LANE = 128

EPSILON = 1e-05
MASKED = -1e30
ALL = ("items", "heads")


def rounded(values):
    return values.astype(jnp.bfloat16)


def widened(values):
    return values.astype(jnp.float32)


def product(left_side, right_side):
    return jnp.dot(left_side, right_side, preferred_element_type=jnp.float32)


def product_tn(left_side, right_side):
    return lax.dot_general(
        left_side, right_side, (((0,), (0,)), ((), ())), preferred_element_type=jnp.float32
    )


def product_nt(left_side, right_side):
    return lax.dot_general(
        left_side, right_side, (((1,), (1,)), ((), ())), preferred_element_type=jnp.float32
    )


def split_parts(values):
    high = rounded(values)
    return high, rounded(values - widened(high))


def split_product(left_f32, right_bf16, form=product):
    high, low = split_parts(left_f32)
    return form(high, right_bf16) + form(low, right_bf16)


def norm_rows(values, gain_vec):
    centre = values - jnp.mean(values, axis=-1, keepdims=True)
    spread = jnp.mean(centre * centre, axis=-1, keepdims=True)
    return centre * lax.rsqrt(spread + EPSILON) * gain_vec


def norm_pixels(values):
    centre = values - jnp.mean(values, axis=0, keepdims=True)
    spread = jnp.mean(centre * centre, axis=0, keepdims=True)
    return centre * lax.rsqrt(spread + EPSILON)


def norm_backward(residual, gain_vec, grad_normed):
    unused, norm_back = jax.vjp(norm_rows, residual, gain_vec)
    return norm_back(grad_normed)


def assemble(blocks, kind, items, heads):
    count, first, second = blocks.shape
    if kind == "rows":
        return blocks.reshape(count * first, second)
    if kind == "cols":
        return blocks.transpose(1, 0, 2).reshape(first, count * second)
    if kind == "ih":
        parts = blocks.reshape(items, heads, first, second).transpose(0, 2, 1, 3)
        return parts.reshape(items * first, heads * second)
    parts = blocks.reshape(items, heads, first, second).transpose(1, 2, 0, 3)
    return parts.reshape(heads * first, items * second)


def disassemble(whole, kind, items, heads):
    count = items * heads
    rows, cols = whole.shape
    if kind == "rows":
        return whole.reshape(count, rows // count, cols)
    if kind == "cols":
        return whole.reshape(rows, count, cols // count).transpose(1, 0, 2)
    if kind == "ih":
        parts = whole.reshape(items, rows // items, heads, cols // heads).transpose(0, 2, 1, 3)
        return parts.reshape(count, rows // items, cols // heads)
    parts = whole.reshape(heads, rows // heads, items, cols // items).transpose(2, 0, 1, 3)
    return parts.reshape(count, rows // heads, cols // items)


WEIGHT_KINDS = (
    "rows",
    "cols",
    "cols",
    "rows",
    "ih",
    "hi",
    "ih",
    "ih",
    "ih",
    "hi",
    "ih",
    "hi",
)


WIDTH = 1024
ROW_TILE = 16


def to_rows(flat):
    count, size = flat.shape
    rows = -(-size // (WIDTH * ROW_TILE)) * ROW_TILE
    flat = jnp.pad(flat, ((0, 0), (0, rows * WIDTH - size)))
    return flat.reshape(count, rows, WIDTH)


def pack(pieces):
    blocks, places, row = [], [], 0
    for piece in pieces:
        block = to_rows(piece)
        places.append((row, piece.shape[1]))
        blocks.append(block)
        row += block.shape[1]
    extra = packed_rows(row) - row
    if extra:
        blocks.append(jnp.zeros((pieces[0].shape[0], extra, WIDTH), pieces[0].dtype))
    return jnp.concatenate(blocks, axis=1), places


def packed_rows(rows):
    return -(-rows // 128) * 128


def unpack(packed, place):
    row, size = place
    rows = -(-size // WIDTH)
    return packed[:, row : row + rows, :].reshape(packed.shape[0], rows * WIDTH)[:, :size]


def gather_weights(weights, gains, items, heads):
    count = items * heads
    pieces = [rounded(w).reshape(1, -1) for w in weights]
    pieces.append(rounded(jnp.concatenate(gains)).reshape(1, -1))
    packed, places = pack(pieces)
    local_rows = packed.shape[1]
    gathered = lax.all_gather(packed[0], ALL, axis=0, tiled=True).reshape(count, local_rows, WIDTH)
    whole_weights = []
    for w, kind, place in zip(weights, WEIGHT_KINDS, places):
        blocks = unpack(gathered, place).reshape((count,) + w.shape)
        whole_weights.append(assemble(blocks, kind, items, heads))
    gain_blocks = unpack(gathered, places[-1]).reshape(count, len(gains), -1)
    whole_gains = [widened(gain_blocks[:, k, :].reshape(-1)) for k in range(len(gains))]
    return whole_weights, whole_gains


def reduce_grads(weight_grads, gain_grads, items, heads):
    count = items * heads
    pieces = []
    for g, kind in zip(weight_grads, WEIGHT_KINDS):
        pieces.append(rounded(disassemble(g, kind, items, heads)).reshape(count, -1))
    gain_stack = jnp.stack([g.reshape(count, -1) for g in gain_grads], axis=1)
    pieces.append(rounded(gain_stack).reshape(count, -1))
    packed, places = pack(pieces)
    local_rows = packed.shape[1]
    mine = lax.psum_scatter(
        packed.reshape(count * local_rows, WIDTH), ALL, scatter_dimension=0, tiled=True
    ).reshape(1, local_rows, WIDTH)
    out = [widened(unpack(mine, place)[0]) for place in places[:-1]]
    gain_part = widened(unpack(mine, places[-1])[0]).reshape(len(gain_grads), -1)
    out += [gain_part[k] for k in range(len(gain_grads))]
    return out


def mlp_block(residual, gain_vec, up_w, down_w):
    normed = rounded(norm_rows(residual, gain_vec))
    before = product(normed, up_w)
    hidden = rounded(jax.nn.gelu(before))
    return residual + product(hidden, down_w), (normed, before, hidden)


def mlp_block_back(residual, gain_vec, up_w, down_w, saved, grad_out):
    normed, before, hidden = saved
    grad_round = rounded(grad_out)
    grad_down = product_tn(hidden, grad_round)
    grad_hidden = product_nt(grad_round, down_w)
    unused, gelu_back = jax.vjp(jax.nn.gelu, before)
    grad_before = rounded(gelu_back(grad_hidden)[0])
    grad_up = product_tn(normed, grad_before)
    grad_normed = product_nt(grad_before, up_w)
    grad_residual, grad_gain = norm_backward(residual, gain_vec, grad_normed)
    return grad_out + grad_residual, grad_up, grad_down, grad_gain


def exchange_rows(rows, split):
    if split == 1:
        return [rows]
    heads = lax.axis_size("heads")
    out = [rows]
    for shift in range(1, split):
        pairs = []
        for h in range(heads):
            base, pos = (h // split) * split, h % split
            pairs.append((h, base + (pos - shift) % split))
        out.append(lax.ppermute(rows, "heads", pairs))
    return out


def return_rows(parts, split):
    total = parts[0]
    heads = lax.axis_size("heads")
    for shift in range(1, split):
        pairs = []
        for h in range(heads):
            base, pos = (h // split) * split, h % split
            pairs.append((h, base + (pos + shift) % split))
        total = total + lax.ppermute(parts[shift], "heads", pairs)
    return total


def attention_block(residual, gain_vec, weight_set, split):
    query_w, key_w, value_w, out_w = weight_set
    rows = residual.shape[0]
    heads_n = query_w.shape[1] // HEAD
    normed = rounded(norm_rows(residual, gain_vec))
    query_rows = rounded(product(normed, query_w))
    key_rows = rounded(product(normed, key_w))
    value_rows = rounded(product(normed, value_w))
    key_all = jnp.concatenate(exchange_rows(key_rows, split), axis=0)
    value_all = jnp.concatenate(exchange_rows(value_rows, split), axis=0)
    keys = key_all.shape[0]
    q4 = query_rows.reshape(rows, heads_n, HEAD)
    k4 = key_all.reshape(keys, heads_n, HEAD)
    v4 = value_all.reshape(keys, heads_n, HEAD)
    scores = jnp.einsum("qhd,khd->hqk", q4, k4, preferred_element_type=jnp.float32) * (
        1.0 / math.sqrt(HEAD)
    )
    row_top = jnp.max(scores, axis=-1, keepdims=True)
    raw_weights = jnp.exp(scores - row_top)
    row_total = jnp.sum(raw_weights, axis=-1, keepdims=True)
    weights = raw_weights / row_total
    mixed = jnp.einsum("hqk,khd->qhd", rounded(weights), v4, preferred_element_type=jnp.float32)
    mixed = rounded(mixed.reshape(rows, heads_n * HEAD))
    saved = (normed, q4, k4, v4, weights, mixed)
    return residual + product(mixed, out_w), saved


def attention_block_back(residual, gain_vec, weight_set, split, saved, grad_out):
    query_w, key_w, value_w, out_w = weight_set
    normed, q4, k4, v4, weights, mixed = saved
    rows = residual.shape[0]
    keys = k4.shape[0]
    scale = 1.0 / math.sqrt(HEAD)
    grad_round = rounded(grad_out)
    grad_out_w = product_tn(mixed, grad_round)
    grad_mixed = rounded(product_nt(grad_round, out_w)).reshape(q4.shape)
    grad_value = jnp.einsum(
        "hqk,qhd->khd", rounded(weights), grad_mixed, preferred_element_type=jnp.float32
    ).reshape(keys, -1)
    grad_weights = jnp.einsum("qhd,khd->hqk", grad_mixed, v4, preferred_element_type=jnp.float32)
    grad_scores = weights * (grad_weights - jnp.sum(grad_weights * weights, axis=-1, keepdims=True))
    grad_scores = rounded(grad_scores)
    grad_query = jnp.einsum("hqk,khd->qhd", grad_scores, k4, preferred_element_type=jnp.float32)
    grad_query = rounded((grad_query * scale).reshape(rows, -1))
    grad_key = jnp.einsum("hqk,qhd->khd", grad_scores, q4, preferred_element_type=jnp.float32)
    grad_key = (grad_key * scale).reshape(keys, -1)
    if split > 1:
        grad_key = return_rows(jnp.split(grad_key, split, axis=0), split)
        grad_value = return_rows(jnp.split(grad_value, split, axis=0), split)
    grad_key = rounded(grad_key)
    grad_value = rounded(grad_value)
    grad_query_w = product_tn(normed, grad_query)
    grad_key_w = product_tn(normed, grad_key)
    grad_value_w = product_tn(normed, grad_value)
    grad_normed = (
        product_nt(grad_query, query_w)
        + product_nt(grad_key, key_w)
        + product_nt(grad_value, value_w)
    )
    grad_residual, grad_gain = norm_backward(residual, gain_vec, grad_normed)
    return (grad_out + grad_residual, grad_query_w, grad_key_w, grad_value_w, grad_out_w, grad_gain)


def pixel_window(pixels, item_ids, item):
    count = pixels.shape[1]
    width = min(count, -(-PIX_MOST // LANE) * LANE + LANE)
    start = jnp.sum((item_ids < item).astype(jnp.int32))
    first = jnp.clip((start // LANE) * LANE, 0, count - width)
    window = lax.dynamic_slice_in_dim(pixels, first, width, axis=1)
    ids = lax.dynamic_slice_in_dim(item_ids, first, width, axis=0)
    return window, ids == item


def cross_block(residual, gain_vec, query_w, key_w, value_w, out_w, pixel_norm, allowed):
    scale = 1.0 / math.sqrt(query_w.shape[1])
    normed = rounded(norm_rows(residual, gain_vec))
    query_rows = rounded(product(normed, query_w))
    query_keyed = rounded(product_nt(query_rows, key_w) * scale)
    scores = jnp.where(allowed[None, :], product(query_keyed, pixel_norm), MASKED)
    row_top = jnp.max(scores, axis=-1, keepdims=True)
    raw_weights = jnp.exp(scores - row_top)
    row_total = jnp.sum(raw_weights, axis=-1, keepdims=True)
    weights = raw_weights / row_total
    weights_low = rounded(weights)
    pixel_mix = product_nt(weights_low, pixel_norm)
    mixed = rounded(split_product(pixel_mix, value_w))
    saved = (normed, query_rows, weights, pixel_mix, mixed)
    return residual + product(mixed, out_w), saved


def cross_block_back(
    residual, gain_vec, query_w, key_w, value_w, out_w, pixel_norm, saved, grad_out
):
    normed, query_rows, weights, pixel_mix, mixed = saved
    scale = 1.0 / math.sqrt(query_w.shape[1])
    grad_round = rounded(grad_out)
    grad_out_w = product_tn(mixed, grad_round)
    grad_mixed = rounded(product_nt(grad_round, out_w))
    grad_keyed = rounded(product_nt(grad_mixed, value_w))
    grad_weights = product(grad_keyed, pixel_norm)
    grad_scores = weights * (grad_weights - jnp.sum(grad_weights * weights, axis=-1, keepdims=True))
    grad_scores = rounded(grad_scores)
    score_mix = product_nt(grad_scores, pixel_norm)
    grad_query = rounded(split_product(score_mix, key_w) * scale)
    grad_query_w = product_tn(normed, grad_query)
    grad_key_w = split_product(score_mix, query_rows, product_tn) * scale
    grad_value_w = split_product(pixel_mix, grad_mixed, product_tn)
    grad_normed = product_nt(grad_query, query_w)
    grad_residual, grad_gain = norm_backward(residual, gain_vec, grad_normed)
    return (grad_out + grad_residual, grad_query_w, grad_key_w, grad_value_w, grad_out_w, grad_gain)


def local(latents, pixels, pixel_item, cotangent, *params):
    weights, gains = params[:12], params[12:]
    items = lax.axis_size("items")
    heads = lax.axis_size("heads")
    rows = latents.shape[0]
    split = max(1, NLAT // rows)
    (
        query_cross,
        key_cross,
        value_cross,
        out_cross,
        up_cross,
        down_cross,
        query_self,
        key_self,
        value_self,
        out_self,
        up_self,
        down_self,
    ), gain_list = gather_weights(weights, gains, items, heads)
    attention_set = (query_self, key_self, value_self, out_self)

    item = (lax.axis_index("heads") * rows) // NLAT
    window, allowed = pixel_window(pixels, pixel_item[0], item)
    pixel_norm = rounded(norm_pixels(widened(window)))

    start_rows = widened(latents)
    after_cross, saved_cross = cross_block(
        start_rows, gain_list[0], query_cross, key_cross, value_cross, out_cross, pixel_norm, allowed
    )
    after_mlp_one, saved_mlp_one = mlp_block(after_cross, gain_list[1], up_cross, down_cross)
    after_self, saved_self = attention_block(after_mlp_one, gain_list[2], attention_set, split)
    final_rows, saved_mlp_two = mlp_block(after_self, gain_list[3], up_self, down_self)

    grad_final = widened(cotangent)
    grad_after_self, grad_self_up, grad_self_down, grad_gain_four = mlp_block_back(
        after_self, gain_list[3], up_self, down_self, saved_mlp_two, grad_final
    )
    (
        grad_after_mlp,
        grad_self_query,
        grad_self_key,
        grad_self_value,
        grad_self_out,
        grad_gain_three,
    ) = attention_block_back(
        after_mlp_one, gain_list[2], attention_set, split, saved_self, grad_after_self
    )
    grad_after_cross, grad_cross_up, grad_cross_down, grad_gain_two = mlp_block_back(
        after_cross, gain_list[1], up_cross, down_cross, saved_mlp_one, grad_after_mlp
    )
    (
        latents_grad,
        grad_cross_query,
        grad_cross_key,
        grad_cross_value,
        grad_cross_out,
        grad_gain_one,
    ) = cross_block_back(
        start_rows,
        gain_list[0],
        query_cross,
        key_cross,
        value_cross,
        out_cross,
        pixel_norm,
        saved_cross,
        grad_after_cross,
    )
    weight_grads = (
        grad_cross_query,
        grad_cross_key,
        grad_cross_value,
        grad_cross_out,
        grad_cross_up,
        grad_cross_down,
        grad_self_query,
        grad_self_key,
        grad_self_value,
        grad_self_out,
        grad_self_up,
        grad_self_down,
    )
    gain_grads = (grad_gain_one, grad_gain_two, grad_gain_three, grad_gain_four)
    reduced = reduce_grads(weight_grads, gain_grads, items, heads)
    shaped = [r.reshape(w.shape) for r, w in zip(reduced[:12], weights)]
    shaped += [r.reshape(g.shape) for r, g in zip(reduced[12:], gains)]
    return (rounded(final_rows), latents_grad, *shaped)


def solution(mesh):
    weight_specs = (
        P(ALL, None),
        P(None, ALL),
        P(None, ALL),
        P(ALL, None),
        P("items", "heads"),
        P("heads", "items"),
        P("items", "heads"),
        P("items", "heads"),
        P("items", "heads"),
        P("heads", "items"),
        P("items", "heads"),
        P("heads", "items"),
    )
    gain_specs = (P(ALL),) * 4
    placed = (P(ALL, None), P(None, "items"), P("items", None), P(ALL, None)) + weight_specs + gain_specs
    return jax.shard_map(
        local,
        mesh=mesh,
        in_specs=placed,
        out_specs=(P(ALL, None), P(ALL, None)) + weight_specs + gain_specs,
        check_vma=False,
    )
```

time: 2250 us -> 836 us (0.37)
  waiting for transfers between devices: 1380 us -> 378 us
  blocking collectives: 310 us -> 0 us
  local copies, waits for them, and re-layouts: 51 us -> 243 us
  matrix products: 335 us -> 148 us
  other arithmetic: 103 us -> 39.8 us
  Pallas kernels: 39.8 us -> 0 us
    reduce_scatter x15 -> x1, waiting for transfers between devices: 953 us -> 232 us  [reduce_grads(): lax.psum_scatter(packed.reshape(count * local_rows, WIDTH), ALL, scatter_...]
    all_gather x8 -> x1, waiting for transfers between devices: 395 us -> 146 us  [gather_weights(): lax.all_gather(packed[0], ALL, axis=0, tiled=True)]
    all_gather x10 -> x0, blocking collectives: 229 us -> none  [the longest x1 74.9 us: local(): lax.all_gather(rounded(cross_value), ('items', 'heads'), axis=1, tiled=True)]
    dot_general x14 -> x12, matrix products: 145 us -> 39.3 us  [product_nt(): lax.dot_general(left_side, right_side, (((1,), (1,)), ((), ())), preferre...]
    unnamed x2 -> x0, blocking collectives: 81.7 us -> none
    dot_general x12 -> x14, matrix products: 95.7 us -> 35.9 us  [product_tn(): lax.dot_general(left_side, right_side, (((0,), (0,)), ((), ())), preferre...]
    convert_element_type x4 -> x24, local copies, waits for them, and re-layouts: 13.1 us -> 61.6 us  [rounded(): return values.astype(jnp.bfloat16)]
    unnamed x1 -> x0, Pallas kernels: 39.8 us -> none
  transfers between devices with their start and end apart: 26 -> 2, of which waited for: 20 -> 2; matrix products, arithmetic and copies ran while one was open for 15% -> 2% of each run, Pallas kernels for 2% -> 0%
where the time goes in v1:
time: 836 us; the launch traced here: 827 us
  waiting for transfers between devices  378 us (45%)
  local copies, waits for them, and re-layouts  243 us (29%)
  matrix products  148 us (18%)
  other arithmetic  39.8 us (5%)
  between operations  18.5 us (2%)
    reduce_scatter x1, waiting for transfers between devices, reduce_grads(): lax.psum_scatter(packed.reshape(count * local_rows, WIDTH), ALL, scatter_...  232 us
    all_gather x1, waiting for transfers between devices, gather_weights(): lax.all_gather(packed[0], ALL, axis=0, tiled=True)  146 us
    convert_element_type x24, local copies, waits for them, and re-layouts, rounded(): return values.astype(jnp.bfloat16)  61.6 us
    unnamed x226, local copies, waits for them, and re-layouts  58.3 us
    dot_general x16, matrix products, product(): return jnp.dot(left_side, right_side, preferred_element_type=jnp.float32)  47.8 us
    dot_general x12, matrix products, product_nt(): lax.dot_general(left_side, right_side, (((1,), (1,)), ((), ())), preferre...  39.3 us
    dot_general x14, matrix products, product_tn(): lax.dot_general(left_side, right_side, (((0,), (0,)), ((), ())), preferre...  35.9 us
    transpose x5, local copies, waits for them, and re-layouts, assemble(): parts = blocks.reshape(items, heads, first, second).transpose(0, 2, 1, 3)  21.6 us
  transfers between devices with their start and end apart: 2, of which 2 were waited for; matrix products, arithmetic and copies ran while one was open for 2% of the time, Pallas kernels for 0%

profile of v1, /device:TPU:0, one launch (start us, length us, event | category | flops | bytes accessed | tf_op | source)
XLA Modules:
  0.0 827.4 jit_solution(5867987884034927918)
XLA Ops:
  20.3 3.3 convert_reduce_fusion
  24.3 3.7 fusion.6
  28.0 145.6 %all-gather.3.cloned.1.call-done = bf16[1,12288,1024]{2,1,0:T(8,128)(2,1)} async-done(((bf16[1,384,1024]{2,1,0:T(8,128)(2,1)}), bf16[1,12288,1024]{2,1,0:T(8,128)(2,1)}) %all-gather.3.cloned.1.call-update) | async-done | bytes 25165840 | tf_op jit(solution)/shard_map/all_gather | solution.py:152
  176.5 15.1 %fusion.184 = (bf16[32,32,1024]{2,1,0:T(8,128)(2,1)}, bf16[32,32,1024]{2,1,0:T(8,128)(2,1)}, bf16[32,32,1024]{2,1,0:T(8,128)(2,1)}, bf16[32,32,1024]{2,1,0:T(8,1...) fusion(bf16[32,384,1024]{2,1,0:T(8,128)(2,1)} %bitcast.347), kind=kLoop, calls=%fused_computation.299 | loop fusion | bytes 41943040 | tf_op jit(solution)/shard_map/slice | solution.py:143
  194.6 2.7 reshape.595
  199.2 2.7 reshape.592
  203.7 4.2 reshape_reshape_reshape.33
  207.9 4.4 copy.98
  212.3 2.6 reshape_reshape_reshape.32
  214.9 4.3 copy.97
  219.3 3.0 convolution_convert_fusion.5
  222.2 10.1 %select_reduce_fusion = (f32[512]{0:T(512)S(1)}, f32[512,6272]{1,0:T(8,128)}) fusion(pred[6272]{0:T(1024)(128)(4,1)S(1)} %compare_reduce_fusion, f32[6272]{0:T(1024)S(1)} %add_rsqrt_fusion, f32[6272]{0:T(1024)S(1)} %broadcast_multiply_fusion, bf16[261,16384]{1,0:T(8,128)(2,1)} %param.21, s32[]{:T(128)S(6)} %min.4, ...), kind=kOutput, calls=%fused_computation.4 | convolution fusion | flops 1963195392 | bytes 17798276 | tf_op jit(solution)/shard_map/dot_general | solution.py:27
  232.4 7.3 fusion.2
  240.7 6.5 fusion.10
  260.0 4.4 reshape_reshape_reshape.38
  264.4 4.3 copy.107
  268.7 4.2 reshape_reshape_reshape.39
  272.9 4.3 copy.108
  277.2 4.2 reshape_reshape_reshape.37
  281.3 4.3 copy.106
  285.6 4.3 reshape_reshape_reshape.36
  290.0 4.3 copy.101
  294.3 4.3 reshape_reshape_reshape.35
  298.6 4.3 copy.100
  302.9 4.3 reshape_reshape_reshape.34
  307.3 4.3 copy.99
  311.6 4.3 fusion.127
  322.7 2.4 copy.152
  325.1 7.5 fusion.188
  332.6 4.7 fusion.100
  342.5 2.9 convert_bitcast_fusion
  349.9 3.0 convolution_convert_fusion
  360.6 5.3 fusion.103
  365.9 4.6 multiply_reduce_fusion.1
  371.0 2.5 multiply_convert_fusion.1
  386.5 3.1 fusion.29
  389.7 2.9 convert_bitcast_fusion.5
  394.2 2.9 convolution_convert_fusion.1
  401.3 2.6 convolution_convert_fusion.2
  405.4 13.4 %multiply_reduce_fusion = (f32[512]{0:T(512)S(1)}, f32[512,6272]{1,0:T(8,128)}) fusion(f32[512]{0:T(512)S(1)} %copy-done.84, f32[512]{0:T(512)S(1)} %copy-done.82, f32[512,6272]{1,0:T(8,128)} %get-tuple-element.101, pred[6272]{0:T(1024)(128)(4,1)S(1)} %compare_reduce_fusion, f32[6272]{0:T(1024)S(1)} %add_rsqrt_fusion, f32[6272]{0:T(1024)S(1)} %broadcast_multiply_fusion, ...), kind=kOutput, calls=%fused_computation.2 | convolution fusion | flops 1972695552 | bytes 30647428 | tf_op jit(solution)/shard_map/dot_general | solution.py:27
  418.8 13.0 %fusion.8 = f32[512,261]{0,1:T(8,128)S(1)} fusion(f32[512,6272]{1,0:T(8,128)} %get-tuple-element.116, f32[512]{0:T(512)S(1)} %get-tuple-element.115, f32[6272]{0:T(1024)S(1)} %add_rsqrt_fusion, f32[6272]{0:T(1024)S(1)} %broadcast_multiply_fusion, bf16[261,16384]{1,0:T(8,128)(2,1)} %param.21, s32[]{:T(128)S(6)} %min.4, f32[512,6272]{1,0:T(8,128)} %get-tuple-element.101, ...), kind=kOutput, calls=%fused_computation.18 | convolution fusion | flops 1702095360 | bytes 29598852 | tf_op jit(solution)/shard_map/dot_general | solution.py:37
  436.0 2.7 fusion.38
  438.6 2.8 convolution_convert_fusion.3
  442.7 2.6 copy.139
  449.6 4.2 convert_element_type.579
  453.7 4.5 convert_element_type.573
  458.2 3.4 copy.129
  461.6 4.4 convert_element_type.575
  468.4 2.8 convert_bitcast_fusion.1
  472.7 4.2 convert_element_type.571
  476.9 4.2 convert_bitcast_fusion.2
  481.0 4.3 convert_element_type.568
  489.6 4.2 convert_element_type.559
  493.7 4.5 convert_element_type.553
  498.2 3.3 copy.122
  501.5 4.3 convert_element_type.555
  510.4 2.7 reshape.611
  514.7 2.6 convert_bitcast_fusion.3
  517.3 2.6 convert_bitcast_fusion.4
  520.0 4.4 convert_element_type.562
  524.3 4.7 convert_element_type.565
  568.9 3.7 add_add_fusion.4
  573.8 2.5 add_convert_fusion
  576.3 232.4 %reduce-scatter.2.cloned.1.call-done = bf16[384,1024]{1,0:T(8,128)(2,1)} async-done(((bf16[12288,1024]{1,0:T(8,128)(2,1)}), bf16[384,1024]{1,0:T(8,128)(2,1)}) %reduce-scatter.2.cloned.1.call-update) | async-done | bytes 786448 | tf_op jit(solution)/shard_map/reduce_scatter | solution.py:171
  (376 shorter events, 154.7 us)
Async XLA Ops:
  7.2 8.1 copy-start.64
  7.2 8.2 copy-start.65
  7.2 8.2 copy-start.66
  7.2 8.3 %copy-start.67 = (f32[256,128]{1,0:T(8,128)S(1)}, f32[256,128]{1,0:T(8,128)}, u32[]{:S(2)}) copy-start(f32[256,128]{1,0:T(8,128)} %param.35) | copy-start | bytes 393220
  7.2 8.3 %copy-start.68 = (f32[32,1024]{1,0:T(8,128)S(1)}, f32[32,1024]{1,0:T(8,128)}, u32[]{:S(2)}) copy-start(f32[32,1024]{1,0:T(8,128)} %param.24) | copy-start | bytes 393220
  7.2 8.4 %copy-start.69 = (f32[32,1024]{1,0:T(8,128)S(1)}, f32[32,1024]{1,0:T(8,128)}, u32[]{:S(2)}) copy-start(f32[32,1024]{1,0:T(8,128)} %param.27) | copy-start | bytes 393220
  7.3 166.4 %all-gather.3.cloned.1.call-start = ((), (), s32[]{:S(2)}) async-start(), calls=%async_computation.2 | async-start | bytes 25952256 | tf_op jit(solution)/shard_map/all_gather | solution.py:152
  14.3 2.5 copy-start.70
  15.8 7.8 copy-start.2
  16.7 792.0 %reduce-scatter.2.cloned.1.call-start = ((), (), s32[]{:S(2)}) async-start(), calls=%async_computation.1 | async-start | bytes 25952256 | tf_op jit(solution)/shard_map/reduce_scatter | solution.py:171
  23.8 195.4 %copy-start.73 = (f32[512]{0:T(512)}, f32[512]{0:T(512)S(1)}, u32[]{:S(2)}) copy-start(f32[512]{0:T(512)S(1)} %broadcast_multiply_fusion.4) | copy-start | bytes 6148
  24.2 152.3 %copy-start.75 = (f32[512]{0:T(512)}, f32[512]{0:T(512)S(1)}, u32[]{:S(2)}) copy-start(f32[512]{0:T(512)S(1)} %fusion.37) | copy-start | bytes 6148
  24.3 195.0 %copy-start.77 = (f32[512]{0:T(512)}, f32[512]{0:T(512)S(1)}, u32[]{:S(2)}) copy-start(f32[512]{0:T(512)S(1)} %fusion.158) | copy-start | bytes 6148
  192.1 27.2 %copy-start.71 = (f32[1024]{0:T(1024)}, f32[1024]{0:T(1024)S(1)}, u32[]{:S(2)}) copy-start(f32[1024]{0:T(1024)S(1)} %reshape.619) | copy-start | bytes 12292
  207.9 4.4 copy-start.5
  219.2 3.0 copy-start.22
  222.2 10.1 %copy-start.29 = (bf16[512,1024]{1,0:T(8,128)(2,1)}, bf16[512,1024]{1,0:T(8,128)(2,1)S(1)}, u32[]{:S(2)}) copy-start(bf16[512,1024]{1,0:T(8,128)(2,1)S(1)} %convolution_convert_fusion.5) | copy-start | bytes 3145732
  232.4 7.3 copy-start.81
  232.4 8.3 %copy-start.4 = (f32[512,6272]{1,0:T(8,128)S(1)}, f32[512,6272]{1,0:T(8,128)}, u32[]{:S(2)}) copy-start(f32[512,6272]{1,0:T(8,128)} %get-tuple-element.101) | copy-start | bytes 38535172
  240.7 6.5 copy-start.83
  240.7 6.5 copy-start.24
  250.9 3.7 copy-start.8
  250.9 2.4 copy-start.41
  251.3 3.3 copy-start.79
  311.6 4.3 copy-start.47
  311.6 4.3 copy-start.56
  315.9 2.3 copy-start.49
  332.6 4.8 copy-start.51
  338.8 14.2 %copy-start.6 = (f32[512,1024]{1,0:T(8,128)}, f32[512,1024]{1,0:T(8,128)S(1)}, u32[]{:S(2)}) copy-start(f32[512,1024]{1,0:T(8,128)S(1)} %get-tuple-element.109) | copy-start | bytes 6291460
  338.8 2.3 copy-start.52
  342.5 2.9 copy-start.87
  342.5 2.9 copy-start.39
  360.6 5.4 copy-start.58
  360.6 5.4 copy-start.91
  360.6 10.0 %slice-start = ((s8[8388608]{0:T(1024)(128)(4,1)}), s8[4194304]{0:T(1024)(128)(4,1)S(1)}, s32[]{:S(2)}) async-start(s8[8388608]{0:T(1024)(128)(4,1)} %bitcast.350), calls=%async_computation.3 | async-start | bytes 8388608
  365.9 14.3 %copy-start.55 = (bf16[8,128,512]{2,1,0:T(8,128)(2,1)}, bf16[8,128,512]{2,1,0:T(8,128)(2,1)S(1)}, u32[]{:S(2)}) copy-start(bf16[8,128,512]{2,1,0:T(8,128)(2,1)S(1)} %fusion.103) | copy-start | bytes 3145732
  365.9 5.1 slice-start.1
  371.0 2.5 copy-start.34
  375.0 3.7 copy-start.59
  375.0 2.3 copy-start.50
  375.8 2.9 copy-start.61
  384.3 2.2 copy-start.90
  389.6 2.9 copy-start.9
  389.7 2.9 copy-start.42
  389.7 2.9 copy-start.80
  401.3 4.1 copy-start.31
  418.8 13.0 %copy-start.30 = (bf16[512,1024]{1,0:T(8,128)(2,1)S(1)}, bf16[512,1024]{1,0:T(8,128)(2,1)}, u32[]{:S(2)}) copy-start(bf16[512,1024]{1,0:T(8,128)(2,1)} %copy-done.29) | copy-start | bytes 3145732
  436.0 2.7 copy-start.78
  438.6 2.8 copy-start.26
  461.6 4.4 copy-start.85
  514.7 2.6 copy-start.62
  524.3 4.7 copy-start.25
  542.2 2.7 copy-start.45
  544.8 2.3 copy-start.15
  547.2 2.3 copy-start.14
  549.5 2.3 copy-start.17
  551.9 2.3 copy-start.16
  554.2 2.3 copy-start.13
  556.6 2.3 copy-start.12
  558.9 2.3 copy-start.11
  561.3 2.3 copy-start.10
  568.9 3.8 copy-start.7
  568.9 3.8 copy-start.40
  568.9 4.9 copy-start.88
  (32 other events, 51.0 us)
Sparse Core Ops, SparseCore 0:
  16.8 156.7 all-gather.2
  567.5 241.1 reduce-scatter.1

commit v2 on v1

--- a/solution.py
+++ b/solution.py
@@ -49,6 +49,11 @@
     return form(high, right_bf16) + form(low, right_bf16)
 
 
+def split_product_right(left_bf16, right_f32):
+    high, low = split_parts(right_f32)
+    return product_tn(left_bf16, high) + product_tn(left_bf16, low)
+
+
 def norm_rows(values, gain_vec):
     centre = values - jnp.mean(values, axis=-1, keepdims=True)
     spread = jnp.mean(centre * centre, axis=-1, keepdims=True)
@@ -68,10 +73,8 @@
 
 def assemble(blocks, kind, items, heads):
     count, first, second = blocks.shape
-    if kind == "rows":
+    if kind in ("rows", "cols"):
         return blocks.reshape(count * first, second)
-    if kind == "cols":
-        return blocks.transpose(1, 0, 2).reshape(first, count * second)
     if kind == "ih":
         parts = blocks.reshape(items, heads, first, second).transpose(0, 2, 1, 3)
         return parts.reshape(items * first, heads * second)
@@ -82,10 +85,8 @@
 def disassemble(whole, kind, items, heads):
     count = items * heads
     rows, cols = whole.shape
-    if kind == "rows":
+    if kind in ("rows", "cols"):
         return whole.reshape(count, rows // count, cols)
-    if kind == "cols":
-        return whole.reshape(rows, count, cols // count).transpose(1, 0, 2)
     if kind == "ih":
         parts = whole.reshape(items, rows // items, heads, cols // heads).transpose(0, 2, 1, 3)
         return parts.reshape(count, rows // items, cols // heads)
@@ -109,51 +110,63 @@
 )
 
 
-WIDTH = 1024
+PANEL = 128
 ROW_TILE = 16
-
-
-def to_rows(flat):
-    count, size = flat.shape
-    rows = -(-size // (WIDTH * ROW_TILE)) * ROW_TILE
-    flat = jnp.pad(flat, ((0, 0), (0, rows * WIDTH - size)))
-    return flat.reshape(count, rows, WIDTH)
+ROW_GROUP = 48
+
+
+def panels(block):
+    count, first, second = block.shape
+    width = -(-second // PANEL) * PANEL
+    if width != second:
+        block = jnp.pad(block, ((0, 0), (0, 0), (0, width - second)))
+    parts = block.reshape(count, first, width // PANEL, PANEL).transpose(0, 2, 1, 3)
+    return parts.reshape(count, (width // PANEL) * first, PANEL)
+
+
+def unpanels(rows, first, second):
+    count = rows.shape[0]
+    width = -(-second // PANEL) * PANEL
+    parts = rows.reshape(count, width // PANEL, first, PANEL).transpose(0, 2, 1, 3)
+    return parts.reshape(count, first, width)[:, :, :second]
 
 
 def pack(pieces):
     blocks, places, row = [], [], 0
     for piece in pieces:
-        block = to_rows(piece)
-        places.append((row, piece.shape[1]))
+        block = panels(piece)
+        extra = -block.shape[1] % ROW_TILE
+        if extra:
+            block = jnp.pad(block, ((0, 0), (0, extra), (0, 0)))
+        places.append((row, piece.shape[1], piece.shape[2]))
         blocks.append(block)
         row += block.shape[1]
-    extra = packed_rows(row) - row
+    extra = -row % ROW_GROUP
     if extra:
-        blocks.append(jnp.zeros((pieces[0].shape[0], extra, WIDTH), pieces[0].dtype))
+        blocks.append(jnp.zeros((pieces[0].shape[0], extra, PANEL), pieces[0].dtype))
     return jnp.concatenate(blocks, axis=1), places
 
 
-def packed_rows(rows):
-    return -(-rows // 128) * 128
-
-
 def unpack(packed, place):
-    row, size = place
-    rows = -(-size // WIDTH)
-    return packed[:, row : row + rows, :].reshape(packed.shape[0], rows * WIDTH)[:, :size]
+    row, first, second = place
+    count = -(-second // PANEL) * first
+    return unpanels(packed[:, row : row + count, :], first, second)
+
+
+def local_block(w, kind):
+    return (w.T if kind == "cols" else w)[None]
 
 
 def gather_weights(weights, gains, items, heads):
     count = items * heads
-    pieces = [rounded(w).reshape(1, -1) for w in weights]
-    pieces.append(rounded(jnp.concatenate(gains)).reshape(1, -1))
+    pieces = [rounded(local_block(w, kind)) for w, kind in zip(weights, WEIGHT_KINDS)]
+    pieces.append(rounded(jnp.concatenate(gains)).reshape(1, 1, -1))
     packed, places = pack(pieces)
     local_rows = packed.shape[1]
-    gathered = lax.all_gather(packed[0], ALL, axis=0, tiled=True).reshape(count, local_rows, WIDTH)
+    gathered = lax.all_gather(packed[0], ALL, axis=0, tiled=True).reshape(count, local_rows, PANEL)
     whole_weights = []
-    for w, kind, place in zip(weights, WEIGHT_KINDS, places):
-        blocks = unpack(gathered, place).reshape((count,) + w.shape)
-        whole_weights.append(assemble(blocks, kind, items, heads))
+    for kind, place in zip(WEIGHT_KINDS, places):
+        whole_weights.append(assemble(unpack(gathered, place), kind, items, heads))
     gain_blocks = unpack(gathered, places[-1]).reshape(count, len(gains), -1)
     whole_gains = [widened(gain_blocks[:, k, :].reshape(-1)) for k in range(len(gains))]
     return whole_weights, whole_gains
@@ -163,15 +176,18 @@
     count = items * heads
     pieces = []
     for g, kind in zip(weight_grads, WEIGHT_KINDS):
-        pieces.append(rounded(disassemble(g, kind, items, heads)).reshape(count, -1))
+        pieces.append(rounded(disassemble(g, kind, items, heads)))
     gain_stack = jnp.stack([g.reshape(count, -1) for g in gain_grads], axis=1)
-    pieces.append(rounded(gain_stack).reshape(count, -1))
+    pieces.append(rounded(gain_stack).reshape(count, 1, -1))
     packed, places = pack(pieces)
     local_rows = packed.shape[1]
     mine = lax.psum_scatter(
-        packed.reshape(count * local_rows, WIDTH), ALL, scatter_dimension=0, tiled=True
-    ).reshape(1, local_rows, WIDTH)
-    out = [widened(unpack(mine, place)[0]) for place in places[:-1]]
+        packed.reshape(count * local_rows, PANEL), ALL, scatter_dimension=0, tiled=True
+    ).reshape(1, local_rows, PANEL)
+    out = []
+    for kind, place in zip(WEIGHT_KINDS, places):
+        block = widened(unpack(mine, place)[0])
+        out.append(block.T if kind == "cols" else block)
     gain_part = widened(unpack(mine, places[-1])[0]).reshape(len(gain_grads), -1)
     out += [gain_part[k] for k in range(len(gain_grads))]
     return out
@@ -300,7 +316,7 @@
     scale = 1.0 / math.sqrt(query_w.shape[1])
     normed = rounded(norm_rows(residual, gain_vec))
     query_rows = rounded(product(normed, query_w))
-    query_keyed = rounded(product_nt(query_rows, key_w) * scale)
+    query_keyed = rounded(product(query_rows, key_w) * scale)
     scores = jnp.where(allowed[None, :], product(query_keyed, pixel_norm), MASKED)
     row_top = jnp.max(scores, axis=-1, keepdims=True)
     raw_weights = jnp.exp(scores - row_top)
@@ -308,7 +324,7 @@
     weights = raw_weights / row_total
     weights_low = rounded(weights)
     pixel_mix = product_nt(weights_low, pixel_norm)
-    mixed = rounded(split_product(pixel_mix, value_w))
+    mixed = rounded(split_product(pixel_mix, value_w, product_nt))
     saved = (normed, query_rows, weights, pixel_mix, mixed)
     return residual + product(mixed, out_w), saved
 
@@ -321,15 +337,15 @@
     grad_round = rounded(grad_out)
     grad_out_w = product_tn(mixed, grad_round)
     grad_mixed = rounded(product_nt(grad_round, out_w))
-    grad_keyed = rounded(product_nt(grad_mixed, value_w))
+    grad_keyed = rounded(product(grad_mixed, value_w))
     grad_weights = product(grad_keyed, pixel_norm)
     grad_scores = weights * (grad_weights - jnp.sum(grad_weights * weights, axis=-1, keepdims=True))
     grad_scores = rounded(grad_scores)
     score_mix = product_nt(grad_scores, pixel_norm)
-    grad_query = rounded(split_product(score_mix, key_w) * scale)
+    grad_query = rounded(split_product(score_mix, key_w, product_nt) * scale)
     grad_query_w = product_tn(normed, grad_query)
-    grad_key_w = split_product(score_mix, query_rows, product_tn) * scale
-    grad_value_w = split_product(pixel_mix, grad_mixed, product_tn)
+    grad_key_w = split_product_right(query_rows, score_mix) * scale
+    grad_value_w = split_product_right(grad_mixed, pixel_mix)
     grad_normed = product_nt(grad_query, query_w)
     grad_residual, grad_gain = norm_backward(residual, gain_vec, grad_normed)
     return (grad_out + grad_residual, grad_query_w, grad_key_w, grad_value_w, grad_out_w, grad_gain)

time: 836 us -> 772 us (0.923)
  local copies, waits for them, and re-layouts: 243 us -> 206 us
  waiting for transfers between devices: 378 us -> 355 us
    another operation x8 -> x1, local copies, waits for them, and re-layouts: 32.4 us -> 0.08 us  [gather_weights(): gain_blocks = unpack(gathered, places[-1]).reshape(count, len(gains), -1)]
    transpose x2 -> x13, local copies, waits for them, and re-layouts: 3.65 us -> 33.8 us  [the longest x7 22.8 us: unpanels(): rows.reshape(count, width // PANEL, first, PANEL).transpose(0, 2, 1, 3)]
    convert_element_type x24 -> x18, local copies, waits for them, and re-layouts: 61.6 us -> 48.3 us  [rounded(): return values.astype(jnp.bfloat16)]
    reduce_scatter x1, waiting for transfers between devices: 232 us -> 221 us  [reduce_grads(): lax.psum_scatter(packed.reshape(count * local_rows, PANEL), ALL, scatter_...]
    all_gather x1, waiting for transfers between devices: 146 us -> 134 us  [gather_weights(): lax.all_gather(packed[0], ALL, axis=0, tiled=True)]
    dot_general x16 -> x12, matrix products: 47.8 us -> 44.1 us  [product(): return jnp.dot(left_side, right_side, preferred_element_type=jnp.float32)]
    unnamed x226 -> x280, local copies, waits for them, and re-layouts: 58.3 us -> 61 us
    slice x7 -> x4, local copies, waits for them, and re-layouts: 20.3 us -> 18.1 us  [unpack(): return unpanels(packed[:, row:row + count, :], first, second)]
where the time goes in v2:
time: 772 us; the launch traced here: 761 us
  waiting for transfers between devices  355 us (46%)
  local copies, waits for them, and re-layouts  206 us (27%)
  matrix products  141 us (18%)
  other arithmetic  40.4 us (5%)
  between operations  18.9 us (2%)
    reduce_scatter x1, waiting for transfers between devices, reduce_grads(): lax.psum_scatter(packed.reshape(count * local_rows, PANEL), ALL, scatter_...  221 us
    all_gather x1, waiting for transfers between devices, gather_weights(): lax.all_gather(packed[0], ALL, axis=0, tiled=True)  134 us
    unnamed x280, local copies, waits for them, and re-layouts  61 us
    convert_element_type x18, local copies, waits for them, and re-layouts, rounded(): return values.astype(jnp.bfloat16)  48.3 us
    dot_general x12, matrix products, product(): return jnp.dot(left_side, right_side, preferred_element_type=jnp.float32)  44.1 us
    dot_general x16, matrix products, product_nt(): lax.dot_general(left_side, right_side, (((1,), (1,)), ((), ())), preferre...  41.4 us
    dot_general x14, matrix products, product_tn(): lax.dot_general(left_side, right_side, (((0,), (0,)), ((), ())), preferre...  34 us
    transpose x7, local copies, waits for them, and re-layouts, unpanels(): rows.reshape(count, width // PANEL, first, PANEL).transpose(0, 2, 1, 3)  22.8 us
  transfers between devices with their start and end apart: 2, of which 2 were waited for; matrix products, arithmetic and copies ran while one was open for 2% of the time, Pallas kernels for 0%

profile of v2, /device:TPU:0, one launch (start us, length us, event | category | flops | bytes accessed | tf_op | source)
XLA Modules:
  0.0 760.9 jit_solution(11532578349145203047)
XLA Ops:
  18.3 3.3 convert_reduce_fusion
  22.2 3.7 fusion.6
  25.9 134.2 %all-gather.3.cloned.1.call-done = bf16[1,89088,128]{2,1,0:T(8,128)(2,1)} async-done(((bf16[1,2784,128]{2,1,0:T(8,128)(2,1)}), bf16[1,89088,128]{2,1,0:T(8,128)(2,1)}) %all-gather.3.cloned.1.call-update) | async-done | bytes 22806544 | tf_op jit(solution)/shard_map/all_gather | solution.py:166
  160.1 14.0 %fusion.210 = (bf16[32,256,128]{2,1,0:T(8,128)(2,1)}, bf16[32,256,128]{2,1,0:T(8,128)(2,1)}, bf16[32,256,128]{2,1,0:T(8,128)(2,1)}, bf16[32,256,128]{2,1,0:T(8,1...) fusion(bf16[32,2784,128]{2,1,0:T(8,128)(2,1)} %bitcast.552), kind=kLoop, calls=%fused_computation.324 | loop fusion | bytes 41943040 | tf_op jit(solution)/shard_map/slice | solution.py:153
  175.1 2.4 fusion.211
  177.5 2.3 copy.141
  180.3 3.2 fusion.120
  183.5 10.1 %select_reduce_fusion = (f32[512]{0:T(512)S(1)}, f32[512,6272]{1,0:T(8,128)}) fusion(pred[6272]{0:T(1024)(128)(4,1)S(1)} %compare_reduce_fusion, f32[6272]{0:T(1024)S(1)} %add_rsqrt_fusion, f32[6272]{0:T(1024)S(1)} %broadcast_multiply_fusion, bf16[261,16384]{1,0:T(8,128)(2,1)} %param.21, s32[]{:T(128)S(6)} %min.4, bf16[512,1024]{1,0:T(8,128)(2,1)S(1)} %fusion.120, ...), kind=kOutput, calls=%fused_computation.4 | convolution fusion | flops 1963195392 | bytes 17798276 | tf_op jit(solution)/shard_map/dot_general | solution.py:27
  193.6 7.3 fusion.2
  201.9 6.5 fusion.10
  215.6 3.0 copy.145
  218.7 4.5 copy.146
  228.9 4.1 copy.152
  233.0 2.9 copy.153
  237.6 2.3 fusion.132
  239.9 2.3 copy.219
  242.1 4.1 copy.150
  246.2 3.0 copy.151
  250.6 2.3 fusion.129
  252.9 2.7 copy.218
  255.6 4.1 copy.148
  259.6 3.0 copy.149
  265.2 2.7 copy.158
  267.9 7.6 fusion.215
  275.5 4.7 fusion.114
  283.9 4.2 copy.159
  288.1 4.3 copy.160
  293.0 3.1 copy.161
  299.7 2.4 fusion.36
  312.0 5.4 multiply_reduce_fusion.1
  318.5 2.7 multiply_convert_fusion.1
  337.4 3.1 fusion.29
  342.2 2.8 convolution_convert_fusion.1
  349.4 13.7 %multiply_reduce_fusion = (f32[512]{0:T(512)S(1)}, f32[512,6272]{1,0:T(8,128)}) fusion(f32[512]{0:T(512)S(1)} %copy-done.105, f32[512]{0:T(512)S(1)} %copy-done.103, f32[512,6272]{1,0:T(8,128)} %get-tuple-element.65, pred[6272]{0:T(1024)(128)(4,1)S(1)} %compare_reduce_fusion, f32[6272]{0:T(1024)S(1)} %add_rsqrt_fusion, f32[6272]{0:T(1024)S(1)} %broadcast_multiply_fusion, ...), kind=kOutput, calls=%fused_computation.2 | convolution fusion | flops 1972695552 | bytes 30647428 | tf_op jit(solution)/shard_map/dot_general | solution.py:27
  363.5 13.2 %fusion.8 = f32[512,261]{0,1:T(8,128)S(1)} fusion(f32[512,6272]{1,0:T(8,128)} %get-tuple-element.80, f32[512]{0:T(512)S(1)} %get-tuple-element.79, f32[6272]{0:T(1024)S(1)} %add_rsqrt_fusion, f32[6272]{0:T(1024)S(1)} %broadcast_multiply_fusion, bf16[261,16384]{1,0:T(8,128)(2,1)} %param.21, s32[]{:T(128)S(6)} %min.4, f32[512,6272]{1,0:T(8,128)} %get-tuple-element.65, ...), kind=kOutput, calls=%fused_computation.18 | convolution fusion | flops 1702095360 | bytes 29598852 | tf_op jit(solution)/shard_map/dot_general | solution.py:37
  382.8 2.8 convert_bitcast_fusion.7
  385.9 2.6 convert_bitcast_fusion.6
  388.5 2.8 convert_bitcast_fusion.5
  391.4 2.9 convolution_convert_fusion
  394.3 2.8 convert_bitcast_fusion
  398.7 2.5 copy.239
  401.2 2.5 copy.207
  403.6 4.1 convert_bitcast_fusion.4
  407.8 4.2 convert_element_type.630
  411.9 3.5 copy.181
  415.4 4.5 convert_element_type.621
  419.9 4.3 copy.177
  424.2 4.1 copy.178
  428.2 2.6 fusion.152
  433.3 3.3 reshape.655
  436.6 2.4 copy.175
  450.3 2.6 convert_bitcast_fusion.3
  452.9 4.0 convert_element_type.633
  456.9 3.6 copy.183
  460.6 2.7 convert_bitcast_fusion.2
  463.2 4.0 convert_element_type.636
  467.3 3.6 copy.185
  472.2 2.8 convert_bitcast_fusion.1
  476.5 4.5 convert_element_type.641
  481.0 4.3 copy.188
  485.3 4.3 copy.189
  514.8 4.4 add_add_fusion.4
  519.6 2.5 add_convert_fusion
  522.1 220.8 %reduce-scatter.2.cloned.1.call-done = bf16[2784,128]{1,0:T(8,128)(2,1)} async-done(((bf16[89088,128]{1,0:T(8,128)(2,1)}), bf16[2784,128]{1,0:T(8,128)(2,1)}) %reduce-scatter.2.cloned.1.call-update) | async-done | bytes 712720 | tf_op jit(solution)/shard_map/reduce_scatter | solution.py:184
  (432 shorter events, 130.9 us)
Async XLA Ops:
  7.2 6.0 copy-start.79
  7.2 6.0 copy-start.80
  7.2 6.1 copy-start.81
  7.2 6.1 copy-start.108
  7.2 6.1 copy-start.107
  7.2 6.2 copy-start.110
  7.3 6.2 copy-start.109
  7.3 6.2 copy-start.82
  7.3 152.9 %all-gather.3.cloned.1.call-start = ((), (), s32[]{:S(2)}) async-start(), calls=%async_computation.2 | async-start | bytes 23519232 | tf_op jit(solution)/shard_map/all_gather | solution.py:166
  8.5 5.1 copy-start.83
  10.2 3.5 copy-start.84
  12.2 2.6 copy-start.85
  13.8 7.8 %copy-start.2 = (bf16[512,1024]{1,0:T(8,128)(2,1)S(1)}, bf16[512,1024]{1,0:T(8,128)(2,1)}, u32[]{:S(2)}) copy-start(bf16[512,1024]{1,0:T(8,128)(2,1)} %param.20) | copy-start | bytes 3145732
  14.6 728.2 %reduce-scatter.2.cloned.1.call-start = ((), (), s32[]{:S(2)}) async-start(), calls=%async_computation.1 | async-start | bytes 23519232 | tf_op jit(solution)/shard_map/reduce_scatter | solution.py:184
  21.8 158.5 %copy-start.88 = (f32[512]{0:T(512)}, f32[512]{0:T(512)S(1)}, u32[]{:S(2)}) copy-start(f32[512]{0:T(512)S(1)} %broadcast_multiply_fusion.4) | copy-start | bytes 6148
  22.2 152.0 %copy-start.90 = (f32[512]{0:T(512)}, f32[512]{0:T(512)S(1)}, u32[]{:S(2)}) copy-start(f32[512]{0:T(512)S(1)} %fusion.37) | copy-start | bytes 6148
  22.2 158.1 %copy-start.92 = (f32[512]{0:T(512)}, f32[512]{0:T(512)S(1)}, u32[]{:S(2)}) copy-start(f32[512]{0:T(512)S(1)} %fusion.183) | copy-start | bytes 6148
  180.1 3.3 copy-start.86
  180.2 3.2 copy-start.31
  183.5 10.1 %copy-start.37 = (bf16[512,1024]{1,0:T(8,128)(2,1)}, bf16[512,1024]{1,0:T(8,128)(2,1)S(1)}, u32[]{:S(2)}) copy-start(bf16[512,1024]{1,0:T(8,128)(2,1)S(1)} %fusion.120) | copy-start | bytes 3145732
  193.6 7.3 copy-start.102
  193.6 8.3 %copy-start.4 = (f32[512,6272]{1,0:T(8,128)S(1)}, f32[512,6272]{1,0:T(8,128)}, u32[]{:S(2)}) copy-start(f32[512,6272]{1,0:T(8,128)} %get-tuple-element.65) | copy-start | bytes 38535172
  201.9 6.5 copy-start.104
  201.9 6.5 copy-start.46
  215.0 9.6 %copy-start.98 = (f32[512]{0:T(512)}, f32[512]{0:T(512)S(1)}, u32[]{:S(2)}) copy-start(f32[512]{0:T(512)S(1)} %fusion.184) | copy-start | bytes 6148
  218.7 4.5 copy-start.8
  246.2 4.4 copy-start.70
  259.6 3.0 copy-start.71
  275.5 4.8 copy-start.62
  293.0 3.1 copy-start.12
  293.0 3.1 copy-start.64
  296.1 3.5 copy-start.34
  312.0 5.4 slice-start
  312.0 6.5 slice-start.1
  318.5 2.7 copy-start.44
  322.7 4.5 copy-start.75
  324.4 5.1 copy-start.77
  325.9 5.2 copy-start.67
  337.4 8.4 %copy-start.6 = (f32[512,1024]{1,0:T(8,128)}, f32[512,1024]{1,0:T(8,128)S(1)}, u32[]{:S(2)}) copy-start(f32[512,1024]{1,0:T(8,128)S(1)} %add_add_fusion.6) | copy-start | bytes 6291460
  337.4 3.2 copy-start.17
  337.4 3.2 copy-start.53
  337.4 3.2 copy-start.95
  337.4 3.2 copy-start.99
  349.4 13.7 %copy-start.40 = (bf16[512,1024]{1,0:T(8,128)(2,1)}, bf16[512,1024]{1,0:T(8,128)(2,1)S(1)}, u32[]{:S(2)}) copy-start(bf16[512,1024]{1,0:T(8,128)(2,1)S(1)} %fusion.123) | copy-start | bytes 3145732
  363.5 13.2 %copy-start.32 = (bf16[32,3,4,8,128]{4,3,1,2,0:T(8,128)(2,1)S(1)}, bf16[32,3,4,8,128]{4,3,1,2,0:T(8,128)(2,1)}, u32[]{:S(2)}) copy-start(bf16[32,3,4,8,128]{4,3,1,2,0:T(8,128)(2,1)} %copy-done.31) | copy-start | bytes 2359300
  382.7 14.5 %copy-start.28 = (f32[512,1024]{1,0:T(8,128)}, f32[512,1024]{1,0:T(8,128)S(1)}, u32[]{:S(2)}) copy-start(f32[512,1024]{1,0:T(8,128)S(1)} %get-tuple-element.82) | copy-start | bytes 6291460
  382.7 2.8 copy-start.27
  382.7 3.1 copy-start.66
  385.9 2.6 copy-start.7
  385.9 2.6 copy-start.117
  388.5 2.9 copy-start.13
  388.5 2.9 copy-start.97
  388.5 2.9 copy-start.101
  388.5 2.9 copy-start.119
  391.4 2.9 copy-start.36
  391.4 2.9 copy-start.113
  394.3 2.8 copy-start.91
  433.3 5.8 copy-start.33
  456.9 3.6 copy-start.68
  456.9 3.6 copy-start.73
  467.3 3.6 copy-start.42
  514.8 4.4 copy-start.14
  514.8 4.4 copy-start.48
  514.8 4.8 copy-start.114
  (60 other events, 107.7 us)
Sparse Core Ops, SparseCore 0:
  14.8 145.3 all-gather.2
  514.9 227.9 reduce-scatter.1

commit v3 on v1

--- a/solution.py
+++ b/solution.py
@@ -44,9 +44,9 @@
     return high, rounded(values - widened(high))
 
 
-def split_product(left_f32, right_bf16, form=product):
-    high, low = split_parts(left_f32)
-    return form(high, right_bf16) + form(low, right_bf16)
+def split_apply_t(values_f32, weight):
+    high, low = split_parts(values_f32)
+    return apply_t(high, weight) + apply_t(low, weight)
 
 
 def norm_rows(values, gain_vec):
@@ -64,33 +64,6 @@
 def norm_backward(residual, gain_vec, grad_normed):
     unused, norm_back = jax.vjp(norm_rows, residual, gain_vec)
     return norm_back(grad_normed)
-
-
-def assemble(blocks, kind, items, heads):
-    count, first, second = blocks.shape
-    if kind == "rows":
-        return blocks.reshape(count * first, second)
-    if kind == "cols":
-        return blocks.transpose(1, 0, 2).reshape(first, count * second)
-    if kind == "ih":
-        parts = blocks.reshape(items, heads, first, second).transpose(0, 2, 1, 3)
-        return parts.reshape(items * first, heads * second)
-    parts = blocks.reshape(items, heads, first, second).transpose(1, 2, 0, 3)
-    return parts.reshape(heads * first, items * second)
-
-
-def disassemble(whole, kind, items, heads):
-    count = items * heads
-    rows, cols = whole.shape
-    if kind == "rows":
-        return whole.reshape(count, rows // count, cols)
-    if kind == "cols":
-        return whole.reshape(rows, count, cols // count).transpose(1, 0, 2)
-    if kind == "ih":
-        parts = whole.reshape(items, rows // items, heads, cols // heads).transpose(0, 2, 1, 3)
-        return parts.reshape(count, rows // items, cols // heads)
-    parts = whole.reshape(heads, rows // heads, items, cols // items).transpose(2, 0, 1, 3)
-    return parts.reshape(count, rows // heads, cols // items)
 
 
 WEIGHT_KINDS = (
@@ -108,91 +81,195 @@
     "hi",
 )
 
-
-WIDTH = 1024
+PANEL = 128
 ROW_TILE = 16
-
-
-def to_rows(flat):
-    count, size = flat.shape
-    rows = -(-size // (WIDTH * ROW_TILE)) * ROW_TILE
-    flat = jnp.pad(flat, ((0, 0), (0, rows * WIDTH - size)))
-    return flat.reshape(count, rows, WIDTH)
-
-
-def pack(pieces):
-    blocks, places, row = [], [], 0
-    for piece in pieces:
-        block = to_rows(piece)
-        places.append((row, piece.shape[1]))
-        blocks.append(block)
-        row += block.shape[1]
-    extra = packed_rows(row) - row
-    if extra:
-        blocks.append(jnp.zeros((pieces[0].shape[0], extra, WIDTH), pieces[0].dtype))
-    return jnp.concatenate(blocks, axis=1), places
-
-
-def packed_rows(rows):
-    return -(-rows // 128) * 128
-
-
-def unpack(packed, place):
-    row, size = place
-    rows = -(-size // WIDTH)
-    return packed[:, row : row + rows, :].reshape(packed.shape[0], rows * WIDTH)[:, :size]
+ROW_GROUP = 48
+
+
+def contract(left, right, left_dims, right_dims):
+    return lax.dot_general(
+        left, right, ((left_dims, right_dims), ((), ())), preferred_element_type=jnp.float32
+    )
+
+
+def lane_pad(values, width):
+    panels = -(-width // PANEL)
+    if panels * PANEL != width:
+        pad = [(0, 0)] * (values.ndim - 1) + [(0, panels * PANEL - width)]
+        values = jnp.pad(values, pad)
+    return values.reshape(values.shape[:-1] + (panels, PANEL))
+
+
+def lane_cut(values, width):
+    values = values.reshape(values.shape[:-2] + (-1,))
+    return values if values.shape[-1] == width else values[..., :width]
+
+
+def local_panels(block):
+    rows, width = block.shape
+    parts = lane_pad(block, width).transpose(1, 0, 2)
+    return parts.reshape(-1, PANEL)
+
+
+def padded_rows(rows):
+    return -(-rows // ROW_TILE) * ROW_TILE
+
+
+def local_shape(w, kind):
+    return (w.shape[1], w.shape[0]) if kind == "cols" else w.shape
+
+
+def make_weight(piece, kind, shape, items, heads):
+    rows, width = shape
+    panels = -(-width // PANEL)
+    blocks = piece[:, : panels * rows, :].reshape(items * heads, panels, rows, PANEL)
+    if kind in ("ih", "hi"):
+        blocks = blocks.reshape(items, heads, panels, rows, PANEL)
+    return kind, blocks, width
+
+
+def apply(values, weight):
+    kind, blocks, width = weight
+    count = values.shape[0]
+    if kind in ("rows", "cols"):
+        devices, panels, rows, lanes = blocks.shape
+        out = contract(values.reshape(count, devices, rows), blocks, (1, 2), (0, 2))
+        return lane_cut(out, width)
+    items, heads, panels, rows, lanes = blocks.shape
+    if kind == "ih":
+        out = contract(values.reshape(count, items, rows), blocks, (1, 2), (0, 3))
+    else:
+        out = contract(values.reshape(count, heads, rows), blocks, (1, 2), (1, 3))
+    return lane_cut(out, width).reshape(count, -1)
+
+
+def apply_t(values, weight):
+    kind, blocks, width = weight
+    count = values.shape[0]
+    if kind in ("rows", "cols"):
+        devices, panels, rows, lanes = blocks.shape
+        out = contract(lane_pad(values, width), blocks, (1, 2), (1, 3))
+        return out.reshape(count, devices * rows)
+    items, heads, panels, rows, lanes = blocks.shape
+    if kind == "ih":
+        spread = lane_pad(values.reshape(count, heads, width), width)
+        out = contract(spread, blocks, (1, 2, 3), (1, 2, 4))
+        return out.reshape(count, items * rows)
+    spread = lane_pad(values.reshape(count, items, width), width)
+    out = contract(spread, blocks, (1, 2, 3), (0, 2, 4))
+    return out.reshape(count, heads * rows)
+
+
+def grad_blocks(values, grads, weight):
+    kind, blocks, width = weight
+    count = values.shape[0]
+    if kind in ("rows", "cols"):
+        devices, panels, rows, lanes = blocks.shape
+        out = contract(values.reshape(count, devices, rows), lane_pad(grads, width), (0,), (0,))
+        out = out.transpose(0, 2, 1, 3)
+    else:
+        items, heads, panels, rows, lanes = blocks.shape
+        devices = items * heads
+        if kind == "ih":
+            spread = lane_pad(grads.reshape(count, heads, width), width)
+            out = contract(values.reshape(count, items, rows), spread, (0,), (0,))
+            out = out.transpose(0, 2, 3, 1, 4)
+        else:
+            spread = lane_pad(grads.reshape(count, items, width), width)
+            out = contract(values.reshape(count, heads, rows), spread, (0,), (0,))
+            out = out.transpose(2, 0, 3, 1, 4)
+    return out.reshape(devices, -1, PANEL)
+
+
+def split_grad_blocks(values, grads_f32, weight):
+    high, low = split_parts(grads_f32)
+    return grad_blocks(values, high, weight) + grad_blocks(values, low, weight)
+
+
+def pad_rows(block, rows):
+    extra = rows - block.shape[-2]
+    if extra == 0:
+        return block
+    pad = [(0, 0)] * (block.ndim - 2) + [(0, extra), (0, 0)]
+    return jnp.pad(block, pad)
 
 
 def gather_weights(weights, gains, items, heads):
     count = items * heads
-    pieces = [rounded(w).reshape(1, -1) for w in weights]
-    pieces.append(rounded(jnp.concatenate(gains)).reshape(1, -1))
-    packed, places = pack(pieces)
-    local_rows = packed.shape[1]
-    gathered = lax.all_gather(packed[0], ALL, axis=0, tiled=True).reshape(count, local_rows, WIDTH)
-    whole_weights = []
-    for w, kind, place in zip(weights, WEIGHT_KINDS, places):
-        blocks = unpack(gathered, place).reshape((count,) + w.shape)
-        whole_weights.append(assemble(blocks, kind, items, heads))
-    gain_blocks = unpack(gathered, places[-1]).reshape(count, len(gains), -1)
-    whole_gains = [widened(gain_blocks[:, k, :].reshape(-1)) for k in range(len(gains))]
-    return whole_weights, whole_gains
-
-
-def reduce_grads(weight_grads, gain_grads, items, heads):
+    pieces, places, row = [], [], 0
+    for w, kind in zip(weights, WEIGHT_KINDS):
+        block = local_panels(rounded(w.T if kind == "cols" else w))
+        rows = padded_rows(block.shape[0])
+        pieces.append(pad_rows(block, rows))
+        places.append((row, rows))
+        row += rows
+    gain_row = rounded(jnp.concatenate(gains)).reshape(1, -1)
+    gain_block = local_panels(gain_row)
+    pieces.append(pad_rows(gain_block, padded_rows(gain_block.shape[0])))
+    places.append((row, pieces[-1].shape[0]))
+    row += pieces[-1].shape[0]
+    total = -(-row // ROW_GROUP) * ROW_GROUP
+    packed = pad_rows(jnp.concatenate(pieces, axis=0), total)
+    gathered = lax.all_gather(packed, ALL, axis=0, tiled=True).reshape(count, total, PANEL)
+    out = []
+    for w, kind, (first, rows) in zip(weights, WEIGHT_KINDS, places):
+        piece = gathered[:, first : first + rows, :]
+        out.append(make_weight(piece, kind, local_shape(w, kind), items, heads))
+    first, rows = places[-1]
+    gain_all = gathered[:, first : first + rows, :].reshape(count, -1)[:, : gain_row.shape[1]]
+    gain_all = gain_all.reshape(count, len(gains), -1)
+    whole_gains = [widened(gain_all[:, k, :].reshape(-1)) for k in range(len(gains))]
+    return out, whole_gains
+
+
+def reduce_grads(grad_parts, gain_grads, weights, items, heads):
     count = items * heads
-    pieces = []
-    for g, kind in zip(weight_grads, WEIGHT_KINDS):
-        pieces.append(rounded(disassemble(g, kind, items, heads)).reshape(count, -1))
-    gain_stack = jnp.stack([g.reshape(count, -1) for g in gain_grads], axis=1)
-    pieces.append(rounded(gain_stack).reshape(count, -1))
-    packed, places = pack(pieces)
-    local_rows = packed.shape[1]
+    pieces, places, row = [], [], 0
+    for part in grad_parts:
+        rows = padded_rows(part.shape[1])
+        pieces.append(pad_rows(rounded(part), rows))
+        places.append((row, part.shape[1]))
+        row += rows
+    gain_stack = jnp.stack([g.reshape(count, -1) for g in gain_grads], axis=1).reshape(count, 1, -1)
+    gain_block = lane_pad(gain_stack, gain_stack.shape[-1]).reshape(count, -1, PANEL)
+    pieces.append(pad_rows(rounded(gain_block), padded_rows(gain_block.shape[1])))
+    places.append((row, gain_block.shape[1]))
+    row += pieces[-1].shape[1]
+    total = -(-row // ROW_GROUP) * ROW_GROUP
+    packed = pad_rows(jnp.concatenate(pieces, axis=1), total)
     mine = lax.psum_scatter(
-        packed.reshape(count * local_rows, WIDTH), ALL, scatter_dimension=0, tiled=True
-    ).reshape(1, local_rows, WIDTH)
-    out = [widened(unpack(mine, place)[0]) for place in places[:-1]]
-    gain_part = widened(unpack(mine, places[-1])[0]).reshape(len(gain_grads), -1)
+        packed.reshape(count * total, PANEL), ALL, scatter_dimension=0, tiled=True
+    )
+    out = []
+    for w, kind, (first, rows) in zip(weights, WEIGHT_KINDS, places):
+        r, width = local_shape(w, kind)
+        panels = -(-width // PANEL)
+        block = mine[first : first + rows].reshape(panels, r, PANEL).transpose(1, 0, 2)
+        block = widened(lane_cut(block, width))
+        out.append(block.T if kind == "cols" else block)
+    first, rows = places[-1]
+    gain_part = widened(mine[first : first + rows].reshape(-1)[: gain_stack.shape[-1]])
+    gain_part = gain_part.reshape(len(gain_grads), -1)
     out += [gain_part[k] for k in range(len(gain_grads))]
     return out
 
 
 def mlp_block(residual, gain_vec, up_w, down_w):
     normed = rounded(norm_rows(residual, gain_vec))
-    before = product(normed, up_w)
+    before = apply(normed, up_w)
     hidden = rounded(jax.nn.gelu(before))
-    return residual + product(hidden, down_w), (normed, before, hidden)
+    return residual + apply(hidden, down_w), (normed, before, hidden)
 
 
 def mlp_block_back(residual, gain_vec, up_w, down_w, saved, grad_out):
     normed, before, hidden = saved
     grad_round = rounded(grad_out)
-    grad_down = product_tn(hidden, grad_round)
-    grad_hidden = product_nt(grad_round, down_w)
+    grad_down = grad_blocks(hidden, grad_round, down_w)
+    grad_hidden = apply_t(grad_round, down_w)
     unused, gelu_back = jax.vjp(jax.nn.gelu, before)
     grad_before = rounded(gelu_back(grad_hidden)[0])
-    grad_up = product_tn(normed, grad_before)
-    grad_normed = product_nt(grad_before, up_w)
+    grad_up = grad_blocks(normed, grad_before, up_w)
+    grad_normed = apply_t(grad_before, up_w)
     grad_residual, grad_gain = norm_backward(residual, gain_vec, grad_normed)
     return grad_out + grad_residual, grad_up, grad_down, grad_gain
 
@@ -226,11 +303,11 @@
 def attention_block(residual, gain_vec, weight_set, split):
     query_w, key_w, value_w, out_w = weight_set
     rows = residual.shape[0]
-    heads_n = query_w.shape[1] // HEAD
     normed = rounded(norm_rows(residual, gain_vec))
-    query_rows = rounded(product(normed, query_w))
-    key_rows = rounded(product(normed, key_w))
-    value_rows = rounded(product(normed, value_w))
+    query_rows = rounded(apply(normed, query_w))
+    key_rows = rounded(apply(normed, key_w))
+    value_rows = rounded(apply(normed, value_w))
+    heads_n = query_rows.shape[1] // HEAD
     key_all = jnp.concatenate(exchange_rows(key_rows, split), axis=0)
     value_all = jnp.concatenate(exchange_rows(value_rows, split), axis=0)
     keys = key_all.shape[0]
@@ -247,7 +324,7 @@
     mixed = jnp.einsum("hqk,khd->qhd", rounded(weights), v4, preferred_element_type=jnp.float32)
     mixed = rounded(mixed.reshape(rows, heads_n * HEAD))
     saved = (normed, q4, k4, v4, weights, mixed)
-    return residual + product(mixed, out_w), saved
+    return residual + apply(mixed, out_w), saved
 
 
 def attention_block_back(residual, gain_vec, weight_set, split, saved, grad_out):
@@ -257,8 +334,8 @@
     keys = k4.shape[0]
     scale = 1.0 / math.sqrt(HEAD)
     grad_round = rounded(grad_out)
-    grad_out_w = product_tn(mixed, grad_round)
-    grad_mixed = rounded(product_nt(grad_round, out_w)).reshape(q4.shape)
+    grad_out_w = grad_blocks(mixed, grad_round, out_w)
+    grad_mixed = rounded(apply_t(grad_round, out_w)).reshape(q4.shape)
     grad_value = jnp.einsum(
         "hqk,qhd->khd", rounded(weights), grad_mixed, preferred_element_type=jnp.float32
     ).reshape(keys, -1)
@@ -274,13 +351,11 @@
         grad_value = return_rows(jnp.split(grad_value, split, axis=0), split)
     grad_key = rounded(grad_key)
     grad_value = rounded(grad_value)
-    grad_query_w = product_tn(normed, grad_query)
-    grad_key_w = product_tn(normed, grad_key)
-    grad_value_w = product_tn(normed, grad_value)
+    grad_query_w = grad_blocks(normed, grad_query, query_w)
+    grad_key_w = grad_blocks(normed, grad_key, key_w)
+    grad_value_w = grad_blocks(normed, grad_value, value_w)
     grad_normed = (
-        product_nt(grad_query, query_w)
-        + product_nt(grad_key, key_w)
-        + product_nt(grad_value, value_w)
+        apply_t(grad_query, query_w) + apply_t(grad_key, key_w) + apply_t(grad_value, value_w)
     )
     grad_residual, grad_gain = norm_backward(residual, gain_vec, grad_normed)
     return (grad_out + grad_residual, grad_query_w, grad_key_w, grad_value_w, grad_out_w, grad_gain)
@@ -297,10 +372,10 @@
 
 
 def cross_block(residual, gain_vec, query_w, key_w, value_w, out_w, pixel_norm, allowed):
-    scale = 1.0 / math.sqrt(query_w.shape[1])
+    scale = 1.0 / math.sqrt(residual.shape[1])
     normed = rounded(norm_rows(residual, gain_vec))
-    query_rows = rounded(product(normed, query_w))
-    query_keyed = rounded(product_nt(query_rows, key_w) * scale)
+    query_rows = rounded(apply(normed, query_w))
+    query_keyed = rounded(apply(query_rows, key_w) * scale)
     scores = jnp.where(allowed[None, :], product(query_keyed, pixel_norm), MASKED)
     row_top = jnp.max(scores, axis=-1, keepdims=True)
     raw_weights = jnp.exp(scores - row_top)
@@ -308,29 +383,29 @@
     weights = raw_weights / row_total
     weights_low = rounded(weights)
     pixel_mix = product_nt(weights_low, pixel_norm)
-    mixed = rounded(split_product(pixel_mix, value_w))
+    mixed = rounded(split_apply_t(pixel_mix, value_w))
     saved = (normed, query_rows, weights, pixel_mix, mixed)
-    return residual + product(mixed, out_w), saved
+    return residual + apply(mixed, out_w), saved
 
 
 def cross_block_back(
     residual, gain_vec, query_w, key_w, value_w, out_w, pixel_norm, saved, grad_out
 ):
     normed, query_rows, weights, pixel_mix, mixed = saved
-    scale = 1.0 / math.sqrt(query_w.shape[1])
+    scale = 1.0 / math.sqrt(residual.shape[1])
     grad_round = rounded(grad_out)
-    grad_out_w = product_tn(mixed, grad_round)
-    grad_mixed = rounded(product_nt(grad_round, out_w))
-    grad_keyed = rounded(product_nt(grad_mixed, value_w))
+    grad_out_w = grad_blocks(mixed, grad_round, out_w)
+    grad_mixed = rounded(apply_t(grad_round, out_w))
+    grad_keyed = rounded(apply(grad_mixed, value_w))
     grad_weights = product(grad_keyed, pixel_norm)
     grad_scores = weights * (grad_weights - jnp.sum(grad_weights * weights, axis=-1, keepdims=True))
     grad_scores = rounded(grad_scores)
     score_mix = product_nt(grad_scores, pixel_norm)
-    grad_query = rounded(split_product(score_mix, key_w) * scale)
-    grad_query_w = product_tn(normed, grad_query)
-    grad_key_w = split_product(score_mix, query_rows, product_tn) * scale
-    grad_value_w = split_product(pixel_mix, grad_mixed, product_tn)
-    grad_normed = product_nt(grad_query, query_w)
+    grad_query = rounded(split_apply_t(score_mix, key_w) * scale)
+    grad_query_w = grad_blocks(normed, grad_query, query_w)
+    grad_key_w = split_grad_blocks(query_rows, score_mix, key_w) * scale
+    grad_value_w = split_grad_blocks(grad_mixed, pixel_mix, value_w)
+    grad_normed = apply_t(grad_query, query_w)
     grad_residual, grad_gain = norm_backward(residual, gain_vec, grad_normed)
     return (grad_out + grad_residual, grad_query_w, grad_key_w, grad_value_w, grad_out_w, grad_gain)
 
@@ -419,7 +494,7 @@
         grad_self_down,
     )
     gain_grads = (grad_gain_one, grad_gain_two, grad_gain_three, grad_gain_four)
-    reduced = reduce_grads(weight_grads, gain_grads, items, heads)
+    reduced = reduce_grads(weight_grads, gain_grads, weights, items, heads)
     shaped = [r.reshape(w.shape) for r, w in zip(reduced[:12], weights)]
     shaped += [r.reshape(g.shape) for r, g in zip(reduced[12:], gains)]
     return (rounded(final_rows), latents_grad, *shaped)

time: 836 us -> 753 us (0.901)
  local copies, waits for them, and re-layouts: 243 us -> 169 us
  waiting for transfers between devices: 378 us -> 351 us
  matrix products: 148 us -> 158 us
    dot_general x14 -> x40, matrix products: 35.9 us -> 92.9 us  [contract(): lax.dot_general(left, right, ((left_dims, right_dims), ((), ())), preferr...]
    convert_element_type x24 -> x8, local copies, waits for them, and re-layouts: 61.6 us -> 14.8 us  [rounded(): return values.astype(jnp.bfloat16)]
    transpose x10 -> x2, local copies, waits for them, and re-layouts: 38.3 us -> 0.01 us  [local_panels(): parts = lane_pad(block, width).transpose(1, 0, 2)]
    dot_general x2 -> x17, local copies, waits for them, and re-layouts: 4.95 us -> 36.8 us  [contract(): lax.dot_general(left, right, ((left_dims, right_dims), ((), ())), preferr...]
    dot_general x16 -> x2, matrix products: 47.8 us -> 21.2 us  [product(): return jnp.dot(left_side, right_side, preferred_element_type=jnp.float32)]
    another operation x13 -> x7, local copies, waits for them, and re-layouts: 32.8 us -> 10.6 us  [the longest x5 5.46 us: reduce_grads(): jnp.stack([g.reshape(count, -1) for g in gain_grads], axis=1)]
    dot_general x12 -> x2, matrix products: 39.3 us -> 17.8 us  [product_nt(): lax.dot_general(left_side, right_side, (((1,), (1,)), ((), ())), preferre...]
    pad x5 -> x8, local copies, waits for them, and re-layouts: 1.67 us -> 21.4 us  [the longest x2 21.2 us: pad_rows(): return jnp.pad(block, pad)]
  transfers between devices with their start and end apart: 2 -> 2, of which waited for: 2 -> 2; matrix products, arithmetic and copies ran while one was open for 2% -> 3% of each run, Pallas kernels for 0% -> 0%
where the time goes in v3:
time: 753 us; the launch traced here: 744 us
  waiting for transfers between devices  351 us (47%)
  local copies, waits for them, and re-layouts  169 us (22%)
  matrix products  158 us (21%)
  other arithmetic  47.8 us (6%)
  between operations  18.2 us (2%)
    reduce_scatter x1, waiting for transfers between devices, reduce_grads(): lax.psum_scatter(packed.reshape(count * total, PANEL), ALL, scatter_dimen...  217 us
    all_gather x1, waiting for transfers between devices, gather_weights(): lax.all_gather(packed, ALL, axis=0, tiled=True).reshape(count, total, PANEL)  134 us
    dot_general x40, matrix products, contract(): lax.dot_general(left, right, ((left_dims, right_dims), ((), ())), preferr...  92.9 us
    unnamed x257, local copies, waits for them, and re-layouts  51.6 us
    dot_general x17, local copies, waits for them, and re-layouts, contract(): lax.dot_general(left, right, ((left_dims, right_dims), ((), ())), preferr...  36.8 us
    dot_general x2, matrix products, product(): return jnp.dot(left_side, right_side, preferred_element_type=jnp.float32)  21.2 us
    pad x2, local copies, waits for them, and re-layouts, pad_rows(): return jnp.pad(block, pad)  21.2 us
    dot_general x2, matrix products, product_nt(): lax.dot_general(left_side, right_side, (((1,), (1,)), ((), ())), preferre...  17.8 us
  transfers between devices with their start and end apart: 2, of which 2 were waited for; matrix products, arithmetic and copies ran while one was open for 3% of the time, Pallas kernels for 0%

profile of v3, /device:TPU:0, one launch (start us, length us, event | category | flops | bytes accessed | tf_op | source)
XLA Modules:
  0.0 744.5 jit_solution(17166350061687265627)
XLA Ops:
  20.6 3.3 convert_reduce_fusion
  25.1 3.7 fusion.6
  28.8 133.6 %all-gather.2.cloned.1.call-done = bf16[89088,128]{1,0:T(8,128)(2,1)} async-done(((bf16[2784,128]{1,0:T(8,128)(2,1)}), bf16[89088,128]{1,0:T(8,128)(2,1)}) %all-gather.2.cloned.1.call-update) | async-done | bytes 22806544 | tf_op jit(solution)/shard_map/all_gather | solution.py:213
  163.4 14.0 %fusion.165 = (bf16[32,256,128]{2,1,0:T(8,128)(2,1)}, bf16[32,256,128]{2,1,0:T(8,128)(2,1)}, bf16[32,256,128]{2,1,0:T(8,128)(2,1)}, bf16[32,256,128]{2,1,0:T(8,1...) fusion(bf16[32,2784,128]{2,1,0:T(8,128)(2,1)} %bitcast.704), kind=kLoop, calls=%fused_computation.333 | loop fusion | bytes 41943040 | tf_op jit(solution)/shard_map/slice | solution.py:216
  177.4 3.4 fusion.166
  182.5 2.3 copy.241
  184.8 4.2 bitcast_convert_fusion.5
  189.0 2.7 copy.243
  191.7 2.1 convolution_bitcast_fusion.1
  193.8 6.2 select_reduce_fusion
  200.0 2.6 fusion.2
  202.6 2.1 copy-done
  204.6 6.5 subtract_convert_fusion.1
  214.0 2.3 copy.248
  216.3 3.9 copy.252
  220.2 2.6 copy.250
  222.9 3.3 fusion.168
  228.5 2.6 copy.254
  231.2 5.3 fusion.57
  238.3 3.9 copy.256
  244.2 2.3 fusion.73
  246.4 2.3 bitcast_convert_fusion.3
  250.2 4.3 copy.258
  254.5 4.2 bitcast_convert_fusion.2
  258.7 2.3 copy.396
  261.0 4.0 copy.264
  265.0 4.1 copy.266
  269.1 7.3 fusion.170
  276.4 4.7 fusion.67
  283.0 2.0 copy-done.9
  287.3 2.7 fusion.56
  290.0 3.3 fusion.36
  293.3 2.2 reshape_reshape.19
  295.5 4.8 fusion.45
  303.3 2.3 bitcast_convert_fusion.1
  307.1 6.0 fusion.70
  313.1 4.4 multiply_reduce_fusion.1
  317.8 2.5 multiply_convert_fusion.1
  320.3 2.5 multiply_convert_fusion.3
  324.9 2.8 reshape.666
  342.7 2.4 multiply_reduce_fusion.3
  352.7 3.3 fusion.29
  356.0 2.9 reshape_reshape.20
  358.9 4.1 fusion.46
  366.4 2.3 bitcast_convert_fusion
  371.0 15.0 %multiply_reduce_fusion = (f32[512]{0:T(512)S(1)}, f32[512,6272]{1,0:T(8,128)}) fusion(f32[512]{0:T(512)S(1)} %fusion.2, f32[512]{0:T(512)S(1)} %get-tuple-element.70, f32[512,6272]{1,0:T(8,128)} %copy-done, pred[6272]{0:T(1024)(128)(4,1)S(1)} %compare_reduce_fusion, f32[6272]{0:T(1024)S(1)} %add_rsqrt_fusion, f32[6272]{0:T(1024)S(1)} %broadcast_multiply_fusion, ...), kind=kOutput, calls=%fused_computation.2 | convolution fusion | flops 1698883584 | bytes 29342724 | tf_op jit(solution)/shard_map/dot_general | solution.py:27
  386.1 11.3 %subtract_convert_fusion = (bf16[512,261]{0,1:T(8,128)(2,1)S(1)}, bf16[512,261]{0,1:T(8,128)(2,1)S(1)}) fusion(f32[6272]{0:T(1024)S(1)} %add_rsqrt_fusion, f32[6272]{0:T(1024)S(1)} %broadcast_multiply_fusion, bf16[261,16384]{1,0:T(8,128)(2,1)} %param.21, s32[]{:T(128)S(6)} %min.4, f32[512,6272]{1,0:T(8,128)} %get-tuple-element.90, ...), kind=kOutput, calls=%fused_computation.207 | convolution fusion | flops 1702629888 | bytes 29598852 | tf_op jit(solution)/shard_map/dot_general | solution.py:37
  400.2 2.6 fusion.38
  406.8 2.6 convolution_convert_fusion.5
  416.3 2.5 copy.364
  418.8 4.4 convolution_convert_fusion.3
  423.2 2.6 convolution_convert_fusion.2
  425.8 2.6 convolution_convert_fusion.1
  432.5 2.6 convolution_convert_fusion
  435.1 2.8 reshape.674
  437.9 2.8 convert_bitcast_fusion
  445.7 3.1 fusion.22
  453.0 2.1 fusion.176
  479.1 20.3 %pad.49 = bf16[32,2784,128]{2,1,0:T(8,128)(2,1)} pad(bf16[32,2768,128]{2,1,0:T(8,128)(2,1)} %pad_dynamic-update-slice_fusion, bf16[]{:T(256)} %constant.81.clone.1), padding=0_0x0_16x0_0 | pad | bytes 45481984 | tf_op jit(solution)/shard_map/jit(_pad)/pad | solution.py:194
  499.4 4.1 copy.268
  503.6 4.5 fusion.55
  508.4 2.2 add_add_fusion.4
  510.6 217.0 %reduce-scatter.2.cloned.1.call-done = bf16[2784,128]{1,0:T(8,128)(2,1)} async-done(((bf16[89088,128]{1,0:T(8,128)(2,1)}), bf16[2784,128]{1,0:T(8,128)(2,1)}) %reduce-scatter.2.cloned.1.call-update) | async-done | bytes 712720 | tf_op jit(solution)/shard_map/reduce_scatter | solution.py:240
  727.6 1.9 slice_convert_fusion.2
  (385 shorter events, 123.1 us)
Async XLA Ops:
  7.2 8.5 %copy-start.84 = (f32[256,128]{1,0:T(8,128)S(1)}, f32[256,128]{1,0:T(8,128)}, u32[]{:S(2)}) copy-start(f32[256,128]{1,0:T(8,128)} %param.29) | copy-start | bytes 393220
  7.2 8.6 %copy-start.85 = (f32[256,128]{1,0:T(8,128)S(1)}, f32[256,128]{1,0:T(8,128)}, u32[]{:S(2)}) copy-start(f32[256,128]{1,0:T(8,128)} %param.33) | copy-start | bytes 393220
  7.2 8.6 %copy-start.86 = (f32[256,128]{1,0:T(8,128)S(1)}, f32[256,128]{1,0:T(8,128)}, u32[]{:S(2)}) copy-start(f32[256,128]{1,0:T(8,128)} %param.35) | copy-start | bytes 393220
  7.2 8.7 %copy-start.101 = (f32[32]{0:T(128)S(1)}, f32[32]{0:T(128)}, u32[]{:S(2)}) copy-start(f32[32]{0:T(128)} %param.39) | copy-start | bytes 388
  7.2 8.7 %copy-start.102 = (f32[32]{0:T(128)S(1)}, f32[32]{0:T(128)}, u32[]{:S(2)}) copy-start(f32[32]{0:T(128)} %param.38) | copy-start | bytes 388
  7.2 8.7 %copy-start.103 = (f32[32]{0:T(128)S(1)}, f32[32]{0:T(128)}, u32[]{:S(2)}) copy-start(f32[32]{0:T(128)} %param.37) | copy-start | bytes 388
  7.3 8.7 %copy-start.104 = (f32[32]{0:T(128)S(1)}, f32[32]{0:T(128)}, u32[]{:S(2)}) copy-start(f32[32]{0:T(128)} %param.36) | copy-start | bytes 388
  7.3 155.2 %all-gather.2.cloned.1.call-start = ((), (), s32[]{:S(2)}) async-start(), calls=%async_computation.1 | async-start | bytes 23519232 | tf_op jit(solution)/shard_map/all_gather | solution.py:213
  12.8 4.2 copy-start.87
  16.9 6.9 copy-start.1
  17.0 710.6 %reduce-scatter.2.cloned.1.call-start = ((), (), s32[]{:S(2)}) async-start(), calls=%async_computation.2 | async-start | bytes 23519232 | tf_op jit(solution)/shard_map/reduce_scatter | solution.py:240
  24.1 157.1 %copy-start.91 = (f32[512]{0:T(512)}, f32[512]{0:T(512)S(1)}, u32[]{:S(2)}) copy-start(f32[512]{0:T(512)S(1)} %broadcast_multiply_fusion.4) | copy-start | bytes 6148
  25.1 156.1 %copy-start.93 = (f32[512]{0:T(512)}, f32[512]{0:T(512)S(1)}, u32[]{:S(2)}) copy-start(f32[512]{0:T(512)S(1)} %fusion.149) | copy-start | bytes 6148
  177.4 42.8 %copy-start.3 = (bf16[32,256,128]{2,1,0:T(8,128)(2,1)}, bf16[32,256,128]{2,1,0:T(8,128)(2,1)S(1)}, u32[]{:S(2)}) copy-start(bf16[32,256,128]{2,1,0:T(8,128)(2,1)S(1)} %get-tuple-element.49) | copy-start | bytes 6291460
  181.2 3.6 copy-start.88
  200.0 4.6 copy-start
  204.6 6.6 copy-start.54
  226.2 2.3 copy-start.7
  231.2 5.3 copy-start.17
  231.2 5.3 copy-start.63
  242.6 3.8 copy-start.71
  244.2 2.3 copy-start.66
  250.2 18.9 %copy-start.42 = (bf16[512,1024]{0,1:T(8,128)(2,1)}, bf16[512,1024]{0,1:T(8,128)(2,1)S(1)}, u32[]{:S(2)}) copy-start(bf16[512,1024]{0,1:T(8,128)(2,1)S(1)} %copy.395) | copy-start | bytes 3145732
  276.4 4.8 copy-start.65
  282.6 3.8 copy-start.10
  282.6 2.4 copy-start.9
  284.9 2.3 copy-start.62
  287.3 2.7 copy-start.28
  287.3 2.7 copy-start.45
  295.5 4.8 copy-start.39
  295.5 4.8 copy-start.11
  307.1 6.0 copy-start.107
  307.1 10.4 %slice-start.4 = ((s8[8388608]{0:T(1024)(128)(4,1)}), s8[4194304]{0:T(1024)(128)(4,1)S(1)}, s32[]{:S(2)}) async-start(s8[8388608]{0:T(1024)(128)(4,1)} %bitcast.724), calls=%async_computation.7 | async-start | bytes 8388608
  313.1 4.6 slice-start.5
  317.8 2.5 copy-start.43
  320.3 2.5 copy-start.44
  346.7 2.3 copy-start.23
  346.7 2.6 copy-start.47
  349.3 2.8 copy-start.29
  349.3 3.4 copy-start.108
  356.0 2.9 copy-start.19
  366.4 19.6 %slice-start = ((s8[12845056]{0:T(1024)(128)(4,1)}), s8[262144]{0:T(1024)(128)(4,1)S(1)}, s32[]{:S(2)}) async-start(s8[12845056]{0:T(1024)(128)(4,1)} %bitcast.701), calls=%async_computation.3 | async-start | bytes 524288
  370.3 15.7 %copy-start.26 = (bf16[512,1024]{0,1:T(8,128)(2,1)}, bf16[512,1024]{0,1:T(8,128)(2,1)S(1)}, u32[]{:S(2)}) copy-start(bf16[512,1024]{0,1:T(8,128)(2,1)S(1)} %copy.294) | copy-start | bytes 3145732
  371.0 15.1 %slice-start.1 = ((s8[12845056]{0:T(1024)(128)(4,1)}), s8[4194304]{0:T(1024)(128)(4,1)S(1)}, s32[]{:S(2)}) async-start(s8[12845056]{0:T(1024)(128)(4,1)} %bitcast.701), calls=%async_computation.4 | async-start | bytes 8388608
  371.0 15.1 %slice-start.2 = ((s8[12845056]{0:T(1024)(128)(4,1)}), s8[4194304]{0:T(1024)(128)(4,1)S(1)}, s32[]{:S(2)}) async-start(s8[12845056]{0:T(1024)(128)(4,1)} %bitcast.701), calls=%async_computation.5 | async-start | bytes 8388608
  371.0 15.1 %slice-start.3 = ((s8[12845056]{0:T(1024)(128)(4,1)}), s8[4194304]{0:T(1024)(128)(4,1)S(1)}, s32[]{:S(2)}) async-start(s8[12845056]{0:T(1024)(128)(4,1)} %bitcast.701), calls=%async_computation.6 | async-start | bytes 8388608
  386.1 11.3 %copy-start.53 = (bf16[32,96,128]{2,1,0:T(8,128)(2,1)S(1)}, bf16[32,96,128]{2,1,0:T(8,128)(2,1)}, u32[]{:S(2)}) copy-start(bf16[32,96,128]{2,1,0:T(8,128)(2,1)} %get-tuple-element.53) | copy-start | bytes 2359300
  400.2 2.6 copy-start.96
  400.2 3.2 copy-start.72
  418.8 4.4 copy-start.76
  418.8 4.4 copy-start.80
  423.2 2.6 copy-start.68
  425.8 2.6 copy-start.78
  425.8 2.6 copy-start.106
  461.2 2.2 copy-start.33
  470.1 2.2 copy-start.34
  499.4 4.1 copy-start.100
  499.4 4.1 copy-start.13
  503.5 4.6 copy-start.15
  503.5 4.6 copy-start.21
  503.5 4.9 copy-start.36
  503.5 4.8 copy-start.94
  503.6 4.8 copy-start.98
  503.6 4.8 copy-start.99
  (53 other events, 84.4 us)
Sparse Core Ops, SparseCore 0:
  17.1 145.3 all-gather.1
  499.5 227.9 reduce-scatter.1

commit v4 on v3

--- a/solution.py
+++ b/solution.py
@@ -205,11 +205,10 @@
         row += rows
     gain_row = rounded(jnp.concatenate(gains)).reshape(1, -1)
     gain_block = local_panels(gain_row)
-    pieces.append(pad_rows(gain_block, padded_rows(gain_block.shape[0])))
-    places.append((row, pieces[-1].shape[0]))
-    row += pieces[-1].shape[0]
-    total = -(-row // ROW_GROUP) * ROW_GROUP
-    packed = pad_rows(jnp.concatenate(pieces, axis=0), total)
+    total = -(-(row + gain_block.shape[0]) // ROW_GROUP) * ROW_GROUP
+    pieces.append(pad_rows(gain_block, total - row))
+    places.append((row, gain_block.shape[0]))
+    packed = jnp.concatenate(pieces, axis=0)
     gathered = lax.all_gather(packed, ALL, axis=0, tiled=True).reshape(count, total, PANEL)
     out = []
     for w, kind, (first, rows) in zip(weights, WEIGHT_KINDS, places):
@@ -232,11 +231,10 @@
         row += rows
     gain_stack = jnp.stack([g.reshape(count, -1) for g in gain_grads], axis=1).reshape(count, 1, -1)
     gain_block = lane_pad(gain_stack, gain_stack.shape[-1]).reshape(count, -1, PANEL)
-    pieces.append(pad_rows(rounded(gain_block), padded_rows(gain_block.shape[1])))
+    total = -(-(row + gain_block.shape[1]) // ROW_GROUP) * ROW_GROUP
+    pieces.append(pad_rows(rounded(gain_block), total - row))
     places.append((row, gain_block.shape[1]))
-    row += pieces[-1].shape[1]
-    total = -(-row // ROW_GROUP) * ROW_GROUP
-    packed = pad_rows(jnp.concatenate(pieces, axis=1), total)
+    packed = jnp.concatenate(pieces, axis=1)
     mine = lax.psum_scatter(
         packed.reshape(count * total, PANEL), ALL, scatter_dimension=0, tiled=True
     )

time: 753 us -> 733 us (0.973)
  local copies, waits for them, and re-layouts: 169 us -> 149 us
    pad x2 -> x0, local copies, waits for them, and re-layouts: 21.2 us -> none  [pad_rows(): return jnp.pad(block, pad)]
    unnamed x257 -> x258, local copies, waits for them, and re-layouts: 51.6 us -> 52.8 us
where the time goes in v4:
time: 733 us; the launch traced here: 725 us
  waiting for transfers between devices  351 us (48%)
  matrix products  158 us (22%)
  local copies, waits for them, and re-layouts  149 us (20%)
  other arithmetic  47.8 us (7%)
  between operations  18.2 us (2%)
    reduce_scatter x1, waiting for transfers between devices, reduce_grads(): lax.psum_scatter(packed.reshape(count * total, PANEL), ALL, scatter_dimen...  217 us
    all_gather x1, waiting for transfers between devices, gather_weights(): lax.all_gather(packed, ALL, axis=0, tiled=True).reshape(count, total, PANEL)  134 us
    dot_general x40, matrix products, contract(): lax.dot_general(left, right, ((left_dims, right_dims), ((), ())), preferr...  92.9 us
    unnamed x258, local copies, waits for them, and re-layouts  52.8 us
    dot_general x17, local copies, waits for them, and re-layouts, contract(): lax.dot_general(left, right, ((left_dims, right_dims), ((), ())), preferr...  36.8 us
    dot_general x2, matrix products, product(): return jnp.dot(left_side, right_side, preferred_element_type=jnp.float32)  21.2 us
    dot_general x2, matrix products, product_nt(): lax.dot_general(left_side, right_side, (((1,), (1,)), ((), ())), preferre...  17.8 us
    slice x2, local copies, waits for them, and re-layouts, gather_weights(): piece = gathered[:, first:first + rows, :]  17.5 us
  transfers between devices with their start and end apart: 2, of which 2 were waited for; matrix products, arithmetic and copies ran while one was open for 3% of the time, Pallas kernels for 0%

profile of v4, /device:TPU:0, one launch (start us, length us, event | category | flops | bytes accessed | tf_op | source)
XLA Modules:
  0.0 724.5 jit_solution(17792136323491754225)
XLA Ops:
  20.5 3.3 convert_reduce_fusion
  25.0 3.7 fusion.6
  28.8 133.6 %all-gather.2.cloned.1.call-done = bf16[89088,128]{1,0:T(8,128)(2,1)} async-done(((bf16[2784,128]{1,0:T(8,128)(2,1)}), bf16[89088,128]{1,0:T(8,128)(2,1)}) %all-gather.2.cloned.1.call-update) | async-done | bytes 22806544 | tf_op jit(solution)/shard_map/all_gather | solution.py:212
  163.3 14.1 %fusion.165 = (bf16[32,256,128]{2,1,0:T(8,128)(2,1)}, bf16[32,256,128]{2,1,0:T(8,128)(2,1)}, bf16[32,256,128]{2,1,0:T(8,128)(2,1)}, bf16[32,256,128]{2,1,0:T(8,1...) fusion(bf16[32,2784,128]{2,1,0:T(8,128)(2,1)} %bitcast.700), kind=kLoop, calls=%fused_computation.333 | loop fusion | bytes 41943040 | tf_op jit(solution)/shard_map/slice | solution.py:215
  177.4 3.5 fusion.166
  182.6 2.3 copy.241
  184.8 4.2 bitcast_convert_fusion.5
  189.0 2.7 copy.243
  191.7 2.1 convolution_bitcast_fusion.1
  193.8 6.2 select_reduce_fusion
  200.0 2.6 fusion.2
  202.6 2.1 copy-done
  204.7 6.5 subtract_convert_fusion.1
  214.0 2.3 copy.248
  216.4 4.0 copy.252
  220.3 2.6 copy.250
  223.0 3.3 fusion.168
  228.6 2.6 copy.254
  231.3 5.2 fusion.57
  238.3 3.9 copy.256
  244.2 2.3 fusion.73
  246.5 2.3 bitcast_convert_fusion.3
  250.3 4.3 copy.258
  254.6 4.2 bitcast_convert_fusion.2
  258.8 2.3 copy.396
  261.1 4.0 copy.264
  265.0 4.1 copy.266
  269.2 7.3 %fusion.170 = (f32[8,512]{1,0:T(8,128)S(1)}, f32[8,512,512]{1,2,0:T(8,128)}) fusion(bf16[512,8,128]{0,2,1:T(8,128)(2,1)S(1)} %bitcast.743, bf16[512,8,128]{0,2,1:T(8,128)(2,1)} %bitcast.745), kind=kOutput, calls=%fused_computation.338 | convolution fusion | flops 543162880 | bytes 10502144 | tf_op jit(solution)/shard_map/sub | solution.py:319
  276.5 4.7 fusion.67
  283.0 2.0 copy-done.9
  287.4 2.7 fusion.56
  290.0 3.3 fusion.36
  293.3 2.2 reshape_reshape.22
  295.6 4.8 fusion.45
  303.5 2.3 bitcast_convert_fusion.1
  307.3 6.0 fusion.70
  313.3 4.4 multiply_reduce_fusion.1
  317.9 2.5 multiply_convert_fusion.1
  320.5 2.5 multiply_convert_fusion.3
  325.0 2.8 reshape.658
  333.8 1.8 copy.292
  342.9 2.4 multiply_reduce_fusion.3
  352.8 3.3 fusion.29
  356.1 2.9 reshape_reshape.23
  359.0 4.1 fusion.46
  366.7 2.3 bitcast_convert_fusion
  371.2 15.0 %multiply_reduce_fusion = (f32[512]{0:T(512)S(1)}, f32[512,6272]{1,0:T(8,128)}) fusion(f32[512]{0:T(512)S(1)} %fusion.2, f32[512]{0:T(512)S(1)} %get-tuple-element.70, f32[512,6272]{1,0:T(8,128)} %copy-done, pred[6272]{0:T(1024)(128)(4,1)S(1)} %compare_reduce_fusion, f32[6272]{0:T(1024)S(1)} %add_rsqrt_fusion, f32[6272]{0:T(1024)S(1)} %broadcast_multiply_fusion, ...), kind=kOutput, calls=%fused_computation.2 | convolution fusion | flops 1698883584 | bytes 29342724 | tf_op jit(solution)/shard_map/dot_general | solution.py:27
  386.3 11.3 %subtract_convert_fusion = (bf16[512,261]{0,1:T(8,128)(2,1)S(1)}, bf16[512,261]{0,1:T(8,128)(2,1)S(1)}) fusion(f32[6272]{0:T(1024)S(1)} %add_rsqrt_fusion, f32[6272]{0:T(1024)S(1)} %broadcast_multiply_fusion, bf16[261,16384]{1,0:T(8,128)(2,1)} %param.21, s32[]{:T(128)S(6)} %min.4, f32[512,6272]{1,0:T(8,128)} %get-tuple-element.90, ...), kind=kOutput, calls=%fused_computation.207 | convolution fusion | flops 1702629888 | bytes 29598852 | tf_op jit(solution)/shard_map/dot_general | solution.py:37
  400.4 2.7 fusion.38
  407.1 2.6 convolution_convert_fusion.5
  416.6 2.5 copy.364
  419.1 4.3 convolution_convert_fusion.3
  423.4 2.6 convolution_convert_fusion.2
  426.0 2.6 convolution_convert_fusion.1
  432.7 2.6 convolution_convert_fusion
  435.3 2.8 reshape.666
  438.1 2.8 convert_bitcast_fusion
  445.9 3.1 fusion.22
  453.2 2.1 fusion.176
  479.5 4.1 copy.268
  483.7 4.5 fusion.55
  488.5 2.2 add_add_fusion.4
  490.7 216.9 %reduce-scatter.2.cloned.1.call-done = bf16[2784,128]{1,0:T(8,128)(2,1)} async-done(((bf16[89088,128]{1,0:T(8,128)(2,1)}), bf16[2784,128]{1,0:T(8,128)(2,1)}) %reduce-scatter.2.cloned.1.call-update) | async-done | bytes 712720 | tf_op jit(solution)/shard_map/reduce_scatter | solution.py:238
  707.6 1.9 slice_convert_fusion.2
  (383 shorter events, 121.6 us)
Async XLA Ops:
  7.2 8.5 %copy-start.85 = (f32[256,128]{1,0:T(8,128)S(1)}, f32[256,128]{1,0:T(8,128)}, u32[]{:S(2)}) copy-start(f32[256,128]{1,0:T(8,128)} %param.29) | copy-start | bytes 393220
  7.2 8.6 %copy-start.86 = (f32[256,128]{1,0:T(8,128)S(1)}, f32[256,128]{1,0:T(8,128)}, u32[]{:S(2)}) copy-start(f32[256,128]{1,0:T(8,128)} %param.33) | copy-start | bytes 393220
  7.2 8.6 %copy-start.87 = (f32[256,128]{1,0:T(8,128)S(1)}, f32[256,128]{1,0:T(8,128)}, u32[]{:S(2)}) copy-start(f32[256,128]{1,0:T(8,128)} %param.35) | copy-start | bytes 393220
  7.2 8.6 %copy-start.102 = (f32[32]{0:T(128)S(1)}, f32[32]{0:T(128)}, u32[]{:S(2)}) copy-start(f32[32]{0:T(128)} %param.39) | copy-start | bytes 388
  7.2 8.6 %copy-start.103 = (f32[32]{0:T(128)S(1)}, f32[32]{0:T(128)}, u32[]{:S(2)}) copy-start(f32[32]{0:T(128)} %param.38) | copy-start | bytes 388
  7.2 8.7 %copy-start.104 = (f32[32]{0:T(128)S(1)}, f32[32]{0:T(128)}, u32[]{:S(2)}) copy-start(f32[32]{0:T(128)} %param.37) | copy-start | bytes 388
  7.3 8.7 %copy-start.105 = (f32[32]{0:T(128)S(1)}, f32[32]{0:T(128)}, u32[]{:S(2)}) copy-start(f32[32]{0:T(128)} %param.36) | copy-start | bytes 388
  7.3 9.7 %copy-start.88 = (s32[1,16384]{1,0:T(1,128)S(1)}, s32[1,16384]{1,0:T(1,128)}, u32[]{:S(2)}) copy-start(s32[1,16384]{1,0:T(1,128)} %param.22) | copy-start | bytes 196612
  7.3 155.1 %all-gather.2.cloned.1.call-start = ((), (), s32[]{:S(2)}) async-start(), calls=%async_computation.1 | async-start | bytes 23519232 | tf_op jit(solution)/shard_map/all_gather | solution.py:212
  16.0 7.8 %copy-start.1 = (bf16[512,1024]{1,0:T(8,128)(2,1)S(1)}, bf16[512,1024]{1,0:T(8,128)(2,1)}, u32[]{:S(2)}) copy-start(bf16[512,1024]{1,0:T(8,128)(2,1)} %param.20) | copy-start | bytes 3145732
  16.9 690.7 %reduce-scatter.2.cloned.1.call-start = ((), (), s32[]{:S(2)}) async-start(), calls=%async_computation.2 | async-start | bytes 23519232 | tf_op jit(solution)/shard_map/reduce_scatter | solution.py:238
  24.0 157.2 %copy-start.92 = (f32[512]{0:T(512)}, f32[512]{0:T(512)S(1)}, u32[]{:S(2)}) copy-start(f32[512]{0:T(512)S(1)} %broadcast_multiply_fusion.4) | copy-start | bytes 6148
  25.0 156.2 %copy-start.94 = (f32[512]{0:T(512)}, f32[512]{0:T(512)S(1)}, u32[]{:S(2)}) copy-start(f32[512]{0:T(512)S(1)} %fusion.149) | copy-start | bytes 6148
  177.3 43.0 %copy-start.3 = (bf16[32,256,128]{2,1,0:T(8,128)(2,1)}, bf16[32,256,128]{2,1,0:T(8,128)(2,1)S(1)}, u32[]{:S(2)}) copy-start(bf16[32,256,128]{2,1,0:T(8,128)(2,1)S(1)} %get-tuple-element.49) | copy-start | bytes 6291460
  181.2 3.7 copy-start.89
  200.0 4.6 copy-start
  204.7 6.6 copy-start.54
  226.3 2.3 copy-start.7
  231.3 5.2 copy-start.17
  231.3 5.2 copy-start.63
  242.6 3.8 copy-start.71
  244.2 2.3 copy-start.66
  250.3 18.9 %copy-start.42 = (bf16[512,1024]{0,1:T(8,128)(2,1)}, bf16[512,1024]{0,1:T(8,128)(2,1)S(1)}, u32[]{:S(2)}) copy-start(bf16[512,1024]{0,1:T(8,128)(2,1)S(1)} %copy.395) | copy-start | bytes 3145732
  276.5 4.8 copy-start.65
  282.7 3.8 copy-start.10
  282.7 2.4 copy-start.9
  285.0 2.3 copy-start.62
  287.4 2.7 copy-start.28
  287.4 2.7 copy-start.45
  295.5 4.8 copy-start.39
  295.6 4.8 copy-start.11
  307.3 6.0 copy-start.108
  307.3 10.4 %slice-start.4 = ((s8[8388608]{0:T(1024)(128)(4,1)}), s8[4194304]{0:T(1024)(128)(4,1)S(1)}, s32[]{:S(2)}) async-start(s8[8388608]{0:T(1024)(128)(4,1)} %bitcast.720), calls=%async_computation.7 | async-start | bytes 8388608
  313.3 4.6 slice-start.5
  317.9 2.5 copy-start.43
  320.5 2.5 copy-start.44
  346.9 2.3 copy-start.23
  346.9 2.6 copy-start.47
  349.5 2.8 copy-start.29
  349.5 3.4 copy-start.109
  356.1 2.9 copy-start.19
  366.7 19.6 %slice-start = ((s8[12845056]{0:T(1024)(128)(4,1)}), s8[262144]{0:T(1024)(128)(4,1)S(1)}, s32[]{:S(2)}) async-start(s8[12845056]{0:T(1024)(128)(4,1)} %bitcast.696), calls=%async_computation.3 | async-start | bytes 524288
  370.6 15.7 %copy-start.26 = (bf16[512,1024]{0,1:T(8,128)(2,1)}, bf16[512,1024]{0,1:T(8,128)(2,1)S(1)}, u32[]{:S(2)}) copy-start(bf16[512,1024]{0,1:T(8,128)(2,1)S(1)} %copy.294) | copy-start | bytes 3145732
  371.2 15.0 %slice-start.1 = ((s8[12845056]{0:T(1024)(128)(4,1)}), s8[4194304]{0:T(1024)(128)(4,1)S(1)}, s32[]{:S(2)}) async-start(s8[12845056]{0:T(1024)(128)(4,1)} %bitcast.696), calls=%async_computation.4 | async-start | bytes 8388608
  371.2 15.0 %slice-start.2 = ((s8[12845056]{0:T(1024)(128)(4,1)}), s8[4194304]{0:T(1024)(128)(4,1)S(1)}, s32[]{:S(2)}) async-start(s8[12845056]{0:T(1024)(128)(4,1)} %bitcast.696), calls=%async_computation.5 | async-start | bytes 8388608
  371.2 15.0 %slice-start.3 = ((s8[12845056]{0:T(1024)(128)(4,1)}), s8[4194304]{0:T(1024)(128)(4,1)S(1)}, s32[]{:S(2)}) async-start(s8[12845056]{0:T(1024)(128)(4,1)} %bitcast.696), calls=%async_computation.6 | async-start | bytes 8388608
  386.3 11.3 %copy-start.53 = (bf16[32,96,128]{2,1,0:T(8,128)(2,1)S(1)}, bf16[32,96,128]{2,1,0:T(8,128)(2,1)}, u32[]{:S(2)}) copy-start(bf16[32,96,128]{2,1,0:T(8,128)(2,1)} %get-tuple-element.53) | copy-start | bytes 2359300
  400.4 2.7 copy-start.97
  400.4 3.3 copy-start.72
  419.1 4.4 copy-start.76
  419.1 4.4 copy-start.80
  423.4 2.6 copy-start.68
  426.0 2.6 copy-start.78
  426.0 2.6 copy-start.107
  461.5 2.2 copy-start.33
  463.7 2.2 copy-start.60
  479.5 4.1 copy-start.101
  479.5 4.1 copy-start.13
  483.6 4.6 copy-start.15
  483.6 4.6 copy-start.21
  483.6 4.9 copy-start.36
  483.6 4.9 copy-start.95
  483.7 4.9 copy-start.99
  483.7 4.9 copy-start.100
  (54 other events, 85.3 us)
Sparse Core Ops, SparseCore 0:
  17.0 145.3 all-gather.1
  479.6 227.9 reduce-scatter.1

commit v5 on v4

--- a/solution.py
+++ b/solution.py
@@ -236,8 +236,9 @@
     places.append((row, gain_block.shape[1]))
     packed = jnp.concatenate(pieces, axis=1)
     mine = lax.psum_scatter(
-        packed.reshape(count * total, PANEL), ALL, scatter_dimension=0, tiled=True
-    )
+        packed.reshape(count * total, PANEL), "items", scatter_dimension=0, tiled=True
+    )
+    mine = lax.psum_scatter(mine, "heads", scatter_dimension=0, tiled=True)
     out = []
     for w, kind, (first, rows) in zip(weights, WEIGHT_KINDS, places):
         r, width = local_shape(w, kind)

time: 733 us -> 706 us (0.963)
  waiting for transfers between devices: 351 us -> 324 us
    reduce_scatter x1 -> x2, waiting for transfers between devices: 217 us -> 190 us  [the longest x1 143 us: reduce_grads(): lax.psum_scatter(packed.reshape(count * total, PANEL), 'items', scatter_d...]
  transfers between devices with their start and end apart: 2 -> 3, of which waited for: 2 -> 3; matrix products, arithmetic and copies ran while one was open for 3% -> 3% of each run, Pallas kernels for 0% -> 0%
where the time goes in v5:
time: 706 us; the launch traced here: 697 us
  waiting for transfers between devices  324 us (46%)
  matrix products  158 us (22%)
  local copies, waits for them, and re-layouts  149 us (21%)
  other arithmetic  47.8 us (7%)
  between operations  17.9 us (3%)
    reduce_scatter x1, waiting for transfers between devices, reduce_grads(): lax.psum_scatter(packed.reshape(count * total, PANEL), 'items', scatter_d...  143 us
    all_gather x1, waiting for transfers between devices, gather_weights(): lax.all_gather(packed, ALL, axis=0, tiled=True).reshape(count, total, PANEL)  134 us
    dot_general x40, matrix products, contract(): lax.dot_general(left, right, ((left_dims, right_dims), ((), ())), preferr...  92.6 us
    unnamed x258, local copies, waits for them, and re-layouts  52.6 us
    reduce_scatter x1, waiting for transfers between devices, reduce_grads(): mine = lax.psum_scatter(mine, 'heads', scatter_dimension=0, tiled=True)  47.5 us
    dot_general x17, local copies, waits for them, and re-layouts, contract(): lax.dot_general(left, right, ((left_dims, right_dims), ((), ())), preferr...  36.8 us
    dot_general x2, matrix products, product(): return jnp.dot(left_side, right_side, preferred_element_type=jnp.float32)  21.2 us
    dot_general x2, matrix products, product_nt(): lax.dot_general(left_side, right_side, (((1,), (1,)), ((), ())), preferre...  17.8 us
  transfers between devices with their start and end apart: 3, of which 3 were waited for; matrix products, arithmetic and copies ran while one was open for 3% of the time, Pallas kernels for 0%

profile of v5, /device:TPU:0, one launch (start us, length us, event | category | flops | bytes accessed | tf_op | source)
XLA Modules:
  0.0 697.4 jit_solution(7777271935173312599)
XLA Ops:
  20.5 3.3 convert_reduce_fusion
  25.0 3.7 fusion.6
  28.8 133.6 %all-gather.2.cloned.1.call-done = bf16[89088,128]{1,0:T(8,128)(2,1)} async-done(((bf16[2784,128]{1,0:T(8,128)(2,1)}), bf16[89088,128]{1,0:T(8,128)(2,1)}) %all-gather.2.cloned.1.call-update) | async-done | bytes 22806544 | tf_op jit(solution)/shard_map/all_gather | solution.py:212
  163.3 14.1 %fusion.165 = (bf16[32,256,128]{2,1,0:T(8,128)(2,1)}, bf16[32,256,128]{2,1,0:T(8,128)(2,1)}, bf16[32,256,128]{2,1,0:T(8,128)(2,1)}, bf16[32,256,128]{2,1,0:T(8,1...) fusion(bf16[32,2784,128]{2,1,0:T(8,128)(2,1)} %bitcast.700), kind=kLoop, calls=%fused_computation.333 | loop fusion | bytes 41943040 | tf_op jit(solution)/shard_map/slice | solution.py:215
  177.4 3.5 fusion.166
  182.6 2.3 copy.241
  184.8 4.2 bitcast_convert_fusion.5
  189.0 2.7 copy.243
  191.7 2.1 convolution_bitcast_fusion.1
  193.8 6.2 select_reduce_fusion
  200.0 2.6 fusion.2
  202.6 2.1 copy-done
  204.7 6.5 subtract_convert_fusion.1
  214.0 2.3 copy.248
  216.4 4.0 copy.252
  220.3 2.6 copy.250
  223.0 3.3 fusion.168
  228.6 2.6 copy.254
  231.3 5.2 fusion.57
  238.3 3.9 copy.256
  244.2 2.3 fusion.73
  246.5 2.3 bitcast_convert_fusion.3
  250.3 4.3 copy.258
  254.6 4.2 bitcast_convert_fusion.2
  258.8 2.3 copy.396
  261.1 4.0 copy.264
  265.0 4.1 copy.266
  269.2 7.3 %fusion.170 = (f32[8,512]{1,0:T(8,128)S(1)}, f32[8,512,512]{1,2,0:T(8,128)}) fusion(bf16[512,8,128]{0,2,1:T(8,128)(2,1)S(1)} %bitcast.743, bf16[512,8,128]{0,2,1:T(8,128)(2,1)} %bitcast.745), kind=kOutput, calls=%fused_computation.338 | convolution fusion | flops 543162880 | bytes 10502144 | tf_op jit(solution)/shard_map/sub | solution.py:320
  276.5 4.7 fusion.67
  283.0 2.0 copy-done.9
  287.4 2.7 fusion.56
  290.0 3.3 fusion.36
  293.3 2.2 reshape_reshape.22
  295.6 4.8 fusion.45
  303.5 2.3 bitcast_convert_fusion.1
  307.3 6.0 fusion.70
  313.3 4.4 multiply_reduce_fusion.1
  317.9 2.5 multiply_convert_fusion.1
  320.5 2.5 multiply_convert_fusion.3
  325.0 2.8 reshape.658
  342.9 2.4 multiply_reduce_fusion.3
  352.8 3.3 fusion.29
  356.1 2.9 reshape_reshape.23
  359.0 4.1 fusion.46
  366.7 2.3 bitcast_convert_fusion
  371.2 15.0 %multiply_reduce_fusion = (f32[512]{0:T(512)S(1)}, f32[512,6272]{1,0:T(8,128)}) fusion(f32[512]{0:T(512)S(1)} %fusion.2, f32[512]{0:T(512)S(1)} %get-tuple-element.70, f32[512,6272]{1,0:T(8,128)} %copy-done, pred[6272]{0:T(1024)(128)(4,1)S(1)} %compare_reduce_fusion, f32[6272]{0:T(1024)S(1)} %add_rsqrt_fusion, f32[6272]{0:T(1024)S(1)} %broadcast_multiply_fusion, ...), kind=kOutput, calls=%fused_computation.2 | convolution fusion | flops 1698883584 | bytes 29342724 | tf_op jit(solution)/shard_map/dot_general | solution.py:27
  386.3 11.3 %subtract_convert_fusion = (bf16[512,261]{0,1:T(8,128)(2,1)S(1)}, bf16[512,261]{0,1:T(8,128)(2,1)S(1)}) fusion(f32[6272]{0:T(1024)S(1)} %add_rsqrt_fusion, f32[6272]{0:T(1024)S(1)} %broadcast_multiply_fusion, bf16[261,16384]{1,0:T(8,128)(2,1)} %param.21, s32[]{:T(128)S(6)} %min.4, f32[512,6272]{1,0:T(8,128)} %get-tuple-element.90, ...), kind=kOutput, calls=%fused_computation.207 | convolution fusion | flops 1702629888 | bytes 29598852 | tf_op jit(solution)/shard_map/dot_general | solution.py:37
  400.4 2.6 fusion.38
  407.0 2.6 convolution_convert_fusion.5
  416.5 2.5 copy.364
  419.0 4.3 convolution_convert_fusion.3
  423.4 2.6 convolution_convert_fusion.2
  426.0 2.6 convolution_convert_fusion.1
  432.7 2.6 convolution_convert_fusion
  435.3 2.8 reshape.666
  438.1 2.8 convert_bitcast_fusion
  445.9 3.1 fusion.22
  453.3 2.1 fusion.176
  479.6 143.0 %reduce-scatter.3.cloned.1.call-done = bf16[11136,128]{1,0:T(8,128)(2,1)} async-done(((bf16[89088,128]{1,0:T(8,128)(2,1)}), bf16[11136,128]{1,0:T(8,128)(2,1)}) %reduce-scatter.3.cloned.1.call-update) | async-done | bytes 2850832 | tf_op jit(solution)/shard_map/reduce_scatter | solution.py:238
  622.7 4.1 copy.268
  626.8 4.3 fusion.55
  631.2 2.2 add_add_fusion.4
  633.4 47.5 %reduce-scatter.5.cloned.1.call-done = bf16[2784,128]{1,0:T(8,128)(2,1)} async-done(((bf16[11136,128]{1,0:T(8,128)(2,1)}), bf16[2784,128]{1,0:T(8,128)(2,1)}) %reduce-scatter.5.cloned.1.call-update) | async-done | bytes 712720 | tf_op jit(solution)/shard_map/reduce_scatter | solution.py:241
  680.8 1.9 slice_convert_fusion.2
  (386 shorter events, 123.3 us)
Async XLA Ops:
  7.2 8.5 %copy-start.85 = (f32[256,128]{1,0:T(8,128)S(1)}, f32[256,128]{1,0:T(8,128)}, u32[]{:S(2)}) copy-start(f32[256,128]{1,0:T(8,128)} %param.29) | copy-start | bytes 393220
  7.2 8.6 %copy-start.86 = (f32[256,128]{1,0:T(8,128)S(1)}, f32[256,128]{1,0:T(8,128)}, u32[]{:S(2)}) copy-start(f32[256,128]{1,0:T(8,128)} %param.33) | copy-start | bytes 393220
  7.2 8.6 %copy-start.87 = (f32[256,128]{1,0:T(8,128)S(1)}, f32[256,128]{1,0:T(8,128)}, u32[]{:S(2)}) copy-start(f32[256,128]{1,0:T(8,128)} %param.35) | copy-start | bytes 393220
  7.2 8.6 %copy-start.102 = (f32[32]{0:T(128)S(1)}, f32[32]{0:T(128)}, u32[]{:S(2)}) copy-start(f32[32]{0:T(128)} %param.39) | copy-start | bytes 388
  7.2 8.6 %copy-start.103 = (f32[32]{0:T(128)S(1)}, f32[32]{0:T(128)}, u32[]{:S(2)}) copy-start(f32[32]{0:T(128)} %param.38) | copy-start | bytes 388
  7.2 8.7 %copy-start.104 = (f32[32]{0:T(128)S(1)}, f32[32]{0:T(128)}, u32[]{:S(2)}) copy-start(f32[32]{0:T(128)} %param.37) | copy-start | bytes 388
  7.3 8.7 %copy-start.105 = (f32[32]{0:T(128)S(1)}, f32[32]{0:T(128)}, u32[]{:S(2)}) copy-start(f32[32]{0:T(128)} %param.36) | copy-start | bytes 388
  7.3 9.7 %copy-start.88 = (s32[1,16384]{1,0:T(1,128)S(1)}, s32[1,16384]{1,0:T(1,128)}, u32[]{:S(2)}) copy-start(s32[1,16384]{1,0:T(1,128)} %param.22) | copy-start | bytes 196612
  7.3 155.1 %all-gather.2.cloned.1.call-start = ((), (), s32[]{:S(2)}) async-start(), calls=%async_computation.2 | async-start | bytes 23519232 | tf_op jit(solution)/shard_map/all_gather | solution.py:212
  16.0 7.8 %copy-start.1 = (bf16[512,1024]{1,0:T(8,128)(2,1)S(1)}, bf16[512,1024]{1,0:T(8,128)(2,1)}, u32[]{:S(2)}) copy-start(bf16[512,1024]{1,0:T(8,128)(2,1)} %param.20) | copy-start | bytes 3145732
  16.9 605.7 %reduce-scatter.3.cloned.1.call-start = ((), (), s32[]{:S(2)}) async-start(), calls=%async_computation.3 | async-start | bytes 25657344 | tf_op jit(solution)/shard_map/reduce_scatter | solution.py:238
  24.0 157.2 %copy-start.92 = (f32[512]{0:T(512)}, f32[512]{0:T(512)S(1)}, u32[]{:S(2)}) copy-start(f32[512]{0:T(512)S(1)} %broadcast_multiply_fusion.4) | copy-start | bytes 6148
  25.0 156.2 %copy-start.94 = (f32[512]{0:T(512)}, f32[512]{0:T(512)S(1)}, u32[]{:S(2)}) copy-start(f32[512]{0:T(512)S(1)} %fusion.149) | copy-start | bytes 6148
  177.3 43.0 %copy-start.3 = (bf16[32,256,128]{2,1,0:T(8,128)(2,1)}, bf16[32,256,128]{2,1,0:T(8,128)(2,1)S(1)}, u32[]{:S(2)}) copy-start(bf16[32,256,128]{2,1,0:T(8,128)(2,1)S(1)} %get-tuple-element.49) | copy-start | bytes 6291460
  181.2 3.7 copy-start.89
  200.0 4.6 copy-start
  204.7 6.6 copy-start.54
  226.3 2.3 copy-start.7
  231.3 5.2 copy-start.17
  231.3 5.2 copy-start.63
  242.6 3.8 copy-start.71
  244.2 2.3 copy-start.66
  250.3 18.9 %copy-start.42 = (bf16[512,1024]{0,1:T(8,128)(2,1)}, bf16[512,1024]{0,1:T(8,128)(2,1)S(1)}, u32[]{:S(2)}) copy-start(bf16[512,1024]{0,1:T(8,128)(2,1)S(1)} %copy.395) | copy-start | bytes 3145732
  276.5 4.8 copy-start.65
  282.7 3.8 copy-start.10
  282.7 2.4 copy-start.9
  285.0 2.3 copy-start.62
  287.4 2.7 copy-start.28
  287.4 2.7 copy-start.45
  295.5 4.8 copy-start.39
  295.6 4.8 copy-start.11
  307.3 6.0 copy-start.108
  307.3 10.4 %slice-start.4 = ((s8[8388608]{0:T(1024)(128)(4,1)}), s8[4194304]{0:T(1024)(128)(4,1)S(1)}, s32[]{:S(2)}) async-start(s8[8388608]{0:T(1024)(128)(4,1)} %bitcast.720), calls=%async_computation.9 | async-start | bytes 8388608
  313.3 4.6 slice-start.5
  317.9 2.5 copy-start.43
  320.5 2.5 copy-start.44
  346.9 2.3 copy-start.23
  346.9 2.6 copy-start.47
  349.5 2.8 copy-start.29
  349.5 3.4 copy-start.109
  356.1 2.9 copy-start.19
  366.7 19.6 %slice-start = ((s8[12845056]{0:T(1024)(128)(4,1)}), s8[262144]{0:T(1024)(128)(4,1)S(1)}, s32[]{:S(2)}) async-start(s8[12845056]{0:T(1024)(128)(4,1)} %bitcast.696), calls=%async_computation.5 | async-start | bytes 524288
  370.6 15.7 %copy-start.26 = (bf16[512,1024]{0,1:T(8,128)(2,1)}, bf16[512,1024]{0,1:T(8,128)(2,1)S(1)}, u32[]{:S(2)}) copy-start(bf16[512,1024]{0,1:T(8,128)(2,1)S(1)} %copy.294) | copy-start | bytes 3145732
  371.2 15.0 %slice-start.1 = ((s8[12845056]{0:T(1024)(128)(4,1)}), s8[4194304]{0:T(1024)(128)(4,1)S(1)}, s32[]{:S(2)}) async-start(s8[12845056]{0:T(1024)(128)(4,1)} %bitcast.696), calls=%async_computation.6 | async-start | bytes 8388608
  371.2 15.0 %slice-start.2 = ((s8[12845056]{0:T(1024)(128)(4,1)}), s8[4194304]{0:T(1024)(128)(4,1)S(1)}, s32[]{:S(2)}) async-start(s8[12845056]{0:T(1024)(128)(4,1)} %bitcast.696), calls=%async_computation.7 | async-start | bytes 8388608
  371.2 15.0 %slice-start.3 = ((s8[12845056]{0:T(1024)(128)(4,1)}), s8[4194304]{0:T(1024)(128)(4,1)S(1)}, s32[]{:S(2)}) async-start(s8[12845056]{0:T(1024)(128)(4,1)} %bitcast.696), calls=%async_computation.8 | async-start | bytes 8388608
  386.3 11.3 %copy-start.53 = (bf16[32,96,128]{2,1,0:T(8,128)(2,1)S(1)}, bf16[32,96,128]{2,1,0:T(8,128)(2,1)}, u32[]{:S(2)}) copy-start(bf16[32,96,128]{2,1,0:T(8,128)(2,1)} %get-tuple-element.53) | copy-start | bytes 2359300
  400.4 2.6 copy-start.97
  400.4 3.2 copy-start.72
  419.0 4.4 copy-start.76
  419.0 4.4 copy-start.80
  423.4 2.6 copy-start.68
  426.0 2.6 copy-start.78
  426.0 2.6 copy-start.107
  463.8 2.2 copy-start.60
  479.5 201.3 %reduce-scatter.5.cloned.1.call-start = ((), (), s32[]{:S(2)}) async-start(), calls=%async_computation.4 | async-start | bytes 3563520 | tf_op jit(solution)/shard_map/reduce_scatter | solution.py:241
  622.6 4.1 copy-start.101
  622.6 4.1 copy-start.13
  626.7 4.4 copy-start.15
  626.7 4.4 copy-start.21
  626.8 4.4 copy-start.36
  626.8 4.4 copy-start.95
  626.8 4.4 copy-start.99
  626.8 4.4 copy-start.100
  (55 other events, 87.5 us)
Sparse Core Ops, SparseCore 0:
  17.0 145.3 all-gather.1
  479.7 142.8 reduce-scatter.2
  624.9 55.8 reduce-scatter.4

commit v6 on v5

--- a/solution.py
+++ b/solution.py
@@ -319,16 +319,16 @@
     row_top = jnp.max(scores, axis=-1, keepdims=True)
     raw_weights = jnp.exp(scores - row_top)
     row_total = jnp.sum(raw_weights, axis=-1, keepdims=True)
-    weights = raw_weights / row_total
-    mixed = jnp.einsum("hqk,khd->qhd", rounded(weights), v4, preferred_element_type=jnp.float32)
-    mixed = rounded(mixed.reshape(rows, heads_n * HEAD))
-    saved = (normed, q4, k4, v4, weights, mixed)
+    weights_low = rounded(raw_weights / row_total)
+    mixed_full = jnp.einsum("hqk,khd->qhd", weights_low, v4, preferred_element_type=jnp.float32)
+    mixed = rounded(mixed_full.reshape(rows, heads_n * HEAD))
+    saved = (normed, q4, k4, v4, weights_low, mixed_full, mixed)
     return residual + apply(mixed, out_w), saved
 
 
 def attention_block_back(residual, gain_vec, weight_set, split, saved, grad_out):
     query_w, key_w, value_w, out_w = weight_set
-    normed, q4, k4, v4, weights, mixed = saved
+    normed, q4, k4, v4, weights_low, mixed_full, mixed = saved
     rows = residual.shape[0]
     keys = k4.shape[0]
     scale = 1.0 / math.sqrt(HEAD)
@@ -336,11 +336,11 @@
     grad_out_w = grad_blocks(mixed, grad_round, out_w)
     grad_mixed = rounded(apply_t(grad_round, out_w)).reshape(q4.shape)
     grad_value = jnp.einsum(
-        "hqk,qhd->khd", rounded(weights), grad_mixed, preferred_element_type=jnp.float32
+        "hqk,qhd->khd", weights_low, grad_mixed, preferred_element_type=jnp.float32
     ).reshape(keys, -1)
+    row_dot = jnp.sum(widened(grad_mixed) * mixed_full, axis=-1).T[:, :, None]
     grad_weights = jnp.einsum("qhd,khd->hqk", grad_mixed, v4, preferred_element_type=jnp.float32)
-    grad_scores = weights * (grad_weights - jnp.sum(grad_weights * weights, axis=-1, keepdims=True))
-    grad_scores = rounded(grad_scores)
+    grad_scores = rounded(widened(weights_low) * (grad_weights - row_dot))
     grad_query = jnp.einsum("hqk,khd->qhd", grad_scores, k4, preferred_element_type=jnp.float32)
     grad_query = rounded((grad_query * scale).reshape(rows, -1))
     grad_key = jnp.einsum("hqk,qhd->khd", grad_scores, q4, preferred_element_type=jnp.float32)
@@ -379,26 +379,25 @@
     row_top = jnp.max(scores, axis=-1, keepdims=True)
     raw_weights = jnp.exp(scores - row_top)
     row_total = jnp.sum(raw_weights, axis=-1, keepdims=True)
-    weights = raw_weights / row_total
-    weights_low = rounded(weights)
+    weights_low = rounded(raw_weights / row_total)
     pixel_mix = product_nt(weights_low, pixel_norm)
     mixed = rounded(split_apply_t(pixel_mix, value_w))
-    saved = (normed, query_rows, weights, pixel_mix, mixed)
+    saved = (normed, query_rows, weights_low, pixel_mix, mixed)
     return residual + apply(mixed, out_w), saved
 
 
 def cross_block_back(
     residual, gain_vec, query_w, key_w, value_w, out_w, pixel_norm, saved, grad_out
 ):
-    normed, query_rows, weights, pixel_mix, mixed = saved
+    normed, query_rows, weights_low, pixel_mix, mixed = saved
     scale = 1.0 / math.sqrt(residual.shape[1])
     grad_round = rounded(grad_out)
     grad_out_w = grad_blocks(mixed, grad_round, out_w)
     grad_mixed = rounded(apply_t(grad_round, out_w))
     grad_keyed = rounded(apply(grad_mixed, value_w))
+    row_dot = jnp.sum(widened(grad_keyed) * pixel_mix, axis=-1, keepdims=True)
     grad_weights = product(grad_keyed, pixel_norm)
-    grad_scores = weights * (grad_weights - jnp.sum(grad_weights * weights, axis=-1, keepdims=True))
-    grad_scores = rounded(grad_scores)
+    grad_scores = rounded(widened(weights_low) * (grad_weights - row_dot))
     score_mix = product_nt(grad_scores, pixel_norm)
     grad_query = rounded(split_apply_t(score_mix, key_w) * scale)
     grad_query_w = grad_blocks(normed, grad_query, query_w)

time: 706 us -> 703 us (level)
  matrix products: 158 us -> 130 us
  other arithmetic: 47.8 us -> 65.8 us
    dot_general x2 -> x1, matrix products: 21.2 us -> 6.21 us  [product(): return jnp.dot(left_side, right_side, preferred_element_type=jnp.float32)]
    convert_element_type x4 -> x5, other arithmetic: 5.46 us -> 18.2 us  [rounded(): return values.astype(jnp.bfloat16)]
    dot_general x17, local copies, waits for them, and re-layouts: 36.8 us -> 46.2 us  [contract(): lax.dot_general(left, right, ((left_dims, right_dims), ((), ())), preferr...]
    dot_general x40, matrix products: 92.6 us -> 84 us  [contract(): lax.dot_general(left, right, ((left_dims, right_dims), ((), ())), preferr...]
    unnamed x258 -> x252, local copies, waits for them, and re-layouts: 52.6 us -> 50.2 us
    convert_element_type x8 -> x9, local copies, waits for them, and re-layouts: 14.9 us -> 17 us  [rounded(): return values.astype(jnp.bfloat16)]
where the time goes in v6:
time: 703 us; the launch traced here: 694 us
  waiting for transfers between devices  325 us (46%)
  local copies, waits for them, and re-layouts  156 us (22%)
  matrix products  130 us (18%)
  other arithmetic  65.8 us (9%)
  between operations  18.1 us (3%)
    reduce_scatter x1, waiting for transfers between devices, reduce_grads(): lax.psum_scatter(packed.reshape(count * total, PANEL), 'items', scatter_d...  143 us
    all_gather x1, waiting for transfers between devices, gather_weights(): lax.all_gather(packed, ALL, axis=0, tiled=True).reshape(count, total, PANEL)  134 us
    dot_general x40, matrix products, contract(): lax.dot_general(left, right, ((left_dims, right_dims), ((), ())), preferr...  84 us
    unnamed x252, local copies, waits for them, and re-layouts  50.2 us
    reduce_scatter x1, waiting for transfers between devices, reduce_grads(): mine = lax.psum_scatter(mine, 'heads', scatter_dimension=0, tiled=True)  47.5 us
    dot_general x17, local copies, waits for them, and re-layouts, contract(): lax.dot_general(left, right, ((left_dims, right_dims), ((), ())), preferr...  46.2 us
    dot_general x2, matrix products, product_nt(): lax.dot_general(left_side, right_side, (((1,), (1,)), ((), ())), preferre...  19.4 us
    convert_element_type x5, other arithmetic, rounded(): return values.astype(jnp.bfloat16)  18.2 us
  transfers between devices with their start and end apart: 3, of which 3 were waited for; matrix products, arithmetic and copies ran while one was open for 3% of the time, Pallas kernels for 0%

profile of v6, /device:TPU:0, one launch (start us, length us, event | category | flops | bytes accessed | tf_op | source)
XLA Modules:
  0.0 694.2 jit_solution(10191204657976706052)
XLA Ops:
  21.7 3.3 convert_reduce_fusion
  25.7 3.7 fusion.5
  29.4 134.2 %all-gather.2.cloned.1.call-done = bf16[89088,128]{1,0:T(8,128)(2,1)} async-done(((bf16[2784,128]{1,0:T(8,128)(2,1)}), bf16[89088,128]{1,0:T(8,128)(2,1)}) %all-gather.2.cloned.1.call-update) | async-done | bytes 22806544 | tf_op jit(solution)/shard_map/all_gather | solution.py:212
  164.5 2.6 fusion.155
  167.1 14.0 %fusion.154 = (bf16[32,256,128]{2,1,0:T(8,128)(2,1)}, bf16[32,256,128]{2,1,0:T(8,128)(2,1)}, bf16[32,256,128]{2,1,0:T(8,128)(2,1)}, bf16[32,256,128]{2,1,0:T(8,1...) fusion(bf16[32,2784,128]{2,1,0:T(8,128)(2,1)} %bitcast.706), kind=kLoop, calls=%fused_computation.330 | loop fusion | bytes 41943040 | tf_op jit(solution)/shard_map/slice | solution.py:215
  183.0 2.3 copy.245
  185.3 2.1 copy.249
  187.4 4.2 bitcast_convert_fusion.6
  191.5 2.3 copy.247
  193.8 2.6 copy.254
  196.4 4.3 copy.256
  201.3 6.2 select_reduce_fusion
  207.6 4.6 copy-done
  212.2 2.6 fusion.1
  214.8 10.5 %divide_convert_fusion = bf16[512,6272]{1,0:T(8,128)(2,1)} fusion(f32[512,6272]{1,0:T(8,128)} %copy-done, f32[512]{0:T(512)S(1)} %fusion.1, f32[512]{0:T(512)S(1)} %get-tuple-element.70, pred[6272]{0:T(1024)(128)(4,1)S(1)} %compare_reduce_fusion), kind=kLoop, calls=%fused_computation.2 | loop fusion | flops 12845056 | bytes 19277952 | tf_op jit(solution)/shard_map/convert_element_type | solution.py:19
  225.2 7.1 %subtract_convert_fusion.1 = (bf16[512,261]{0,1:T(8,128)(2,1)S(1)}, bf16[512,261]{0,1:T(8,128)(2,1)S(1)}, f32[512,261]{0,1:T(8,128)}) fusion(bf16[512,6272]{1,0:T(8,128)(2,1)} %divide_convert_fusion, f32[6272]{0:T(1024)S(1)} %add_rsqrt_fusion, f32[6272]{0:T(1024)S(1)} %broadcast_multiply_fusion, bf16[261,16384]{1,0:T(8,128)(2,1)} %param.21, s32[]{:T(128)S(6)} %min.4), kind=kOutput, calls=%fused_computation.204 | convolution fusion | flops 1683362304 | bytes 10853380 | tf_op jit(solution)/shard_map/dot_general | solution.py:37
  235.8 2.4 copy.252
  238.2 2.6 fusion.157
  243.5 3.0 fusion.53
  251.0 2.7 reshape.658
  253.7 3.9 copy.258
  257.6 3.9 copy.260
  261.5 3.9 copy.262
  265.5 3.9 copy.268
  269.4 3.2 copy.276
  272.6 3.9 copy.270
  276.5 4.3 fusion.59
  280.8 2.3 bitcast_convert_fusion.3
  283.1 2.3 bitcast_convert_fusion.4
  285.4 2.3 copy.402
  287.6 2.4 copy.403
  290.1 7.6 %fusion.159 = (f32[8,512]{1,0:T(8,128)S(1)}, f32[8,512,512]{1,2,0:T(8,128)}) fusion(bf16[512,8,128]{0,2,1:T(8,128)(2,1)} %bitcast.750, bf16[512,8,128]{0,2,1:T(8,128)(2,1)} %bitcast.752), kind=kOutput, calls=%fused_computation.335 | convolution fusion | flops 543162880 | bytes 10502144 | tf_op jit(solution)/shard_map/sub | solution.py:320
  297.7 4.7 divide_convert_fusion.1
  302.4 2.1 bitcast_convert_fusion.2
  309.6 2.7 fusion.51
  312.3 3.3 fusion.31
  315.6 2.7 reshape_reshape.22
  318.3 4.2 fusion.40
  325.6 2.3 bitcast_convert_fusion.1
  327.9 2.3 copy.279
  330.2 2.3 fusion.52
  332.5 4.8 convolution_convert_fusion.7
  338.7 2.5 multiply_convert_fusion.2
  359.1 2.9 copy.371
  363.6 2.6 convolution_convert_fusion
  366.3 2.8 convert_bitcast_fusion.1
  382.5 3.3 fusion.24
  385.8 2.0 reshape_reshape.23
  387.8 2.5 convert_bitcast_fusion.2
  394.9 2.6 convolution_convert_fusion.4
  399.8 2.0 convert_bitcast_fusion.3
  402.8 2.3 bitcast_convert_fusion
  408.4 12.2 %subtract_convert_fusion = (bf16[512,261]{0,1:T(8,128)(2,1)}, bf16[512,261]{0,1:T(8,128)(2,1)}) fusion(f32[6272]{0:T(1024)S(1)} %add_rsqrt_fusion, f32[6272]{0:T(1024)S(1)} %broadcast_multiply_fusion, bf16[261,16384]{1,0:T(8,128)(2,1)} %param.21, s32[]{:T(128)S(6)} %min.4, bf16[512,6272]{1,0:T(8,128)(2,1)} %divide_convert_fusion, ...), kind=kOutput, calls=%fused_computation.202 | convolution fusion | flops 3379035136 | bytes 13968384 | tf_op jit(solution)/shard_map/dot_general | solution.py:37
  420.7 3.9 convolution_convert_fusion.5
  425.4 2.9 reshape.666
  428.3 2.5 convert_bitcast_fusion
  436.3 2.6 convolution_convert_fusion.6
  444.7 2.7 convolution_convert_fusion.1
  459.8 2.0 constant_dynamic-update-slice_fusion.17
  476.1 143.0 %reduce-scatter.3.cloned.1.call-done = bf16[11136,128]{1,0:T(8,128)(2,1)} async-done(((bf16[89088,128]{1,0:T(8,128)(2,1)}), bf16[11136,128]{1,0:T(8,128)(2,1)}) %reduce-scatter.3.cloned.1.call-update) | async-done | bytes 2850832 | tf_op jit(solution)/shard_map/reduce_scatter | solution.py:238
  619.1 4.1 copy.272
  623.3 4.3 fusion.50
  627.6 2.2 add_add_fusion.4
  629.8 47.5 %reduce-scatter.5.cloned.1.call-done = bf16[2784,128]{1,0:T(8,128)(2,1)} async-done(((bf16[11136,128]{1,0:T(8,128)(2,1)}), bf16[2784,128]{1,0:T(8,128)(2,1)}) %reduce-scatter.5.cloned.1.call-update) | async-done | bytes 712720 | tf_op jit(solution)/shard_map/reduce_scatter | solution.py:241
  (380 shorter events, 128.3 us)
Async XLA Ops:
  7.2 9.7 %copy-start.93 = (f32[256,128]{1,0:T(8,128)S(1)}, f32[256,128]{1,0:T(8,128)}, u32[]{:S(2)}) copy-start(f32[256,128]{1,0:T(8,128)} %param.29) | copy-start | bytes 393220
  7.2 9.8 %copy-start.94 = (f32[256,128]{1,0:T(8,128)S(1)}, f32[256,128]{1,0:T(8,128)}, u32[]{:S(2)}) copy-start(f32[256,128]{1,0:T(8,128)} %param.33) | copy-start | bytes 393220
  7.2 9.9 %copy-start.95 = (f32[256,128]{1,0:T(8,128)S(1)}, f32[256,128]{1,0:T(8,128)}, u32[]{:S(2)}) copy-start(f32[256,128]{1,0:T(8,128)} %param.35) | copy-start | bytes 393220
  7.2 156.3 %all-gather.2.cloned.1.call-start = ((), (), s32[]{:S(2)}) async-start(), calls=%async_computation.2 | async-start | bytes 23519232 | tf_op jit(solution)/shard_map/all_gather | solution.py:212
  8.2 10.0 %copy-start.96 = (s32[1,16384]{1,0:T(1,128)S(1)}, s32[1,16384]{1,0:T(1,128)}, u32[]{:S(2)}) copy-start(s32[1,16384]{1,0:T(1,128)} %param.22) | copy-start | bytes 196612
  17.2 7.8 %copy-start.3 = (bf16[512,1024]{1,0:T(8,128)(2,1)S(1)}, bf16[512,1024]{1,0:T(8,128)(2,1)}, u32[]{:S(2)}) copy-start(bf16[512,1024]{1,0:T(8,128)(2,1)} %param.20) | copy-start | bytes 3145732
  18.1 601.0 %reduce-scatter.3.cloned.1.call-start = ((), (), s32[]{:S(2)}) async-start(), calls=%async_computation.3 | async-start | bytes 25657344 | tf_op jit(solution)/shard_map/reduce_scatter | solution.py:238
  25.2 156.4 %copy-start.100 = (f32[512]{0:T(512)}, f32[512]{0:T(512)S(1)}, u32[]{:S(2)}) copy-start(f32[512]{0:T(512)S(1)} %broadcast_multiply_fusion.4) | copy-start | bytes 6148
  25.6 141.5 %copy-start.105 = (f32[512]{0:T(512)}, f32[512]{0:T(512)S(1)}, u32[]{:S(2)}) copy-start(f32[512]{0:T(512)S(1)} %fusion.32) | copy-start | bytes 6148
  25.6 156.0 %copy-start.102 = (f32[512]{0:T(512)}, f32[512]{0:T(512)S(1)}, u32[]{:S(2)}) copy-start(f32[512]{0:T(512)S(1)} %fusion.140) | copy-start | bytes 6148
  181.1 12.7 %copy-start.7 = (bf16[32,256,128]{2,1,0:T(8,128)(2,1)}, bf16[32,256,128]{2,1,0:T(8,128)(2,1)S(1)}, u32[]{:S(2)}) copy-start(bf16[32,256,128]{2,1,0:T(8,128)(2,1)S(1)} %get-tuple-element.49) | copy-start | bytes 6291460
  181.6 3.6 copy-start.97
  196.4 4.3 copy-start.22
  196.4 4.3 copy-start.59
  207.6 4.6 copy-start
  225.2 8.1 %copy-start.37 = (bf16[32,32,3,128]{3,1,0,2:T(8,128)(2,1)S(1)}, bf16[32,32,3,128]{3,1,0,2:T(8,128)(2,1)}, u32[]{:S(2)}) copy-start(bf16[32,32,3,128]{3,1,0,2:T(8,128)(2,1)} %copy.249) | copy-start | bytes 2359300
  235.8 2.4 copy-start.26
  240.8 5.7 copy-start.12
  241.1 2.4 copy-start.66
  243.5 3.0 copy-start.65
  276.5 4.3 copy-start.73
  276.5 4.3 copy-start.76
  297.7 4.7 copy-start.46
  302.4 2.8 copy-start.1
  302.4 3.1 copy-start.68
  307.2 2.3 copy-start.67
  309.6 2.7 copy-start.24
  309.6 2.7 copy-start.48
  318.3 4.3 copy-start.10
  332.5 4.9 copy-start.2
  332.5 4.9 copy-start.47
  338.7 2.5 copy-start.44
  341.2 2.7 copy-start.28
  347.9 2.3 copy-start.6
  350.2 2.3 copy-start.5
  369.1 2.3 copy-start.70
  369.1 2.6 copy-start.83
  379.1 2.9 copy-start.25
  379.1 3.4 copy-start.112
  390.4 2.3 copy-start.13
  390.4 3.0 copy-start.63
  398.3 3.6 copy-start.14
  398.3 3.5 copy-start.107
  399.8 3.0 copy-start.62
  405.1 3.2 copy-start.89
  408.4 12.2 %copy-start.75 = (bf16[64,8,8,128]{3,2,1,0:T(8,128)(2,1)S(1)}, bf16[64,8,8,128]{3,2,1,0:T(8,128)(2,1)}, u32[]{:S(2)}) copy-start(bf16[64,8,8,128]{3,2,1,0:T(8,128)(2,1)} %copy-done.74) | copy-start | bytes 3145732
  420.7 3.9 copy-start.91
  420.7 3.9 copy-start.90
  424.5 3.7 copy-start.51
  436.2 2.6 copy-start.33
  436.3 2.6 copy-start.109
  436.3 2.6 copy-start.103
  438.9 5.8 copy-start.42
  444.7 2.7 copy-start.79
  444.7 2.7 copy-start.82
  476.0 201.3 %reduce-scatter.5.cloned.1.call-start = ((), (), s32[]{:S(2)}) async-start(), calls=%async_computation.4 | async-start | bytes 3563520 | tf_op jit(solution)/shard_map/reduce_scatter | solution.py:241
  619.1 4.1 copy-start.111
  619.1 4.1 copy-start.11
  623.2 4.4 copy-start.15
  623.2 4.4 copy-start.16
  623.2 4.4 copy-start.34
  623.2 4.4 copy-start.104
  623.3 4.4 copy-start.108
  623.3 4.4 copy-start.110
  (52 other events, 84.3 us)
Sparse Core Ops, SparseCore 0:
  18.2 145.3 all-gather.1
  476.1 142.9 reduce-scatter.2
  621.4 55.8 reduce-scatter.4

commit v7 on v6

--- a/solution.py
+++ b/solution.py
@@ -432,7 +432,7 @@
 
     item = (lax.axis_index("heads") * rows) // NLAT
     window, allowed = pixel_window(pixels, pixel_item[0], item)
-    pixel_norm = rounded(norm_pixels(widened(window)))
+    pixel_norm = lax.optimization_barrier(rounded(norm_pixels(widened(window))))
 
     start_rows = widened(latents)
     after_cross, saved_cross = cross_block(

time: 703 us -> 701 us (level)
    convert_element_type x5 -> x6, other arithmetic: 18.2 us -> 24.4 us  [rounded(): return values.astype(jnp.bfloat16)]
    unnamed x252 -> x254, local copies, waits for them, and re-layouts: 50.2 us -> 49.6 us
  transfers between devices with their start and end apart: 3 -> 3, of which waited for: 3 -> 3; matrix products, arithmetic and copies ran while one was open for 3% -> 4% of each run, Pallas kernels for 0% -> 0%
where the time goes in v7:
time: 701 us; the launch traced here: 691 us
  waiting for transfers between devices  319 us (46%)
  local copies, waits for them, and re-layouts  155 us (22%)
  matrix products  127 us (18%)
  other arithmetic  71.9 us (10%)
  between operations  18.1 us (3%)
    reduce_scatter x1, waiting for transfers between devices, reduce_grads(): lax.psum_scatter(packed.reshape(count * total, PANEL), 'items', scatter_d...  143 us
    all_gather x1, waiting for transfers between devices, gather_weights(): lax.all_gather(packed, ALL, axis=0, tiled=True).reshape(count, total, PANEL)  128 us
    dot_general x40, matrix products, contract(): lax.dot_general(left, right, ((left_dims, right_dims), ((), ())), preferr...  84.2 us
    unnamed x254, local copies, waits for them, and re-layouts  49.6 us
    reduce_scatter x1, waiting for transfers between devices, reduce_grads(): mine = lax.psum_scatter(mine, 'heads', scatter_dimension=0, tiled=True)  47.5 us
    dot_general x17, local copies, waits for them, and re-layouts, contract(): lax.dot_general(left, right, ((left_dims, right_dims), ((), ())), preferr...  46.3 us
    convert_element_type x6, other arithmetic, rounded(): return values.astype(jnp.bfloat16)  24.4 us
    dot_general x2, matrix products, product_nt(): lax.dot_general(left_side, right_side, (((1,), (1,)), ((), ())), preferre...  17.1 us
  transfers between devices with their start and end apart: 3, of which 3 were waited for; matrix products, arithmetic and copies ran while one was open for 4% of the time, Pallas kernels for 0%

profile of v7, /device:TPU:0, one launch (start us, length us, event | category | flops | bytes accessed | tf_op | source)
XLA Modules:
  0.0 691.3 jit_solution(10991057324838970015)
XLA Ops:
  21.5 3.3 convert_reduce_fusion
  24.8 3.7 fusion.5
  28.5 6.0 fusion.6
  35.4 128.1 %all-gather.2.cloned.1.call-done = bf16[89088,128]{1,0:T(8,128)(2,1)} async-done(((bf16[2784,128]{1,0:T(8,128)(2,1)}), bf16[89088,128]{1,0:T(8,128)(2,1)}) %all-gather.2.cloned.1.call-update) | async-done | bytes 22806544 | tf_op jit(solution)/shard_map/all_gather | solution.py:212
  164.5 2.6 fusion.146
  167.1 14.0 %fusion.145 = (bf16[32,256,128]{2,1,0:T(8,128)(2,1)}, bf16[32,256,128]{2,1,0:T(8,128)(2,1)}, bf16[32,256,128]{2,1,0:T(8,128)(2,1)}, bf16[32,256,128]{2,1,0:T(8,1...) fusion(bf16[32,2784,128]{2,1,0:T(8,128)(2,1)} %bitcast.710), kind=kLoop, calls=%fused_computation.326 | loop fusion | bytes 41943040 | tf_op jit(solution)/shard_map/slice | solution.py:215
  183.0 2.3 copy.245
  185.3 2.1 copy.249
  187.4 4.2 bitcast_convert_fusion.6
  191.5 2.3 copy.247
  193.8 2.6 copy.254
  196.4 4.2 copy.256
  201.3 6.0 select_reduce_fusion
  207.3 4.7 copy-done
  212.0 2.6 fusion.1
  214.6 10.6 %divide_convert_fusion = bf16[512,6272]{1,0:T(8,128)(2,1)} fusion(f32[512,6272]{1,0:T(8,128)} %copy-done, f32[512]{0:T(512)S(1)} %fusion.1, f32[512]{0:T(512)S(1)} %get-tuple-element.70, pred[6272]{0:T(1024)(128)(4,1)S(1)} %compare_reduce_fusion), kind=kLoop, calls=%fused_computation.2 | loop fusion | flops 12845056 | bytes 19277952 | tf_op jit(solution)/shard_map/convert_element_type | solution.py:19
  225.2 5.8 subtract_convert_fusion.1
  234.0 2.4 copy.252
  236.4 2.6 fusion.148
  241.7 3.0 fusion.53
  249.2 2.7 reshape.658
  251.9 3.9 copy.258
  255.9 3.9 copy.260
  259.8 3.9 copy.262
  263.7 3.9 copy.268
  267.6 3.2 copy.276
  270.8 3.9 copy.270
  274.8 4.3 fusion.59
  279.1 2.3 bitcast_convert_fusion.3
  281.3 2.3 bitcast_convert_fusion.4
  283.6 2.3 copy.402
  285.9 2.4 copy.403
  288.3 7.6 %fusion.150 = (f32[8,512]{1,0:T(8,128)S(1)}, f32[8,512,512]{1,2,0:T(8,128)}) fusion(bf16[512,8,128]{0,2,1:T(8,128)(2,1)} %bitcast.754, bf16[512,8,128]{0,2,1:T(8,128)(2,1)} %bitcast.756), kind=kOutput, calls=%fused_computation.331 | convolution fusion | flops 543162880 | bytes 10502144 | tf_op jit(solution)/shard_map/sub | solution.py:320
  295.9 4.7 divide_convert_fusion.1
  300.6 2.1 bitcast_convert_fusion.2
  307.8 2.6 fusion.51
  310.5 3.3 fusion.31
  313.7 2.8 reshape_reshape.22
  316.5 4.2 fusion.40
  323.9 2.2 bitcast_convert_fusion.1
  326.1 2.3 copy.279
  328.4 2.3 fusion.52
  330.8 4.8 convolution_convert_fusion.7
  336.8 2.4 multiply_convert_fusion.2
  357.2 2.8 copy.371
  361.7 2.6 convolution_convert_fusion
  364.3 2.8 convert_bitcast_fusion.1
  380.6 3.2 fusion.24
  383.8 2.0 reshape_reshape.23
  385.9 2.5 convert_bitcast_fusion.2
  393.0 2.6 convolution_convert_fusion.4
  397.8 2.0 convert_bitcast_fusion.3
  400.8 2.3 bitcast_convert_fusion
  406.2 11.4 %subtract_convert_fusion = (bf16[512,261]{0,1:T(8,128)(2,1)}, bf16[512,261]{0,1:T(8,128)(2,1)}) fusion(bf16[261,6272]{1,0:T(8,128)(2,1)} %fusion.6, bf16[512,6272]{1,0:T(8,128)(2,1)} %divide_convert_fusion, f32[512]{0:T(512)S(1)} %multiply_reduce_fusion.8, bf16[512,384]{0,1:T(8,128)(2,1)} %copy-done.93), kind=kOutput, calls=%fused_computation.200 | convolution fusion | flops 3365939200 | bytes 13852672 | tf_op jit(solution)/shard_map/dot_general | solution.py:37
  417.6 3.9 convolution_convert_fusion.5
  422.3 2.9 reshape.666
  425.2 2.5 convert_bitcast_fusion
  433.3 2.6 convolution_convert_fusion.6
  441.6 2.7 convolution_convert_fusion.1
  473.2 143.0 %reduce-scatter.3.cloned.1.call-done = bf16[11136,128]{1,0:T(8,128)(2,1)} async-done(((bf16[89088,128]{1,0:T(8,128)(2,1)}), bf16[11136,128]{1,0:T(8,128)(2,1)}) %reduce-scatter.3.cloned.1.call-update) | async-done | bytes 2850832 | tf_op jit(solution)/shard_map/reduce_scatter | solution.py:238
  616.3 4.1 copy.272
  620.4 4.3 fusion.50
  624.8 2.2 add_add_fusion.4
  627.0 47.5 %reduce-scatter.5.cloned.1.call-done = bf16[2784,128]{1,0:T(8,128)(2,1)} async-done(((bf16[11136,128]{1,0:T(8,128)(2,1)}), bf16[2784,128]{1,0:T(8,128)(2,1)}) %reduce-scatter.5.cloned.1.call-update) | async-done | bytes 712720 | tf_op jit(solution)/shard_map/reduce_scatter | solution.py:241
  (383 shorter events, 129.9 us)
Async XLA Ops:
  7.2 9.7 %copy-start.94 = (f32[256,128]{1,0:T(8,128)S(1)}, f32[256,128]{1,0:T(8,128)}, u32[]{:S(2)}) copy-start(f32[256,128]{1,0:T(8,128)} %param.29) | copy-start | bytes 393220
  7.2 9.8 %copy-start.95 = (f32[256,128]{1,0:T(8,128)S(1)}, f32[256,128]{1,0:T(8,128)}, u32[]{:S(2)}) copy-start(f32[256,128]{1,0:T(8,128)} %param.33) | copy-start | bytes 393220
  7.2 9.9 %copy-start.96 = (f32[256,128]{1,0:T(8,128)S(1)}, f32[256,128]{1,0:T(8,128)}, u32[]{:S(2)}) copy-start(f32[256,128]{1,0:T(8,128)} %param.35) | copy-start | bytes 393220
  7.2 156.3 %all-gather.2.cloned.1.call-start = ((), (), s32[]{:S(2)}) async-start(), calls=%async_computation.2 | async-start | bytes 23519232 | tf_op jit(solution)/shard_map/all_gather | solution.py:212
  8.2 10.0 %copy-start.97 = (s32[1,16384]{1,0:T(1,128)S(1)}, s32[1,16384]{1,0:T(1,128)}, u32[]{:S(2)}) copy-start(s32[1,16384]{1,0:T(1,128)} %param.22) | copy-start | bytes 196612
  18.1 598.2 %reduce-scatter.3.cloned.1.call-start = ((), (), s32[]{:S(2)}) async-start(), calls=%async_computation.3 | async-start | bytes 25657344 | tf_op jit(solution)/shard_map/reduce_scatter | solution.py:238
  28.5 6.2 copy-start.3
  35.0 146.6 %copy-start.101 = (f32[512]{0:T(512)}, f32[512]{0:T(512)S(1)}, u32[]{:S(2)}) copy-start(f32[512]{0:T(512)S(1)} %broadcast_multiply_fusion.4) | copy-start | bytes 6148
  35.4 131.7 %copy-start.106 = (f32[512]{0:T(512)}, f32[512]{0:T(512)S(1)}, u32[]{:S(2)}) copy-start(f32[512]{0:T(512)S(1)} %fusion.32) | copy-start | bytes 6148
  35.4 146.2 %copy-start.103 = (f32[512]{0:T(512)}, f32[512]{0:T(512)S(1)}, u32[]{:S(2)}) copy-start(f32[512]{0:T(512)S(1)} %fusion.135) | copy-start | bytes 6148
  181.1 12.7 %copy-start.7 = (bf16[32,256,128]{2,1,0:T(8,128)(2,1)}, bf16[32,256,128]{2,1,0:T(8,128)(2,1)S(1)}, u32[]{:S(2)}) copy-start(bf16[32,256,128]{2,1,0:T(8,128)(2,1)S(1)} %get-tuple-element.49) | copy-start | bytes 6291460
  181.6 3.7 copy-start.98
  196.4 4.3 copy-start.23
  196.4 4.3 copy-start.60
  207.3 4.7 copy-start
  214.6 10.6 %copy-start.20 = (bf16[261,6272]{1,0:T(8,128)(2,1)S(1)}, bf16[261,6272]{1,0:T(8,128)(2,1)}, u32[]{:S(2)}) copy-start(bf16[261,6272]{1,0:T(8,128)(2,1)} %fusion.6) | copy-start | bytes 9821956
  225.2 5.9 copy-start.38
  234.0 2.4 copy-start.27
  239.0 5.7 copy-start.12
  239.4 2.4 copy-start.67
  241.7 3.0 copy-start.66
  274.7 4.3 copy-start.74
  274.7 4.3 copy-start.75
  295.9 4.7 copy-start.47
  300.6 2.8 copy-start.1
  300.6 3.1 copy-start.69
  305.5 2.4 copy-start.68
  307.8 2.7 copy-start.25
  307.8 2.7 copy-start.49
  316.5 4.3 copy-start.10
  330.7 4.8 copy-start.2
  330.7 4.8 copy-start.48
  336.8 2.4 copy-start.45
  339.2 2.7 copy-start.29
  346.0 2.3 copy-start.6
  367.1 2.3 copy-start.71
  367.2 2.6 copy-start.84
  377.2 2.8 copy-start.26
  377.2 3.4 copy-start.113
  388.4 2.3 copy-start.13
  388.4 3.0 copy-start.64
  396.3 3.5 copy-start.14
  396.3 3.5 copy-start.108
  397.8 3.0 copy-start.63
  403.1 3.0 copy-start.90
  406.2 11.4 %copy-start.77 = (bf16[64,8,8,128]{3,2,1,0:T(8,128)(2,1)S(1)}, bf16[64,8,8,128]{3,2,1,0:T(8,128)(2,1)}, u32[]{:S(2)}) copy-start(bf16[64,8,8,128]{3,2,1,0:T(8,128)(2,1)} %copy-done.76) | copy-start | bytes 3145732
  417.6 3.9 copy-start.92
  417.6 3.9 copy-start.91
  421.5 3.7 copy-start.52
  433.2 2.6 copy-start.34
  433.2 2.6 copy-start.110
  433.2 2.6 copy-start.104
  435.8 5.8 copy-start.43
  441.6 2.7 copy-start.80
  441.6 2.7 copy-start.83
  473.2 201.3 %reduce-scatter.5.cloned.1.call-start = ((), (), s32[]{:S(2)}) async-start(), calls=%async_computation.4 | async-start | bytes 3563520 | tf_op jit(solution)/shard_map/reduce_scatter | solution.py:241
  616.3 4.1 copy-start.112
  616.3 4.1 copy-start.11
  620.4 4.4 copy-start.15
  620.4 4.4 copy-start.16
  620.4 4.4 copy-start.35
  620.4 4.4 copy-start.105
  620.4 4.4 copy-start.109
  620.4 4.4 copy-start.111
  (53 other events, 86.5 us)
Sparse Core Ops, SparseCore 0:
  18.2 145.3 all-gather.1
  473.3 142.8 reduce-scatter.2
  618.6 55.8 reduce-scatter.4

commit v8 on v7

--- a/solution.py
+++ b/solution.py
@@ -196,26 +196,34 @@
 
 def gather_weights(weights, gains, items, heads):
     count = items * heads
-    pieces, places, row = [], [], 0
-    for w, kind in zip(weights, WEIGHT_KINDS):
-        block = local_panels(rounded(w.T if kind == "cols" else w))
-        rows = padded_rows(block.shape[0])
-        pieces.append(pad_rows(block, rows))
-        places.append((row, rows))
-        row += rows
+    blocks = [local_panels(rounded(w.T if kind == "cols" else w)) for w, kind in zip(weights, WEIGHT_KINDS)]
+    large = [k for k, kind in enumerate(WEIGHT_KINDS) if kind != "cols"]
+    small = [k for k, kind in enumerate(WEIGHT_KINDS) if kind == "cols"]
+    slot = padded_rows(max(blocks[k].shape[0] for k in large))
     gain_row = rounded(jnp.concatenate(gains)).reshape(1, -1)
-    gain_block = local_panels(gain_row)
-    total = -(-(row + gain_block.shape[0]) // ROW_GROUP) * ROW_GROUP
-    pieces.append(pad_rows(gain_block, total - row))
-    places.append((row, gain_block.shape[0]))
-    packed = jnp.concatenate(pieces, axis=0)
-    gathered = lax.all_gather(packed, ALL, axis=0, tiled=True).reshape(count, total, PANEL)
-    out = []
-    for w, kind, (first, rows) in zip(weights, WEIGHT_KINDS, places):
-        piece = gathered[:, first : first + rows, :]
-        out.append(make_weight(piece, kind, local_shape(w, kind), items, heads))
-    first, rows = places[-1]
-    gain_all = gathered[:, first : first + rows, :].reshape(count, -1)[:, : gain_row.shape[1]]
+    tail, places, row = [], {}, 0
+    for k in small:
+        places[k] = (row, blocks[k].shape[0])
+        tail.append(blocks[k])
+        row += blocks[k].shape[0]
+    gain_place = (row, 1)
+    tail.append(local_panels(gain_row))
+    row += tail[-1].shape[0]
+    tail_slots = -(-row // slot)
+    tail_block = pad_rows(jnp.concatenate(tail, axis=0), tail_slots * slot)
+    packed = jnp.stack([pad_rows(blocks[k], slot) for k in large] + list(tail_block.reshape(tail_slots, slot, PANEL)))
+    gathered = lax.all_gather(packed, ALL, axis=1, tiled=False)
+    out = [None] * len(weights)
+    for position, k in enumerate(large):
+        shape = local_shape(weights[k], WEIGHT_KINDS[k])
+        out[k] = make_weight(gathered[position], WEIGHT_KINDS[k], shape, items, heads)
+    rest = gathered[len(large) :].transpose(1, 0, 2, 3).reshape(count, tail_slots * slot, PANEL)
+    for k in small:
+        first, rows = places[k]
+        shape = local_shape(weights[k], WEIGHT_KINDS[k])
+        out[k] = make_weight(rest[:, first : first + rows, :], WEIGHT_KINDS[k], shape, items, heads)
+    first, rows = gain_place
+    gain_all = rest[:, first : first + rows, :].reshape(count, -1)[:, : gain_row.shape[1]]
     gain_all = gain_all.reshape(count, len(gains), -1)
     whole_gains = [widened(gain_all[:, k, :].reshape(-1)) for k in range(len(gains))]
     return out, whole_gains

time: 701 us -> 722 us (1.030)
  local copies, waits for them, and re-layouts: 155 us -> 174 us
    another operation x0 -> x17, local copies, waits for them, and re-layouts: none -> 56.1 us  [the longest x10 33.9 us: make_weight(): blocks = blocks.reshape(items, heads, panels, rows, PANEL)]
    dot_general x17 -> x4, local copies, waits for them, and re-layouts: 46.3 us -> 8.2 us  [contract(): lax.dot_general(left, right, ((left_dims, right_dims), ((), ())), preferr...]
    unnamed x254 -> x274, local copies, waits for them, and re-layouts: 49.6 us -> 47.7 us
where the time goes in v8:
time: 722 us; the launch traced here: 714 us
  waiting for transfers between devices  320 us (44%)
  local copies, waits for them, and re-layouts  174 us (24%)
  matrix products  129 us (18%)
  other arithmetic  72.4 us (10%)
  between operations  18 us (2%)
    reduce_scatter x1, waiting for transfers between devices, reduce_grads(): lax.psum_scatter(packed.reshape(count * total, PANEL), 'items', scatter_d...  144 us
    all_gather x1, waiting for transfers between devices, gather_weights(): gathered = lax.all_gather(packed, ALL, axis=1, tiled=False)  129 us
    dot_general x40, matrix products, contract(): lax.dot_general(left, right, ((left_dims, right_dims), ((), ())), preferr...  85.3 us
    unnamed x274, local copies, waits for them, and re-layouts  47.7 us
    reduce_scatter x1, waiting for transfers between devices, reduce_grads(): mine = lax.psum_scatter(mine, 'heads', scatter_dimension=0, tiled=True)  47.5 us
    another operation x10, local copies, waits for them, and re-layouts, make_weight(): blocks = blocks.reshape(items, heads, panels, rows, PANEL)  33.9 us
    convert_element_type x6, other arithmetic, rounded(): return values.astype(jnp.bfloat16)  24.4 us
    dot_general x2, matrix products, product_nt(): lax.dot_general(left_side, right_side, (((1,), (1,)), ((), ())), preferre...  17.1 us
  transfers between devices with their start and end apart: 3, of which 3 were waited for; matrix products, arithmetic and copies ran while one was open for 4% of the time, Pallas kernels for 0%

profile of v8, /device:TPU:0, one launch (start us, length us, event | category | flops | bytes accessed | tf_op | source)
XLA Modules:
  0.0 714.0 jit_solution(3565048296305707237)
XLA Ops:
  21.5 3.3 convert_reduce_fusion
  24.8 3.7 fusion.5
  28.5 6.1 fusion.6
  35.4 128.7 %all-gather.3.cloned.1.call-done = bf16[11,8192,128]{2,1,0:T(8,128)(2,1)} async-done(((bf16[11,256,128]{2,1,0:T(8,128)(2,1)}), bf16[11,8192,128]{2,1,0:T(8,128)(2,1)}) %all-gather.3.cloned.1.call-update) | async-done | bytes 23068688 | tf_op jit(solution)/shard_map/all_gather | solution.py:215
  164.1 15.2 %fusion.141 = (bf16[1,8192,128]{2,1,0:T(8,128)(2,1)}, bf16[1,8192,128]{2,1,0:T(8,128)(2,1)}, bf16[1,8192,128]{2,1,0:T(8,128)(2,1)S(1)}, bf16[1,8192,128]{2,1,0:T...) fusion(bf16[11,8192,128]{2,1,0:T(8,128)(2,1)} %all-gather.3.clo, ...), kind=kLoop, calls=%fused_computation.325 | loop fusion | bytes 46137344 | tf_op jit(solution)/shard_map/slice | solution.py:219
  182.9 3.9 copy.269
  186.8 3.2 copy.283
  190.0 3.9 copy.277
  193.9 3.1 copy.292
  197.0 3.9 copy.267
  201.0 3.2 copy.299
  204.2 3.9 copy.265
  208.1 3.1 copy.302
  211.2 3.9 copy.261
  215.2 3.5 copy.304
  218.7 2.3 copy.579
  222.7 2.3 copy.580
  229.5 2.3 copy.252
  231.8 2.3 dot_general.261
  234.1 2.8 dot_general.249
  236.9 3.5 bitcast_convert_fusion.6
  241.9 4.5 copy.263
  247.0 6.0 select_reduce_fusion
  253.1 4.6 copy-done
  257.7 2.6 fusion.1
  260.3 10.6 %divide_convert_fusion = bf16[512,6272]{1,0:T(8,128)(2,1)} fusion(f32[512,6272]{1,0:T(8,128)} %copy-done, f32[512]{0:T(512)S(1)} %fusion.1, f32[512]{0:T(512)S(1)} %get-tuple-element.71, pred[6272]{0:T(1024)(128)(4,1)S(1)} %compare_reduce_fusion), kind=kLoop, calls=%fused_computation.2 | loop fusion | flops 12845056 | bytes 19277952 | tf_op jit(solution)/shard_map/convert_element_type | solution.py:19
  270.8 5.8 subtract_convert_fusion.1
  279.5 2.4 copy.259
  281.9 2.6 fusion.144
  287.2 3.0 fusion.47
  295.3 2.7 reshape.622
  299.3 3.9 copy.275
  303.2 4.3 fusion.49
  312.1 2.3 copy.409
  314.4 2.7 copy.410
  317.0 8.2 %fusion.146 = (f32[8,512]{1,0:T(8,128)}, f32[8,512,512]{1,2,0:T(8,128)}) fusion(bf16[512,8,128]{0,2,1:T(8,128)(2,1)} %bitcast.767, bf16[512,8,128]{0,2,1:T(8,128)(2,1)} %bitcast.769), kind=kOutput, calls=%fused_computation.330 | convolution fusion | flops 543162880 | bytes 10502144 | tf_op jit(solution)/shard_map/sub | solution.py:328
  325.3 4.7 divide_convert_fusion.1
  337.2 2.7 fusion.45
  339.9 3.3 fusion.31
  343.2 2.7 reshape_reshape.7
  346.0 4.8 fusion.34
  353.9 2.3 bitcast_convert_fusion.1
  356.2 2.3 copy.286
  358.5 2.3 fusion.46
  360.8 4.8 convolution_convert_fusion.7
  366.9 2.5 multiply_convert_fusion.2
  375.2 2.6 copy.378
  379.4 2.6 convolution_convert_fusion
  383.4 2.8 convert_bitcast_fusion.1
  392.5 2.4 multiply_reduce_fusion.1
  400.1 3.3 fusion.24
  403.4 2.3 reshape_reshape.8
  405.8 2.5 convert_bitcast_fusion.2
  413.4 2.6 convolution_convert_fusion.4
  427.9 11.3 %subtract_convert_fusion = (bf16[512,261]{0,1:T(8,128)(2,1)}, bf16[512,261]{0,1:T(8,128)(2,1)}) fusion(bf16[261,6272]{1,0:T(8,128)(2,1)} %fusion.6, bf16[512,6272]{1,0:T(8,128)(2,1)} %divide_convert_fusion, f32[512]{0:T(512)S(1)} %multiply_reduce_fusion.8, bf16[512,384]{0,1:T(8,128)(2,1)} %copy-done.89), kind=kOutput, calls=%fused_computation.196 | convolution fusion | flops 3365939200 | bytes 13852672 | tf_op jit(solution)/shard_map/dot_general | solution.py:37
  439.2 3.9 convolution_convert_fusion.5
  444.8 2.8 reshape.630
  447.6 2.5 convert_bitcast_fusion
  455.7 2.6 convolution_convert_fusion.6
  464.1 2.7 convolution_convert_fusion.1
  495.5 143.7 %reduce-scatter.3.cloned.1.call-done = bf16[11136,128]{1,0:T(8,128)(2,1)} async-done(((bf16[89088,128]{1,0:T(8,128)(2,1)}), bf16[11136,128]{1,0:T(8,128)(2,1)}) %reduce-scatter.3.cloned.1.call-update) | async-done | bytes 2850832 | tf_op jit(solution)/shard_map/reduce_scatter | solution.py:246
  639.3 4.1 copy.279
  643.4 4.3 fusion.44
  649.9 47.5 %reduce-scatter.5.cloned.1.call-done = bf16[2784,128]{1,0:T(8,128)(2,1)} async-done(((bf16[11136,128]{1,0:T(8,128)(2,1)}), bf16[2784,128]{1,0:T(8,128)(2,1)}) %reduce-scatter.5.cloned.1.call-update) | async-done | bytes 712720 | tf_op jit(solution)/shard_map/reduce_scatter | solution.py:249
  (407 shorter events, 142.8 us)
Async XLA Ops:
  7.2 9.7 %copy-start.90 = (f32[256,128]{1,0:T(8,128)S(1)}, f32[256,128]{1,0:T(8,128)}, u32[]{:S(2)}) copy-start(f32[256,128]{1,0:T(8,128)} %param.29) | copy-start | bytes 393220
  7.2 9.8 %copy-start.91 = (f32[256,128]{1,0:T(8,128)S(1)}, f32[256,128]{1,0:T(8,128)}, u32[]{:S(2)}) copy-start(f32[256,128]{1,0:T(8,128)} %param.33) | copy-start | bytes 393220
  7.2 9.8 %copy-start.92 = (f32[256,128]{1,0:T(8,128)S(1)}, f32[256,128]{1,0:T(8,128)}, u32[]{:S(2)}) copy-start(f32[256,128]{1,0:T(8,128)} %param.35) | copy-start | bytes 393220
  7.2 156.9 %all-gather.3.cloned.1.call-start = ((), (), s32[]{:S(2)}) async-start(), calls=%async_computation.4 | async-start | bytes 23789568 | tf_op jit(solution)/shard_map/all_gather | solution.py:215
  8.2 9.9 %copy-start.93 = (s32[1,16384]{1,0:T(1,128)S(1)}, s32[1,16384]{1,0:T(1,128)}, u32[]{:S(2)}) copy-start(s32[1,16384]{1,0:T(1,128)} %param.22) | copy-start | bytes 196612
  18.1 621.2 %reduce-scatter.3.cloned.1.call-start = ((), (), s32[]{:S(2)}) async-start(), calls=%async_computation.2 | async-start | bytes 25657344 | tf_op jit(solution)/shard_map/reduce_scatter | solution.py:246
  28.5 6.2 copy-start.3
  35.0 193.2 %copy-start.95 = (f32[512]{0:T(512)}, f32[512]{0:T(512)S(1)}, u32[]{:S(2)}) copy-start(f32[512]{0:T(512)S(1)} %broadcast_multiply_fusion.4) | copy-start | bytes 6148
  35.4 144.0 %copy-start.111 = (f32[512]{0:T(512)}, f32[512]{0:T(512)S(1)}, u32[]{:S(2)}) copy-start(f32[512]{0:T(512)S(1)} %fusion.32) | copy-start | bytes 6148
  35.4 192.8 %copy-start.105 = (f32[512]{0:T(512)}, f32[512]{0:T(512)S(1)}, u32[]{:S(2)}) copy-start(f32[512]{0:T(512)S(1)} %fusion.131) | copy-start | bytes 6148
  215.2 3.5 copy-start.6
  226.0 60.4 %copy-start.97 = (f32[1024]{0:T(1024)}, f32[1024]{0:T(1024)S(1)}, u32[]{:S(2)}) copy-start(f32[1024]{0:T(1024)S(1)} %reshape.647) | copy-start | bytes 12292
  228.2 3.6 copy-start.29
  241.9 4.5 copy-start.20
  241.9 4.5 copy-start.58
  253.0 4.6 copy-start
  260.3 10.6 %copy-start.17 = (bf16[261,6272]{1,0:T(8,128)(2,1)S(1)}, bf16[261,6272]{1,0:T(8,128)(2,1)}, u32[]{:S(2)}) copy-start(bf16[261,6272]{1,0:T(8,128)(2,1)} %fusion.6) | copy-start | bytes 9821956
  270.8 5.9 copy-start.34
  284.5 5.7 copy-start.4
  284.9 5.3 copy-start.107
  287.2 3.0 copy-start.70
  303.2 4.3 copy-start.66
  303.2 4.3 copy-start.74
  325.3 4.7 copy-start.45
  330.0 2.8 copy-start.1
  330.0 3.1 copy-start.72
  335.2 4.7 copy-start.109
  337.2 2.7 copy-start.22
  337.2 2.7 copy-start.47
  345.9 4.9 copy-start.118
  345.9 4.9 copy-start.9
  345.9 4.9 copy-start.100
  345.9 4.9 copy-start.104
  346.0 4.9 copy-start.110
  360.8 4.8 copy-start.2
  360.8 4.8 copy-start.46
  371.2 2.8 copy-start.37
  386.2 2.6 copy-start.80
  396.8 2.9 copy-start.23
  396.8 3.3 copy-start.124
  405.7 4.0 copy-start.98
  405.8 4.0 copy-start.102
  405.8 4.0 copy-start.108
  408.3 3.0 copy-start.62
  413.4 2.7 copy-start.114
  416.8 4.8 copy-start.11
  419.5 3.0 copy-start.61
  427.9 11.3 %copy-start.41 = (bf16[512,1024]{0,1:T(8,128)(2,1)S(1)}, bf16[512,1024]{0,1:T(8,128)(2,1)}, u32[]{:S(2)}) copy-start(bf16[512,1024]{0,1:T(8,128)(2,1)} %copy.259) | copy-start | bytes 3145732
  439.2 3.9 copy-start.88
  439.2 4.8 copy-start.87
  443.2 4.4 copy-start.50
  455.6 2.6 copy-start.31
  455.6 2.6 copy-start.121
  455.6 2.6 copy-start.106
  458.2 5.8 copy-start.39
  464.1 2.7 copy-start.75
  464.1 2.7 copy-start.79
  495.5 201.9 %reduce-scatter.5.cloned.1.call-start = ((), (), s32[]{:S(2)}) async-start(), calls=%async_computation.3 | async-start | bytes 3563520 | tf_op jit(solution)/shard_map/reduce_scatter | solution.py:249
  639.2 4.1 copy-start.123
  639.3 4.1 copy-start.10
  643.4 4.4 copy-start.12
  643.4 4.4 copy-start.13
  643.4 4.3 copy-start.32
  643.4 4.3 copy-start.122
  (64 other events, 107.1 us)
Sparse Core Ops, SparseCore 0:
  18.2 145.9 all-gather.2
  495.6 143.6 reduce-scatter.2
  641.6 55.7 reduce-scatter.4

commit v9 on v6

--- a/solution.py
+++ b/solution.py
@@ -3,6 +3,8 @@
 import jax
 import jax.numpy as jnp
 from jax import lax
+from jax.experimental import pallas as pl
+from jax.experimental.pallas import tpu as pltpu
 from jax.sharding import PartitionSpec as P
 
 HEAD = 128
@@ -370,17 +372,62 @@
     return window, ids == item
 
 
+SOFTMAX_ROWS = 128
+
+
+def softmax_mix_kernel(keyed_ref, pixel_ref, mask_ref, weights_ref, mix_ref):
+    scores = jnp.dot(keyed_ref[...], pixel_ref[...], preferred_element_type=jnp.float32)
+    scores = jnp.where(mask_ref[...] > 0.0, scores, MASKED)
+    row_top = jnp.max(scores, axis=-1, keepdims=True)
+    raw = jnp.exp(scores - row_top)
+    row_total = jnp.sum(raw, axis=-1, keepdims=True)
+    weights = (raw / row_total).astype(jnp.bfloat16)
+    weights_ref[...] = weights
+    mix_ref[...] = lax.dot_general(
+        weights, pixel_ref[...], (((1,), (1,)), ((), ())), preferred_element_type=jnp.float32
+    )
+
+
+def softmax_mix(keyed, pixel_pad, mask):
+    rows, channels = keyed.shape
+    width = pixel_pad.shape[1]
+    block = min(SOFTMAX_ROWS, rows)
+    cost = pl.CostEstimate(
+        flops=4 * rows * channels * width,
+        transcendentals=rows * width,
+        bytes_accessed=2 * (rows * channels + channels * width + rows * width) + 4 * rows * channels,
+    )
+    return pl.pallas_call(
+        softmax_mix_kernel,
+        grid=(rows // block,),
+        in_specs=[
+            pl.BlockSpec((block, channels), lambda i: (i, 0)),
+            pl.BlockSpec((channels, width), lambda i: (0, 0)),
+            pl.BlockSpec((1, width), lambda i: (0, 0)),
+        ],
+        out_specs=[
+            pl.BlockSpec((block, width), lambda i: (i, 0)),
+            pl.BlockSpec((block, channels), lambda i: (i, 0)),
+        ],
+        out_shape=[
+            jax.ShapeDtypeStruct((rows, width), jnp.bfloat16),
+            jax.ShapeDtypeStruct((rows, channels), jnp.float32),
+        ],
+        compiler_params=pltpu.CompilerParams(vmem_limit_bytes=48 * 1024 * 1024),
+        cost_estimate=cost,
+    )(keyed, pixel_pad, mask)
+
+
 def cross_block(residual, gain_vec, query_w, key_w, value_w, out_w, pixel_norm, allowed):
     scale = 1.0 / math.sqrt(residual.shape[1])
     normed = rounded(norm_rows(residual, gain_vec))
     query_rows = rounded(apply(normed, query_w))
     query_keyed = rounded(apply(query_rows, key_w) * scale)
-    scores = jnp.where(allowed[None, :], product(query_keyed, pixel_norm), MASKED)
-    row_top = jnp.max(scores, axis=-1, keepdims=True)
-    raw_weights = jnp.exp(scores - row_top)
-    row_total = jnp.sum(raw_weights, axis=-1, keepdims=True)
-    weights_low = rounded(raw_weights / row_total)
-    pixel_mix = product_nt(weights_low, pixel_norm)
+    pixel_pad, mask = allowed
+    channels = pixel_norm.shape[0]
+    keyed_pad = jnp.pad(query_keyed, ((0, 0), (0, pixel_pad.shape[0] - channels)))
+    weights_low, pixel_mix = softmax_mix(keyed_pad, pixel_pad, mask)
+    pixel_mix = pixel_mix[:, :channels]
     mixed = rounded(split_apply_t(pixel_mix, value_w))
     saved = (normed, query_rows, weights_low, pixel_mix, mixed)
     return residual + apply(mixed, out_w), saved
@@ -433,6 +480,11 @@
     item = (lax.axis_index("heads") * rows) // NLAT
     window, allowed = pixel_window(pixels, pixel_item[0], item)
     pixel_norm = rounded(norm_pixels(widened(window)))
+    channels = pixel_norm.shape[0]
+    pixel_pad = jnp.pad(pixel_norm, ((0, -channels % LANE), (0, 0)))
+    mask = allowed.astype(jnp.float32)[None, :]
+    pixel_norm, pixel_pad, mask = lax.optimization_barrier((pixel_norm, pixel_pad, mask))
+    allowed = (pixel_pad, mask)
 
     start_rows = widened(latents)
     after_cross, saved_cross = cross_block(

time: 703 us -> 685 us (0.974)
  matrix products: 130 us -> 112 us
  Pallas kernels: 0 us -> 12.8 us
  other arithmetic: 65.8 us -> 56.2 us
  waiting for transfers between devices: 325 us -> 317 us
    pallas_call x0 -> x1, Pallas kernels: none -> 12.8 us  [softmax_mix(): pl.pallas_call(softmax_mix_kernel, grid=(rows // block,), in_specs=[pl.Bl...]
    dot_general x2 -> x1, matrix products: 19.4 us -> 9.12 us  [product_nt(): lax.dot_general(left_side, right_side, (((1,), (1,)), ((), ())), preferre...]
    all_gather x1, waiting for transfers between devices: 134 us -> 127 us  [gather_weights(): lax.all_gather(packed, ALL, axis=0, tiled=True).reshape(count, total, PANEL)]
    convert_element_type x5 -> x7, other arithmetic: 18.2 us -> 11.1 us  [rounded(): return values.astype(jnp.bfloat16)]
    unnamed x252 -> x256, local copies, waits for them, and re-layouts: 50.2 us -> 51.6 us
  transfers between devices with their start and end apart: 3 -> 3, of which waited for: 3 -> 3; matrix products, arithmetic and copies ran while one was open for 3% -> 4% of each run, Pallas kernels for 0% -> 0%
where the time goes in v9:
time: 685 us; the launch traced here: 676 us
  waiting for transfers between devices  317 us (46%)
  local copies, waits for them, and re-layouts  160 us (23%)
  matrix products  112 us (16%)
  other arithmetic  56.2 us (8%)
  between operations  18.2 us (3%)
  Pallas kernels  12.8 us (2%)
    reduce_scatter x1, waiting for transfers between devices, reduce_grads(): lax.psum_scatter(packed.reshape(count * total, PANEL), 'items', scatter_d...  143 us
    all_gather x1, waiting for transfers between devices, gather_weights(): lax.all_gather(packed, ALL, axis=0, tiled=True).reshape(count, total, PANEL)  127 us
    dot_general x40, matrix products, contract(): lax.dot_general(left, right, ((left_dims, right_dims), ((), ())), preferr...  83 us
    unnamed x256, local copies, waits for them, and re-layouts  51.6 us
    reduce_scatter x1, waiting for transfers between devices, reduce_grads(): mine = lax.psum_scatter(mine, 'heads', scatter_dimension=0, tiled=True)  47.4 us
    dot_general x17, local copies, waits for them, and re-layouts, contract(): lax.dot_general(left, right, ((left_dims, right_dims), ((), ())), preferr...  46.2 us
    slice x2, local copies, waits for them, and re-layouts, gather_weights(): piece = gathered[:, first:first + rows, :]  17.3 us
  transfers between devices with their start and end apart: 3, of which 3 were waited for; matrix products, arithmetic and copies ran while one was open for 4% of the time, Pallas kernels for 0%

profile of v9, /device:TPU:0, one launch (start us, length us, event | category | flops | bytes accessed | tf_op | source)
XLA Modules:
  0.0 676.4 jit_solution(13624118775498309698)
XLA Ops:
  21.5 3.3 convert_reduce_fusion
  24.8 3.7 fusion.4
  28.5 4.2 fusion.5
  32.8 2.6 pad.43.pixel_ref
  36.9 126.6 %all-gather.2.cloned.1.call-done = bf16[89088,128]{1,0:T(8,128)(2,1)} async-done(((bf16[2784,128]{1,0:T(8,128)(2,1)}), bf16[89088,128]{1,0:T(8,128)(2,1)}) %all-gather.2.cloned.1.call-update) | async-done | bytes 22806544 | tf_op jit(solution)/shard_map/all_gather | solution.py:214
  164.5 2.4 fusion.141
  166.8 15.0 %fusion.140 = (bf16[32,256,128]{2,1,0:T(8,128)(2,1)}, bf16[32,256,128]{2,1,0:T(8,128)(2,1)}, bf16[32,256,128]{2,1,0:T(8,128)(2,1)}, bf16[32,256,128]{2,1,0:T(8,1...) fusion(bf16[32,2784,128]{2,1,0:T(8,128)(2,1)} %bitcast.707), kind=kLoop, calls=%fused_computation.320 | loop fusion | bytes 41943040 | tf_op jit(solution)/shard_map/slice | solution.py:217
  185.0 4.2 bitcast_convert_fusion.6
  191.8 3.9 copy.265
  195.7 3.9 copy.267
  199.6 2.4 copy-done
  202.0 12.8 %shard_map.331 = (bf16[512,6272]{1,0:T(8,128)(2,1)}, f32[512,384]{1,0:T(8,128)S(1)}) custom-call(bf16[512,384]{1,0:T(8,128)(2,1)S(1)} %pad.42.keyed_ref, bf16[384,6272]{1,0:T(8,128)(2,1)S(1)} %copy-done, f32[1,6272]{1,0:T(1,128)S(1)} %compare_convert_fusion.1.mask_ref), custom_call_target="tpu_custom_call" | custom-call | flops 4932501504 | bytes 12419072 | tf_op jit(solution)/shard_map/pallas_call | solution.py:400
  221.9 1.9 copy.263
  223.8 3.3 fusion.143
  229.9 2.9 fusion.52
  237.4 2.6 reshape.656
  240.1 3.9 copy.269
  244.0 4.0 copy.271
  248.0 3.9 copy.273
  251.9 3.9 copy.279
  255.9 3.2 copy.287
  259.0 3.9 copy.281
  263.0 4.4 fusion.58
  267.4 2.3 bitcast_convert_fusion.3
  269.7 2.3 bitcast_convert_fusion.4
  272.0 2.3 copy.420
  274.2 2.4 copy.421
  276.7 7.6 %fusion.145 = (f32[8,512]{1,0:T(8,128)S(1)}, f32[8,512,512]{1,2,0:T(8,128)}) fusion(bf16[512,8,128]{0,2,1:T(8,128)(2,1)} %bitcast.751, bf16[512,8,128]{0,2,1:T(8,128)(2,1)} %bitcast.753), kind=kOutput, calls=%fused_computation.325 | convolution fusion | flops 543162880 | bytes 10502144 | tf_op jit(solution)/shard_map/sub | solution.py:322
  284.3 4.7 divide_convert_fusion
  289.0 2.1 bitcast_convert_fusion.2
  296.2 2.7 fusion.50
  298.9 3.3 fusion.30
  302.2 2.8 reshape_reshape.22
  305.0 4.2 fusion.39
  312.3 2.3 bitcast_convert_fusion.1
  314.6 2.3 copy.290
  316.9 2.3 fusion.51
  319.2 4.8 convolution_convert_fusion.7
  325.3 2.5 multiply_convert_fusion.2
  332.6 1.8 copy.308
  345.8 2.8 copy.385
  350.3 2.7 convolution_convert_fusion
  353.0 2.8 convert_bitcast_fusion.1
  362.1 1.9 multiply_reduce_fusion.1
  365.9 1.8 convert_bitcast_fusion.4
  369.2 3.2 fusion.23
  372.5 2.0 reshape_reshape.23
  374.6 2.5 convert_bitcast_fusion.2
  381.6 2.7 convolution_convert_fusion.4
  386.5 2.0 convert_bitcast_fusion.3
  389.6 2.2 bitcast_convert_fusion
  395.3 2.6 convolution_convert_fusion.5
  397.9 9.1 %subtract_convert_fusion.1 = (bf16[512,261]{0,1:T(8,128)(2,1)}, bf16[512,261]{0,1:T(8,128)(2,1)}) fusion(bf16[261,6272]{1,0:T(8,128)(2,1)S(1)} %copy-done.21, bf16[512,6272]{1,0:T(8,128)(2,1)} %get-tuple-element.26, f32[512]{0:T(512)S(1)} %multiply_reduce_fusion.8, bf16[512,384]{1,0:T(8,128)(2,1)} %copy-done.93), kind=kOutput, calls=%fused_computation.199 | convolution fusion | flops 3365939200 | bytes 13975552 | tf_op jit(solution)/shard_map/dot_general | solution.py:39
  409.9 2.1 reshape.664
  418.7 2.6 convolution_convert_fusion.6
  427.1 3.0 convolution_convert_fusion.1
  442.6 1.9 constant_dynamic-update-slice_fusion.17
  454.0 1.8 constant_dynamic-update-slice_fusion.11
  458.4 143.0 %reduce-scatter.3.cloned.1.call-done = bf16[11136,128]{1,0:T(8,128)(2,1)} async-done(((bf16[89088,128]{1,0:T(8,128)(2,1)}), bf16[11136,128]{1,0:T(8,128)(2,1)}) %reduce-scatter.3.cloned.1.call-update) | async-done | bytes 2850832 | tf_op jit(solution)/shard_map/reduce_scatter | solution.py:240
  601.5 4.1 copy.283
  605.6 4.3 fusion.49
  610.0 2.2 add_add_fusion.4
  612.2 47.4 %reduce-scatter.5.cloned.1.call-done = bf16[2784,128]{1,0:T(8,128)(2,1)} async-done(((bf16[11136,128]{1,0:T(8,128)(2,1)}), bf16[2784,128]{1,0:T(8,128)(2,1)}) %reduce-scatter.5.cloned.1.call-update) | async-done | bytes 712720 | tf_op jit(solution)/shard_map/reduce_scatter | solution.py:243
  662.9 1.9 slice_convert_fusion.4
  (386 shorter events, 130.0 us)
Async XLA Ops:
  7.2 9.7 %copy-start.94 = (f32[256,128]{1,0:T(8,128)S(1)}, f32[256,128]{1,0:T(8,128)}, u32[]{:S(2)}) copy-start(f32[256,128]{1,0:T(8,128)} %param.29) | copy-start | bytes 393220
  7.2 9.8 %copy-start.95 = (f32[256,128]{1,0:T(8,128)S(1)}, f32[256,128]{1,0:T(8,128)}, u32[]{:S(2)}) copy-start(f32[256,128]{1,0:T(8,128)} %param.33) | copy-start | bytes 393220
  7.2 9.9 %copy-start.96 = (f32[256,128]{1,0:T(8,128)S(1)}, f32[256,128]{1,0:T(8,128)}, u32[]{:S(2)}) copy-start(f32[256,128]{1,0:T(8,128)} %param.35) | copy-start | bytes 393220
  7.2 156.3 %all-gather.2.cloned.1.call-start = ((), (), s32[]{:S(2)}) async-start(), calls=%async_computation.2 | async-start | bytes 23519232 | tf_op jit(solution)/shard_map/all_gather | solution.py:214
  8.2 10.0 %copy-start.97 = (s32[1,16384]{1,0:T(1,128)S(1)}, s32[1,16384]{1,0:T(1,128)}, u32[]{:S(2)}) copy-start(s32[1,16384]{1,0:T(1,128)} %param.22) | copy-start | bytes 196612
  18.1 583.3 %reduce-scatter.3.cloned.1.call-start = ((), (), s32[]{:S(2)}) async-start(), calls=%async_computation.3 | async-start | bytes 25657344 | tf_op jit(solution)/shard_map/reduce_scatter | solution.py:240
  32.7 3.4 copy-start.20
  32.8 3.5 copy-start.3
  36.5 145.8 %copy-start.101 = (f32[512]{0:T(512)}, f32[512]{0:T(512)S(1)}, u32[]{:S(2)}) copy-start(f32[512]{0:T(512)S(1)} %broadcast_multiply_fusion.4) | copy-start | bytes 6148
  36.9 129.9 %copy-start.106 = (f32[512]{0:T(512)}, f32[512]{0:T(512)S(1)}, u32[]{:S(2)}) copy-start(f32[512]{0:T(512)S(1)} %fusion.31) | copy-start | bytes 6148
  36.9 145.4 %copy-start.103 = (f32[512]{0:T(512)}, f32[512]{0:T(512)S(1)}, u32[]{:S(2)}) copy-start(f32[512]{0:T(512)S(1)} %fusion.131) | copy-start | bytes 6148
  166.8 17.2 %copy-start.59 = (bf16[32,96,128]{2,1,0:T(8,128)(2,1)}, bf16[32,96,128]{2,1,0:T(8,128)(2,1)S(1)}, u32[]{:S(2)}) copy-start(bf16[32,96,128]{2,1,0:T(8,128)(2,1)S(1)} %get-tuple-element.62) | copy-start | bytes 2359300
  199.6 2.4 copy-start
  214.8 4.6 copy-start.39
  216.7 3.4 copy-start.53
  223.8 3.3 copy-start.80
  227.1 5.7 copy-start.12
  227.5 2.3 copy-start.68
  229.9 2.9 copy-start.67
  263.0 4.4 copy-start.75
  263.0 4.4 copy-start.76
  267.4 2.3 copy-start.74
  284.3 4.7 copy-start.47
  289.0 2.8 copy-start.1
  289.0 3.1 copy-start.70
  293.9 2.3 copy-start.69
  296.2 2.7 copy-start.28
  296.2 2.7 copy-start.49
  305.0 4.3 copy-start.10
  316.9 2.3 copy-start.19
  319.2 4.8 copy-start.2
  319.2 4.8 copy-start.48
  325.3 2.5 copy-start.45
  327.8 2.8 copy-start.31
  334.6 2.3 copy-start.7
  336.9 2.3 copy-start.6
  339.3 2.3 copy-start.5
  355.8 2.3 copy-start.72
  355.8 2.6 copy-start.87
  365.9 2.8 copy-start.29
  365.9 3.4 copy-start.113
  377.1 2.3 copy-start.13
  377.1 3.0 copy-start.66
  385.0 3.6 copy-start.14
  385.1 3.5 copy-start.108
  386.5 3.0 copy-start.64
  395.3 2.6 copy-start.21
  407.0 4.9 copy-start.52
  418.6 2.6 copy-start.35
  418.6 2.6 copy-start.110
  418.7 2.6 copy-start.104
  427.0 3.0 copy-start.83
  427.1 3.0 copy-start.86
  440.4 2.2 copy-start.23
  449.6 2.2 copy-start.33
  458.3 201.2 %reduce-scatter.5.cloned.1.call-start = ((), (), s32[]{:S(2)}) async-start(), calls=%async_computation.4 | async-start | bytes 3563520 | tf_op jit(solution)/shard_map/reduce_scatter | solution.py:243
  601.4 4.1 copy-start.112
  601.4 4.1 copy-start.11
  605.5 4.4 copy-start.15
  605.5 4.4 copy-start.16
  605.6 4.4 copy-start.36
  605.6 4.4 copy-start.105
  605.6 4.4 copy-start.109
  605.6 4.4 copy-start.111
  (53 other events, 80.7 us)
Sparse Core Ops, SparseCore 0:
  18.2 145.3 all-gather.1
  458.5 142.9 reduce-scatter.2
  603.7 55.7 reduce-scatter.4

commit v10 on v9

--- a/solution.py
+++ b/solution.py
@@ -418,6 +418,40 @@
     )(keyed, pixel_pad, mask)
 
 
+def softmax_back_kernel(grad_ref, pixel_ref, weights_ref, dot_ref, mix_ref):
+    grad_weights = jnp.dot(grad_ref[...], pixel_ref[...], preferred_element_type=jnp.float32)
+    weights = weights_ref[...].astype(jnp.float32)
+    grad_scores = (weights * (grad_weights - dot_ref[...])).astype(jnp.bfloat16)
+    mix_ref[...] = lax.dot_general(
+        grad_scores, pixel_ref[...], (((1,), (1,)), ((), ())), preferred_element_type=jnp.float32
+    )
+
+
+def softmax_back_mix(grad_keyed, pixel_pad, weights_low, row_dot):
+    rows, channels = grad_keyed.shape
+    width = pixel_pad.shape[1]
+    block = min(SOFTMAX_ROWS, rows)
+    cost = pl.CostEstimate(
+        flops=4 * rows * channels * width,
+        transcendentals=0,
+        bytes_accessed=2 * (rows * channels + channels * width + rows * width) + 4 * rows * (channels + 1),
+    )
+    return pl.pallas_call(
+        softmax_back_kernel,
+        grid=(rows // block,),
+        in_specs=[
+            pl.BlockSpec((block, channels), lambda i: (i, 0)),
+            pl.BlockSpec((channels, width), lambda i: (0, 0)),
+            pl.BlockSpec((block, width), lambda i: (i, 0)),
+            pl.BlockSpec((block, 1), lambda i: (i, 0)),
+        ],
+        out_specs=pl.BlockSpec((block, channels), lambda i: (i, 0)),
+        out_shape=jax.ShapeDtypeStruct((rows, channels), jnp.float32),
+        compiler_params=pltpu.CompilerParams(vmem_limit_bytes=48 * 1024 * 1024),
+        cost_estimate=cost,
+    )(grad_keyed, pixel_pad, weights_low, row_dot)
+
+
 def cross_block(residual, gain_vec, query_w, key_w, value_w, out_w, pixel_norm, allowed):
     scale = 1.0 / math.sqrt(residual.shape[1])
     normed = rounded(norm_rows(residual, gain_vec))
@@ -434,7 +468,7 @@
 
 
 def cross_block_back(
-    residual, gain_vec, query_w, key_w, value_w, out_w, pixel_norm, saved, grad_out
+    residual, gain_vec, query_w, key_w, value_w, out_w, pixel_norm, allowed, saved, grad_out
 ):
     normed, query_rows, weights_low, pixel_mix, mixed = saved
     scale = 1.0 / math.sqrt(residual.shape[1])
@@ -443,9 +477,10 @@
     grad_mixed = rounded(apply_t(grad_round, out_w))
     grad_keyed = rounded(apply(grad_mixed, value_w))
     row_dot = jnp.sum(widened(grad_keyed) * pixel_mix, axis=-1, keepdims=True)
-    grad_weights = product(grad_keyed, pixel_norm)
-    grad_scores = rounded(widened(weights_low) * (grad_weights - row_dot))
-    score_mix = product_nt(grad_scores, pixel_norm)
+    pixel_pad = allowed[0]
+    channels = pixel_norm.shape[0]
+    grad_pad = jnp.pad(grad_keyed, ((0, 0), (0, pixel_pad.shape[0] - channels)))
+    score_mix = softmax_back_mix(grad_pad, pixel_pad, weights_low, row_dot)[:, :channels]
     grad_query = rounded(split_apply_t(score_mix, key_w) * scale)
     grad_query_w = grad_blocks(normed, grad_query, query_w)
     grad_key_w = split_grad_blocks(query_rows, score_mix, key_w) * scale
@@ -526,6 +561,7 @@
         value_cross,
         out_cross,
         pixel_norm,
+        allowed,
         saved_cross,
         grad_after_cross,
     )

time: 685 us -> 683 us (level)
  Pallas kernels: 12.8 us -> 25.4 us
  matrix products: 112 us -> 105 us
  local copies, waits for them, and re-layouts: 160 us -> 153 us
    pallas_call x0 -> x1, Pallas kernels: none -> 12.6 us  [softmax_back_mix(): pl.pallas_call(softmax_back_kernel, grid=(rows // block,), in_specs=[pl.B...]
    dot_general x1 -> x0, matrix products: 9.12 us -> none  [product_nt(): lax.dot_general(left_side, right_side, (((1,), (1,)), ((), ())), preferre...]
    unnamed x256 -> x242, local copies, waits for them, and re-layouts: 51.6 us -> 49.8 us
where the time goes in v10:
time: 683 us; the launch traced here: 675 us
  waiting for transfers between devices  318 us (47%)
  local copies, waits for them, and re-layouts  153 us (22%)
  matrix products  105 us (15%)
  other arithmetic  55.4 us (8%)
  Pallas kernels  25.4 us (4%)
  between operations  17.9 us (3%)
    reduce_scatter x1, waiting for transfers between devices, reduce_grads(): lax.psum_scatter(packed.reshape(count * total, PANEL), 'items', scatter_d...  143 us
    all_gather x1, waiting for transfers between devices, gather_weights(): lax.all_gather(packed, ALL, axis=0, tiled=True).reshape(count, total, PANEL)  127 us
    dot_general x40, matrix products, contract(): lax.dot_general(left, right, ((left_dims, right_dims), ((), ())), preferr...  85.1 us
    unnamed x242, local copies, waits for them, and re-layouts  49.8 us
    reduce_scatter x1, waiting for transfers between devices, reduce_grads(): mine = lax.psum_scatter(mine, 'heads', scatter_dimension=0, tiled=True)  47.5 us
    dot_general x17, local copies, waits for them, and re-layouts, contract(): lax.dot_general(left, right, ((left_dims, right_dims), ((), ())), preferr...  45.9 us
    slice x2, local copies, waits for them, and re-layouts, gather_weights(): piece = gathered[:, first:first + rows, :]  17.6 us
  transfers between devices with their start and end apart: 3, of which 3 were waited for; matrix products, arithmetic and copies ran while one was open for 4% of the time, Pallas kernels for 0%

profile of v10, /device:TPU:0, one launch (start us, length us, event | category | flops | bytes accessed | tf_op | source)
XLA Modules:
  0.0 675.3 jit_solution(16968390710267211328)
XLA Ops:
  21.5 3.3 convert_reduce_fusion
  24.8 3.7 fusion.4
  28.5 4.2 fusion.5
  32.8 2.5 pad.46.pixel_ref
  36.1 127.5 %all-gather.2.cloned.1.call-done = bf16[89088,128]{1,0:T(8,128)(2,1)} async-done(((bf16[2784,128]{1,0:T(8,128)(2,1)}), bf16[89088,128]{1,0:T(8,128)(2,1)}) %all-gather.2.cloned.1.call-update) | async-done | bytes 22806544 | tf_op jit(solution)/shard_map/all_gather | solution.py:214
  164.5 2.4 fusion.141
  166.8 15.2 %fusion.140 = (bf16[32,256,128]{2,1,0:T(8,128)(2,1)}, bf16[32,256,128]{2,1,0:T(8,128)(2,1)}, bf16[32,256,128]{2,1,0:T(8,128)(2,1)}, bf16[32,256,128]{2,1,0:T(8,1...) fusion(bf16[32,2784,128]{2,1,0:T(8,128)(2,1)} %bitcast.710), kind=kLoop, calls=%fused_computation.320 | loop fusion | bytes 41943040 | tf_op jit(solution)/shard_map/slice | solution.py:217
  185.3 4.2 bitcast_convert_fusion.6
  192.2 3.9 copy.268
  196.1 3.9 copy.270
  200.0 2.4 copy-done
  202.4 12.8 %shard_map.331 = (bf16[512,6272]{1,0:T(8,128)(2,1)}, f32[512,384]{1,0:T(8,128)S(1)}) custom-call(bf16[512,384]{1,0:T(8,128)(2,1)S(1)} %pad.45.keyed_ref, bf16[384,6272]{1,0:T(8,128)(2,1)S(1)} %copy-done, f32[1,6272]{1,0:T(1,128)S(1)} %compare_convert_fusion.1.mask_ref), custom_call_target="tpu_custom_call" | custom-call | flops 4932501504 | bytes 12419072 | tf_op jit(solution)/shard_map/pallas_call | solution.py:400
  224.0 3.3 fusion.143
  230.0 2.9 fusion.52
  237.4 2.7 reshape.655
  240.1 3.9 copy.272
  244.1 3.9 copy.274
  248.0 3.9 copy.276
  251.9 3.9 copy.282
  255.8 3.2 copy.290
  259.0 3.9 copy.284
  262.9 4.3 fusion.58
  267.3 2.3 bitcast_convert_fusion.3
  269.6 2.3 bitcast_convert_fusion.4
  271.8 2.3 copy.428
  274.1 2.5 copy.429
  276.6 7.7 %fusion.145 = (f32[8,512]{1,0:T(8,128)S(1)}, f32[8,512,512]{1,2,0:T(8,128)}) fusion(bf16[512,8,128]{0,2,1:T(8,128)(2,1)} %bitcast.754, bf16[512,8,128]{0,2,1:T(8,128)(2,1)} %bitcast.756), kind=kOutput, calls=%fused_computation.325 | convolution fusion | flops 543162880 | bytes 10502144 | tf_op jit(solution)/shard_map/sub | solution.py:322
  284.3 4.7 divide_convert_fusion
  289.0 2.1 bitcast_convert_fusion.2
  296.2 2.7 fusion.50
  298.9 3.3 fusion.30
  302.2 3.0 reshape_reshape.22
  305.1 4.2 fusion.39
  312.5 2.3 bitcast_convert_fusion.1
  314.8 2.3 copy.293
  317.1 2.3 fusion.51
  319.4 4.9 convolution_convert_fusion.7
  325.6 2.5 multiply_convert_fusion.1
  346.1 2.6 copy.391
  350.3 2.6 convolution_convert_fusion
  352.9 2.8 convert_bitcast_fusion.1
  362.1 1.9 multiply_reduce_fusion.1
  365.8 1.9 convert_bitcast_fusion.4
  369.1 3.3 fusion.23
  372.4 2.1 reshape_reshape.23
  374.5 2.5 convert_bitcast_fusion.2
  381.6 2.7 convolution_convert_fusion.4
  385.1 2.5 convert_bitcast_fusion.3
  388.7 2.3 bitcast_convert_fusion
  392.6 3.9 convolution_convert_fusion.5
  397.5 12.6 %shard_map.332 = f32[512,384]{1,0:T(8,128)S(1)} custom-call(bf16[512,384]{1,0:T(8,128)(2,1)S(1)} %get-tuple-element.95.grad_ref, bf16[384,6272]{1,0:T(8,128)(2,1)} %pad.46.pixel_ref, bf16[512,6272]{1,0:T(8,128)(2,1)} %get-tuple-element.25.weights_ref, f32[512,1]{1,0:T(8,128)S(1)} %copy.316.dot_ref), custom_call_target="tpu_custom_call" | custom-call | flops 4932501504 | bytes 12421120 | tf_op jit(solution)/shard_map/pallas_call | solution.py:439
  410.7 3.3 reshape.663
  414.0 2.5 convert_bitcast_fusion
  422.2 2.6 convolution_convert_fusion.6
  426.1 2.7 convolution_convert_fusion.1
  439.1 1.8 constant_dynamic-update-slice_fusion.18
  441.3 1.9 constant_dynamic-update-slice_fusion.17
  452.7 1.8 constant_dynamic-update-slice_fusion.11
  457.5 143.0 %reduce-scatter.3.cloned.1.call-done = bf16[11136,128]{1,0:T(8,128)(2,1)} async-done(((bf16[89088,128]{1,0:T(8,128)(2,1)}), bf16[11136,128]{1,0:T(8,128)(2,1)}) %reduce-scatter.3.cloned.1.call-update) | async-done | bytes 2850832 | tf_op jit(solution)/shard_map/reduce_scatter | solution.py:240
  600.5 4.1 copy.286
  604.6 4.3 fusion.49
  609.0 2.2 add_add_fusion.4
  611.2 47.5 %reduce-scatter.5.cloned.1.call-done = bf16[2784,128]{1,0:T(8,128)(2,1)} async-done(((bf16[11136,128]{1,0:T(8,128)(2,1)}), bf16[2784,128]{1,0:T(8,128)(2,1)}) %reduce-scatter.5.cloned.1.call-update) | async-done | bytes 712720 | tf_op jit(solution)/shard_map/reduce_scatter | solution.py:243
  662.0 1.9 slice_convert_fusion.2
  (374 shorter events, 121.2 us)
Async XLA Ops:
  7.2 9.7 %copy-start.92 = (f32[256,128]{1,0:T(8,128)S(1)}, f32[256,128]{1,0:T(8,128)}, u32[]{:S(2)}) copy-start(f32[256,128]{1,0:T(8,128)} %param.29) | copy-start | bytes 393220
  7.2 9.8 %copy-start.93 = (f32[256,128]{1,0:T(8,128)S(1)}, f32[256,128]{1,0:T(8,128)}, u32[]{:S(2)}) copy-start(f32[256,128]{1,0:T(8,128)} %param.33) | copy-start | bytes 393220
  7.2 9.9 %copy-start.94 = (f32[256,128]{1,0:T(8,128)S(1)}, f32[256,128]{1,0:T(8,128)}, u32[]{:S(2)}) copy-start(f32[256,128]{1,0:T(8,128)} %param.35) | copy-start | bytes 393220
  7.2 156.3 %all-gather.2.cloned.1.call-start = ((), (), s32[]{:S(2)}) async-start(), calls=%async_computation.2 | async-start | bytes 23519232 | tf_op jit(solution)/shard_map/all_gather | solution.py:214
  8.2 10.0 %copy-start.95 = (s32[1,16384]{1,0:T(1,128)S(1)}, s32[1,16384]{1,0:T(1,128)}, u32[]{:S(2)}) copy-start(s32[1,16384]{1,0:T(1,128)} %param.22) | copy-start | bytes 196612
  18.1 582.4 %reduce-scatter.3.cloned.1.call-start = ((), (), s32[]{:S(2)}) async-start(), calls=%async_computation.3 | async-start | bytes 25657344 | tf_op jit(solution)/shard_map/reduce_scatter | solution.py:240
  32.7 2.6 copy-start.3
  35.6 146.9 %copy-start.98 = (f32[512]{0:T(512)}, f32[512]{0:T(512)S(1)}, u32[]{:S(2)}) copy-start(f32[512]{0:T(512)S(1)} %broadcast_multiply_fusion.4) | copy-start | bytes 6148
  36.0 130.8 %copy-start.102 = (f32[512]{0:T(512)}, f32[512]{0:T(512)S(1)}, u32[]{:S(2)}) copy-start(f32[512]{0:T(512)S(1)} %fusion.31) | copy-start | bytes 6148
  36.1 146.5 %copy-start.100 = (f32[512]{0:T(512)}, f32[512]{0:T(512)S(1)}, u32[]{:S(2)}) copy-start(f32[512]{0:T(512)S(1)} %fusion.131) | copy-start | bytes 6148
  166.8 17.5 %copy-start.59 = (bf16[32,96,128]{2,1,0:T(8,128)(2,1)}, bf16[32,96,128]{2,1,0:T(8,128)(2,1)S(1)}, u32[]{:S(2)}) copy-start(bf16[32,96,128]{2,1,0:T(8,128)(2,1)S(1)} %get-tuple-element.60) | copy-start | bytes 2359300
  200.0 2.4 copy-start
  215.2 4.6 copy-start.36
  217.1 3.4 copy-start.51
  224.0 3.3 copy-start.80
  227.3 5.6 copy-start.12
  227.7 2.3 copy-start.68
  230.0 2.9 copy-start.67
  262.9 4.3 copy-start.75
  262.9 4.4 copy-start.76
  267.3 2.3 copy-start.74
  284.3 4.7 copy-start.45
  289.0 2.8 copy-start.1
  289.0 3.1 copy-start.70
  293.8 2.3 copy-start.69
  296.2 2.7 copy-start.24
  296.2 2.7 copy-start.47
  305.1 4.3 copy-start.10
  317.1 2.3 copy-start.19
  319.4 4.9 copy-start.2
  319.4 4.9 copy-start.46
  325.6 2.5 copy-start.43
  328.1 2.7 copy-start.27
  334.8 2.3 copy-start.7
  337.2 2.3 copy-start.6
  339.5 2.3 copy-start.5
  355.7 2.3 copy-start.72
  355.7 2.6 copy-start.86
  365.8 2.8 copy-start.25
  365.8 3.3 copy-start.105
  372.4 2.1 copy-start.82
  377.0 2.3 copy-start.13
  377.0 3.0 copy-start.66
  385.0 2.7 copy-start.14
  385.1 3.5 copy-start.64
  392.6 3.9 copy-start.60
  392.6 3.9 copy-start.104
  410.4 3.6 copy-start.50
  410.4 8.4 %copy-start.53 = (bf16[512,384]{0,1:T(8,128)(2,1)}, bf16[512,384]{0,1:T(8,128)(2,1)S(1)}, u32[]{:S(2)}) copy-start(bf16[512,384]{0,1:T(8,128)(2,1)S(1)} %pad.51.clone) | copy-start | bytes 1179652
  410.7 7.4 %copy-start.57 = (bf16[512,384]{0,1:T(8,128)(2,1)}, bf16[512,384]{0,1:T(8,128)(2,1)S(1)}, u32[]{:S(2)}) copy-start(bf16[512,384]{0,1:T(8,128)(2,1)S(1)} %pad.50.clone) | copy-start | bytes 1179652
  422.2 2.6 copy-start.32
  422.2 2.6 copy-start.101
  426.1 2.7 copy-start.81
  426.1 2.7 copy-start.85
  437.0 2.1 copy-start.65
  439.1 2.2 copy-start.21
  448.3 2.2 copy-start.29
  450.5 2.2 copy-start.20
  452.7 2.2 copy-start.31
  457.4 201.3 %reduce-scatter.5.cloned.1.call-start = ((), (), s32[]{:S(2)}) async-start(), calls=%async_computation.4 | async-start | bytes 3563520 | tf_op jit(solution)/shard_map/reduce_scatter | solution.py:243
  600.5 4.1 copy-start.11
  604.6 4.3 copy-start.15
  604.6 4.3 copy-start.16
  604.6 4.3 copy-start.33
  (45 other events, 67.1 us)
Sparse Core Ops, SparseCore 0:
  18.2 145.3 all-gather.1
  457.6 142.9 reduce-scatter.2
  602.8 55.8 reduce-scatter.4

commit v11 on v10

--- a/solution.py
+++ b/solution.py
@@ -372,7 +372,7 @@
     return window, ids == item
 
 
-SOFTMAX_ROWS = 128
+SOFTMAX_ROWS = 256
 
 
 def softmax_mix_kernel(keyed_ref, pixel_ref, mask_ref, weights_ref, mix_ref):

time: 683 us -> 679 us (level)
  no operation moved by 1% of the time
where the time goes in v11:
time: 679 us; the launch traced here: 671 us
  waiting for transfers between devices  318 us (47%)
  local copies, waits for them, and re-layouts  153 us (23%)
  matrix products  105 us (15%)
  other arithmetic  55.4 us (8%)
  Pallas kernels  21.1 us (3%)
  between operations  18.1 us (3%)
    reduce_scatter x1, waiting for transfers between devices, reduce_grads(): lax.psum_scatter(packed.reshape(count * total, PANEL), 'items', scatter_d...  143 us
    all_gather x1, waiting for transfers between devices, gather_weights(): lax.all_gather(packed, ALL, axis=0, tiled=True).reshape(count, total, PANEL)  127 us
    dot_general x40, matrix products, contract(): lax.dot_general(left, right, ((left_dims, right_dims), ((), ())), preferr...  85.1 us
    unnamed x242, local copies, waits for them, and re-layouts  49.9 us
    reduce_scatter x1, waiting for transfers between devices, reduce_grads(): mine = lax.psum_scatter(mine, 'heads', scatter_dimension=0, tiled=True)  47.5 us
    dot_general x17, local copies, waits for them, and re-layouts, contract(): lax.dot_general(left, right, ((left_dims, right_dims), ((), ())), preferr...  45.9 us
    slice x2, local copies, waits for them, and re-layouts, gather_weights(): piece = gathered[:, first:first + rows, :]  17.3 us
  transfers between devices with their start and end apart: 3, of which 3 were waited for; matrix products, arithmetic and copies ran while one was open for 4% of the time, Pallas kernels for 0%

profile of v11, /device:TPU:0, one launch (start us, length us, event | category | flops | bytes accessed | tf_op | source)
XLA Modules:
  0.0 671.0 jit_solution(16689520742022597033)
XLA Ops:
  21.5 3.3 convert_reduce_fusion
  24.8 3.7 fusion.4
  28.5 4.2 fusion.5
  32.8 2.5 pad.46.pixel_ref
  36.1 127.5 %all-gather.2.cloned.1.call-done = bf16[89088,128]{1,0:T(8,128)(2,1)} async-done(((bf16[2784,128]{1,0:T(8,128)(2,1)}), bf16[89088,128]{1,0:T(8,128)(2,1)}) %all-gather.2.cloned.1.call-update) | async-done | bytes 22806544 | tf_op jit(solution)/shard_map/all_gather | solution.py:214
  164.5 2.4 fusion.141
  166.8 15.0 %fusion.140 = (bf16[32,256,128]{2,1,0:T(8,128)(2,1)}, bf16[32,256,128]{2,1,0:T(8,128)(2,1)}, bf16[32,256,128]{2,1,0:T(8,128)(2,1)}, bf16[32,256,128]{2,1,0:T(8,1...) fusion(bf16[32,2784,128]{2,1,0:T(8,128)(2,1)} %bitcast.710), kind=kLoop, calls=%fused_computation.320 | loop fusion | bytes 41943040 | tf_op jit(solution)/shard_map/slice | solution.py:217
  185.0 4.2 bitcast_convert_fusion.6
  191.9 3.9 copy.268
  195.8 3.9 copy.270
  199.7 2.4 copy-done
  202.1 10.6 %shard_map.331 = (bf16[512,6272]{1,0:T(8,128)(2,1)}, f32[512,384]{1,0:T(8,128)S(1)}) custom-call(bf16[512,384]{1,0:T(8,128)(2,1)S(1)} %pad.45.keyed_ref, bf16[384,6272]{1,0:T(8,128)(2,1)S(1)} %copy-done, f32[1,6272]{1,0:T(1,128)S(1)} %compare_convert_fusion.1.mask_ref), custom_call_target="tpu_custom_call" | custom-call | flops 4932501504 | bytes 12419072 | tf_op jit(solution)/shard_map/pallas_call | solution.py:400
  219.8 1.9 copy.266
  221.7 3.3 fusion.143
  227.8 2.9 fusion.52
  235.2 2.7 reshape.655
  237.9 3.9 copy.272
  241.8 3.9 copy.274
  245.7 3.9 copy.276
  249.6 3.9 copy.282
  253.6 3.2 copy.290
  256.7 3.9 copy.284
  260.7 4.3 fusion.58
  265.0 2.3 bitcast_convert_fusion.3
  267.3 2.3 bitcast_convert_fusion.4
  269.6 2.3 copy.428
  271.9 2.4 copy.429
  274.3 7.7 %fusion.145 = (f32[8,512]{1,0:T(8,128)S(1)}, f32[8,512,512]{1,2,0:T(8,128)}) fusion(bf16[512,8,128]{0,2,1:T(8,128)(2,1)} %bitcast.754, bf16[512,8,128]{0,2,1:T(8,128)(2,1)} %bitcast.756), kind=kOutput, calls=%fused_computation.325 | convolution fusion | flops 543162880 | bytes 10502144 | tf_op jit(solution)/shard_map/sub | solution.py:322
  282.0 4.7 divide_convert_fusion
  286.7 2.1 bitcast_convert_fusion.2
  293.9 2.7 fusion.50
  296.6 3.3 fusion.30
  299.9 2.8 reshape_reshape.22
  302.7 4.2 fusion.39
  310.0 2.3 bitcast_convert_fusion.1
  312.4 2.3 copy.293
  314.6 2.3 fusion.51
  317.0 4.9 convolution_convert_fusion.7
  323.1 2.5 multiply_convert_fusion.1
  343.6 2.8 copy.391
  348.0 2.6 convolution_convert_fusion
  350.7 2.8 convert_bitcast_fusion.1
  359.8 1.9 multiply_reduce_fusion.1
  363.6 1.9 convert_bitcast_fusion.4
  366.9 3.3 fusion.23
  370.1 2.0 reshape_reshape.23
  372.2 2.5 convert_bitcast_fusion.2
  379.3 2.7 convolution_convert_fusion.4
  382.9 2.5 convert_bitcast_fusion.3
  386.4 2.3 bitcast_convert_fusion
  390.3 3.9 convolution_convert_fusion.5
  395.2 10.5 %shard_map.332 = f32[512,384]{1,0:T(8,128)S(1)} custom-call(bf16[512,384]{1,0:T(8,128)(2,1)S(1)} %get-tuple-element.95.grad_ref, bf16[384,6272]{1,0:T(8,128)(2,1)} %pad.46.pixel_ref, bf16[512,6272]{1,0:T(8,128)(2,1)} %get-tuple-element.25.weights_ref, f32[512,1]{1,0:T(8,128)S(1)} %copy.316.dot_ref), custom_call_target="tpu_custom_call" | custom-call | flops 4932501504 | bytes 12421120 | tf_op jit(solution)/shard_map/pallas_call | solution.py:439
  406.2 3.2 reshape.663
  409.4 2.5 convert_bitcast_fusion
  417.6 2.6 convolution_convert_fusion.6
  421.5 2.7 convolution_convert_fusion.1
  436.7 2.0 constant_dynamic-update-slice_fusion.17
  448.2 1.8 constant_dynamic-update-slice_fusion.11
  452.9 143.0 %reduce-scatter.3.cloned.1.call-done = bf16[11136,128]{1,0:T(8,128)(2,1)} async-done(((bf16[89088,128]{1,0:T(8,128)(2,1)}), bf16[11136,128]{1,0:T(8,128)(2,1)}) %reduce-scatter.3.cloned.1.call-update) | async-done | bytes 2850832 | tf_op jit(solution)/shard_map/reduce_scatter | solution.py:240
  596.0 4.1 copy.286
  600.1 4.3 fusion.49
  604.4 2.2 add_add_fusion.4
  606.6 47.5 %reduce-scatter.5.cloned.1.call-done = bf16[2784,128]{1,0:T(8,128)(2,1)} async-done(((bf16[11136,128]{1,0:T(8,128)(2,1)}), bf16[2784,128]{1,0:T(8,128)(2,1)}) %reduce-scatter.5.cloned.1.call-update) | async-done | bytes 712720 | tf_op jit(solution)/shard_map/reduce_scatter | solution.py:243
  657.5 1.9 slice_convert_fusion.2
  (374 shorter events, 121.3 us)
Async XLA Ops:
  7.2 9.7 %copy-start.92 = (f32[256,128]{1,0:T(8,128)S(1)}, f32[256,128]{1,0:T(8,128)}, u32[]{:S(2)}) copy-start(f32[256,128]{1,0:T(8,128)} %param.29) | copy-start | bytes 393220
  7.2 9.8 %copy-start.93 = (f32[256,128]{1,0:T(8,128)S(1)}, f32[256,128]{1,0:T(8,128)}, u32[]{:S(2)}) copy-start(f32[256,128]{1,0:T(8,128)} %param.33) | copy-start | bytes 393220
  7.2 9.9 %copy-start.94 = (f32[256,128]{1,0:T(8,128)S(1)}, f32[256,128]{1,0:T(8,128)}, u32[]{:S(2)}) copy-start(f32[256,128]{1,0:T(8,128)} %param.35) | copy-start | bytes 393220
  7.2 156.3 %all-gather.2.cloned.1.call-start = ((), (), s32[]{:S(2)}) async-start(), calls=%async_computation.2 | async-start | bytes 23519232 | tf_op jit(solution)/shard_map/all_gather | solution.py:214
  8.2 10.0 %copy-start.95 = (s32[1,16384]{1,0:T(1,128)S(1)}, s32[1,16384]{1,0:T(1,128)}, u32[]{:S(2)}) copy-start(s32[1,16384]{1,0:T(1,128)} %param.22) | copy-start | bytes 196612
  18.1 577.9 %reduce-scatter.3.cloned.1.call-start = ((), (), s32[]{:S(2)}) async-start(), calls=%async_computation.3 | async-start | bytes 25657344 | tf_op jit(solution)/shard_map/reduce_scatter | solution.py:240
  32.7 2.6 copy-start.3
  35.6 146.7 %copy-start.98 = (f32[512]{0:T(512)}, f32[512]{0:T(512)S(1)}, u32[]{:S(2)}) copy-start(f32[512]{0:T(512)S(1)} %broadcast_multiply_fusion.4) | copy-start | bytes 6148
  36.0 130.8 %copy-start.102 = (f32[512]{0:T(512)}, f32[512]{0:T(512)S(1)}, u32[]{:S(2)}) copy-start(f32[512]{0:T(512)S(1)} %fusion.31) | copy-start | bytes 6148
  36.1 146.2 %copy-start.100 = (f32[512]{0:T(512)}, f32[512]{0:T(512)S(1)}, u32[]{:S(2)}) copy-start(f32[512]{0:T(512)S(1)} %fusion.131) | copy-start | bytes 6148
  166.8 17.2 %copy-start.59 = (bf16[32,96,128]{2,1,0:T(8,128)(2,1)}, bf16[32,96,128]{2,1,0:T(8,128)(2,1)S(1)}, u32[]{:S(2)}) copy-start(bf16[32,96,128]{2,1,0:T(8,128)(2,1)S(1)} %get-tuple-element.60) | copy-start | bytes 2359300
  199.7 2.4 copy-start
  212.7 4.6 copy-start.36
  214.6 3.4 copy-start.51
  221.7 3.3 copy-start.80
  225.1 5.6 copy-start.12
  225.4 2.3 copy-start.68
  227.8 2.9 copy-start.67
  260.7 4.3 copy-start.75
  260.7 4.4 copy-start.76
  265.0 2.3 copy-start.74
  282.0 4.7 copy-start.45
  286.7 2.8 copy-start.1
  286.7 3.1 copy-start.70
  291.6 2.3 copy-start.69
  293.9 2.7 copy-start.24
  293.9 2.7 copy-start.47
  302.7 4.3 copy-start.10
  314.6 2.3 copy-start.19
  317.0 4.9 copy-start.2
  317.0 4.9 copy-start.46
  323.1 2.5 copy-start.43
  325.6 2.7 copy-start.27
  332.3 2.3 copy-start.7
  334.7 2.3 copy-start.6
  337.0 2.3 copy-start.5
  353.5 2.3 copy-start.72
  353.5 2.6 copy-start.86
  363.6 2.8 copy-start.25
  363.6 3.3 copy-start.105
  370.1 2.1 copy-start.82
  374.7 2.3 copy-start.13
  374.7 3.0 copy-start.66
  382.7 2.7 copy-start.14
  382.8 3.5 copy-start.64
  390.3 3.9 copy-start.60
  390.3 3.9 copy-start.104
  406.0 3.4 copy-start.50
  406.0 8.2 %copy-start.53 = (bf16[512,384]{0,1:T(8,128)(2,1)}, bf16[512,384]{0,1:T(8,128)(2,1)S(1)}, u32[]{:S(2)}) copy-start(bf16[512,384]{0,1:T(8,128)(2,1)S(1)} %pad.51.clone) | copy-start | bytes 1179652
  406.2 7.2 %copy-start.57 = (bf16[512,384]{0,1:T(8,128)(2,1)}, bf16[512,384]{0,1:T(8,128)(2,1)S(1)}, u32[]{:S(2)}) copy-start(bf16[512,384]{0,1:T(8,128)(2,1)S(1)} %pad.50.clone) | copy-start | bytes 1179652
  417.6 2.6 copy-start.32
  417.6 2.6 copy-start.101
  421.4 2.7 copy-start.81
  421.4 2.7 copy-start.85
  432.4 2.1 copy-start.65
  434.5 2.2 copy-start.21
  443.8 2.2 copy-start.29
  446.0 2.2 copy-start.20
  448.2 2.2 copy-start.31
  452.9 201.3 %reduce-scatter.5.cloned.1.call-start = ((), (), s32[]{:S(2)}) async-start(), calls=%async_computation.4 | async-start | bytes 3563520 | tf_op jit(solution)/shard_map/reduce_scatter | solution.py:243
  596.0 4.1 copy-start.11
  600.1 4.3 copy-start.15
  600.1 4.3 copy-start.16
  600.1 4.3 copy-start.33
  (45 other events, 67.2 us)
Sparse Core Ops, SparseCore 0:
  18.2 145.3 all-gather.1
  453.0 142.9 reduce-scatter.2
  598.3 55.7 reduce-scatter.4

commit v12 on v11

--- a/solution.py
+++ b/solution.py
@@ -372,7 +372,7 @@
     return window, ids == item
 
 
-SOFTMAX_ROWS = 256
+SOFTMAX_ROWS = 512
 
 
 def softmax_mix_kernel(keyed_ref, pixel_ref, mask_ref, weights_ref, mix_ref):

time: 679 us -> 682 us (level)
  no operation moved by 1% of the time
where the time goes in v12:
time: 682 us; the launch traced here: 671 us
  waiting for transfers between devices  318 us (47%)
  local copies, waits for them, and re-layouts  153 us (22%)
  matrix products  105 us (15%)
  other arithmetic  55.4 us (8%)
  Pallas kernels  21.3 us (3%)
  between operations  18.1 us (3%)
    reduce_scatter x1, waiting for transfers between devices, reduce_grads(): lax.psum_scatter(packed.reshape(count * total, PANEL), 'items', scatter_d...  143 us
    all_gather x1, waiting for transfers between devices, gather_weights(): lax.all_gather(packed, ALL, axis=0, tiled=True).reshape(count, total, PANEL)  127 us
    dot_general x40, matrix products, contract(): lax.dot_general(left, right, ((left_dims, right_dims), ((), ())), preferr...  85.1 us
    unnamed x242, local copies, waits for them, and re-layouts  49.9 us
    reduce_scatter x1, waiting for transfers between devices, reduce_grads(): mine = lax.psum_scatter(mine, 'heads', scatter_dimension=0, tiled=True)  47.5 us
    dot_general x17, local copies, waits for them, and re-layouts, contract(): lax.dot_general(left, right, ((left_dims, right_dims), ((), ())), preferr...  46.1 us
    slice x2, local copies, waits for them, and re-layouts, gather_weights(): piece = gathered[:, first:first + rows, :]  17.3 us
  transfers between devices with their start and end apart: 3, of which 3 were waited for; matrix products, arithmetic and copies ran while one was open for 4% of the time, Pallas kernels for 0%

profile of v12, /device:TPU:0, one launch (start us, length us, event | category | flops | bytes accessed | tf_op | source)
XLA Modules:
  0.0 671.5 jit_solution(8626269467230655862)
XLA Ops:
  21.5 3.3 convert_reduce_fusion
  24.8 3.7 fusion.4
  28.5 4.2 fusion.5
  32.8 2.5 pad.46.pixel_ref
  36.1 127.5 %all-gather.2.cloned.1.call-done = bf16[89088,128]{1,0:T(8,128)(2,1)} async-done(((bf16[2784,128]{1,0:T(8,128)(2,1)}), bf16[89088,128]{1,0:T(8,128)(2,1)}) %all-gather.2.cloned.1.call-update) | async-done | bytes 22806544 | tf_op jit(solution)/shard_map/all_gather | solution.py:214
  164.5 2.4 fusion.141
  166.8 15.0 %fusion.140 = (bf16[32,256,128]{2,1,0:T(8,128)(2,1)}, bf16[32,256,128]{2,1,0:T(8,128)(2,1)}, bf16[32,256,128]{2,1,0:T(8,128)(2,1)}, bf16[32,256,128]{2,1,0:T(8,1...) fusion(bf16[32,2784,128]{2,1,0:T(8,128)(2,1)} %bitcast.710), kind=kLoop, calls=%fused_computation.320 | loop fusion | bytes 41943040 | tf_op jit(solution)/shard_map/slice | solution.py:217
  185.0 4.2 bitcast_convert_fusion.6
  191.9 3.9 copy.268
  195.8 4.1 copy.270
  199.9 2.4 copy-done
  202.3 10.2 %shard_map.331 = (bf16[512,6272]{1,0:T(8,128)(2,1)}, f32[512,384]{1,0:T(8,128)S(1)}) custom-call(bf16[512,384]{1,0:T(8,128)(2,1)S(1)} %pad.45.keyed_ref, bf16[384,6272]{1,0:T(8,128)(2,1)S(1)} %copy-done, f32[1,6272]{1,0:T(1,128)S(1)} %compare_convert_fusion.1.mask_ref), custom_call_target="tpu_custom_call" | custom-call | flops 4932501504 | bytes 12419072 | tf_op jit(solution)/shard_map/pallas_call | solution.py:400
  219.6 1.9 copy.266
  221.5 3.3 fusion.143
  227.6 2.9 fusion.52
  235.0 2.7 reshape.655
  237.7 3.9 copy.272
  241.6 3.9 copy.274
  245.5 3.9 copy.276
  249.4 3.9 copy.282
  253.4 3.2 copy.290
  256.5 3.9 copy.284
  260.5 4.3 fusion.58
  264.8 2.3 bitcast_convert_fusion.3
  267.1 2.3 bitcast_convert_fusion.4
  269.4 2.3 copy.428
  271.6 2.4 copy.429
  274.1 7.7 %fusion.145 = (f32[8,512]{1,0:T(8,128)S(1)}, f32[8,512,512]{1,2,0:T(8,128)}) fusion(bf16[512,8,128]{0,2,1:T(8,128)(2,1)} %bitcast.754, bf16[512,8,128]{0,2,1:T(8,128)(2,1)} %bitcast.756), kind=kOutput, calls=%fused_computation.325 | convolution fusion | flops 543162880 | bytes 10502144 | tf_op jit(solution)/shard_map/sub | solution.py:322
  281.8 4.7 divide_convert_fusion
  286.5 2.1 bitcast_convert_fusion.2
  293.7 2.7 fusion.50
  296.4 3.3 fusion.30
  299.7 2.8 reshape_reshape.22
  302.5 4.2 fusion.39
  309.8 2.3 bitcast_convert_fusion.1
  312.1 2.3 copy.293
  314.4 2.3 fusion.51
  316.8 4.9 convolution_convert_fusion.7
  322.9 2.5 multiply_convert_fusion.1
  343.4 2.8 copy.391
  347.8 2.6 convolution_convert_fusion
  350.5 2.8 convert_bitcast_fusion.1
  359.6 1.9 multiply_reduce_fusion.1
  363.3 1.9 convert_bitcast_fusion.4
  366.7 3.3 fusion.23
  369.9 2.0 reshape_reshape.23
  372.0 2.5 convert_bitcast_fusion.2
  379.1 2.7 convolution_convert_fusion.4
  382.6 2.5 convert_bitcast_fusion.3
  386.2 2.3 bitcast_convert_fusion
  390.1 3.9 convolution_convert_fusion.5
  395.0 11.2 %shard_map.332 = f32[512,384]{1,0:T(8,128)S(1)} custom-call(bf16[512,384]{1,0:T(8,128)(2,1)S(1)} %get-tuple-element.95.grad_ref, bf16[384,6272]{1,0:T(8,128)(2,1)} %pad.46.pixel_ref, bf16[512,6272]{1,0:T(8,128)(2,1)} %get-tuple-element.25.weights_ref, f32[512,1]{1,0:T(8,128)S(1)} %copy.316.dot_ref), custom_call_target="tpu_custom_call" | custom-call | flops 4932501504 | bytes 12421120 | tf_op jit(solution)/shard_map/pallas_call | solution.py:439
  406.7 3.2 reshape.663
  409.9 2.5 convert_bitcast_fusion
  418.1 2.6 convolution_convert_fusion.6
  421.9 2.7 convolution_convert_fusion.1
  437.2 2.0 constant_dynamic-update-slice_fusion.17
  448.7 1.8 constant_dynamic-update-slice_fusion.11
  453.4 143.0 %reduce-scatter.3.cloned.1.call-done = bf16[11136,128]{1,0:T(8,128)(2,1)} async-done(((bf16[89088,128]{1,0:T(8,128)(2,1)}), bf16[11136,128]{1,0:T(8,128)(2,1)}) %reduce-scatter.3.cloned.1.call-update) | async-done | bytes 2850832 | tf_op jit(solution)/shard_map/reduce_scatter | solution.py:240
  596.5 4.1 copy.286
  600.6 4.3 fusion.49
  604.9 2.2 add_add_fusion.4
  607.1 47.5 %reduce-scatter.5.cloned.1.call-done = bf16[2784,128]{1,0:T(8,128)(2,1)} async-done(((bf16[11136,128]{1,0:T(8,128)(2,1)}), bf16[2784,128]{1,0:T(8,128)(2,1)}) %reduce-scatter.5.cloned.1.call-update) | async-done | bytes 712720 | tf_op jit(solution)/shard_map/reduce_scatter | solution.py:243
  658.0 1.9 slice_convert_fusion.2
  (374 shorter events, 121.3 us)
Async XLA Ops:
  7.2 9.7 %copy-start.92 = (f32[256,128]{1,0:T(8,128)S(1)}, f32[256,128]{1,0:T(8,128)}, u32[]{:S(2)}) copy-start(f32[256,128]{1,0:T(8,128)} %param.29) | copy-start | bytes 393220
  7.2 9.8 %copy-start.93 = (f32[256,128]{1,0:T(8,128)S(1)}, f32[256,128]{1,0:T(8,128)}, u32[]{:S(2)}) copy-start(f32[256,128]{1,0:T(8,128)} %param.33) | copy-start | bytes 393220
  7.2 9.9 %copy-start.94 = (f32[256,128]{1,0:T(8,128)S(1)}, f32[256,128]{1,0:T(8,128)}, u32[]{:S(2)}) copy-start(f32[256,128]{1,0:T(8,128)} %param.35) | copy-start | bytes 393220
  7.2 156.3 %all-gather.2.cloned.1.call-start = ((), (), s32[]{:S(2)}) async-start(), calls=%async_computation.2 | async-start | bytes 23519232 | tf_op jit(solution)/shard_map/all_gather | solution.py:214
  8.2 10.0 %copy-start.95 = (s32[1,16384]{1,0:T(1,128)S(1)}, s32[1,16384]{1,0:T(1,128)}, u32[]{:S(2)}) copy-start(s32[1,16384]{1,0:T(1,128)} %param.22) | copy-start | bytes 196612
  18.1 578.4 %reduce-scatter.3.cloned.1.call-start = ((), (), s32[]{:S(2)}) async-start(), calls=%async_computation.3 | async-start | bytes 25657344 | tf_op jit(solution)/shard_map/reduce_scatter | solution.py:240
  32.7 2.6 copy-start.3
  35.6 146.7 %copy-start.98 = (f32[512]{0:T(512)}, f32[512]{0:T(512)S(1)}, u32[]{:S(2)}) copy-start(f32[512]{0:T(512)S(1)} %broadcast_multiply_fusion.4) | copy-start | bytes 6148
  36.0 130.8 %copy-start.102 = (f32[512]{0:T(512)}, f32[512]{0:T(512)S(1)}, u32[]{:S(2)}) copy-start(f32[512]{0:T(512)S(1)} %fusion.31) | copy-start | bytes 6148
  36.1 146.2 %copy-start.100 = (f32[512]{0:T(512)}, f32[512]{0:T(512)S(1)}, u32[]{:S(2)}) copy-start(f32[512]{0:T(512)S(1)} %fusion.131) | copy-start | bytes 6148
  166.8 17.2 %copy-start.59 = (bf16[32,96,128]{2,1,0:T(8,128)(2,1)}, bf16[32,96,128]{2,1,0:T(8,128)(2,1)S(1)}, u32[]{:S(2)}) copy-start(bf16[32,96,128]{2,1,0:T(8,128)(2,1)S(1)} %get-tuple-element.60) | copy-start | bytes 2359300
  199.9 2.4 copy-start
  212.5 4.6 copy-start.36
  214.4 3.4 copy-start.51
  221.5 3.3 copy-start.80
  224.9 5.6 copy-start.12
  225.2 2.3 copy-start.68
  227.6 2.9 copy-start.67
  260.5 4.4 copy-start.75
  260.5 4.4 copy-start.76
  264.8 2.3 copy-start.74
  281.8 4.7 copy-start.45
  286.5 2.8 copy-start.1
  286.5 3.1 copy-start.70
  291.3 2.3 copy-start.69
  293.7 2.7 copy-start.24
  293.7 2.7 copy-start.47
  302.5 4.3 copy-start.10
  314.4 2.3 copy-start.19
  316.7 4.9 copy-start.2
  316.8 4.9 copy-start.46
  322.9 2.5 copy-start.43
  325.4 2.7 copy-start.27
  332.1 2.3 copy-start.7
  334.5 2.3 copy-start.6
  336.8 2.3 copy-start.5
  353.3 2.3 copy-start.72
  353.3 2.6 copy-start.86
  363.3 2.8 copy-start.25
  363.3 3.3 copy-start.105
  369.9 2.1 copy-start.82
  374.5 2.3 copy-start.13
  374.5 3.0 copy-start.66
  382.5 2.7 copy-start.14
  382.6 3.5 copy-start.64
  390.1 3.9 copy-start.60
  390.1 3.9 copy-start.104
  406.5 3.4 copy-start.50
  406.5 8.2 %copy-start.53 = (bf16[512,384]{0,1:T(8,128)(2,1)}, bf16[512,384]{0,1:T(8,128)(2,1)S(1)}, u32[]{:S(2)}) copy-start(bf16[512,384]{0,1:T(8,128)(2,1)S(1)} %pad.51.clone) | copy-start | bytes 1179652
  406.7 7.2 %copy-start.57 = (bf16[512,384]{0,1:T(8,128)(2,1)}, bf16[512,384]{0,1:T(8,128)(2,1)S(1)}, u32[]{:S(2)}) copy-start(bf16[512,384]{0,1:T(8,128)(2,1)S(1)} %pad.50.clone) | copy-start | bytes 1179652
  418.0 2.6 copy-start.32
  418.1 2.6 copy-start.101
  421.9 2.7 copy-start.81
  421.9 2.7 copy-start.85
  432.8 2.1 copy-start.65
  434.9 2.2 copy-start.21
  444.2 2.2 copy-start.29
  446.4 2.2 copy-start.20
  448.7 2.2 copy-start.31
  453.4 201.3 %reduce-scatter.5.cloned.1.call-start = ((), (), s32[]{:S(2)}) async-start(), calls=%async_computation.4 | async-start | bytes 3563520 | tf_op jit(solution)/shard_map/reduce_scatter | solution.py:243
  596.5 4.1 copy-start.11
  600.6 4.3 copy-start.15
  600.6 4.3 copy-start.16
  600.6 4.3 copy-start.33
  (45 other events, 67.2 us)
Sparse Core Ops, SparseCore 0:
  18.2 145.3 all-gather.1
  453.5 142.9 reduce-scatter.2
  598.8 55.7 reduce-scatter.4

commit v13 on v11

--- a/solution.py
+++ b/solution.py
@@ -321,7 +321,7 @@
     row_top = jnp.max(scores, axis=-1, keepdims=True)
     raw_weights = jnp.exp(scores - row_top)
     row_total = jnp.sum(raw_weights, axis=-1, keepdims=True)
-    weights_low = rounded(raw_weights / row_total)
+    weights_low = rounded(raw_weights * (1.0 / row_total))
     mixed_full = jnp.einsum("hqk,khd->qhd", weights_low, v4, preferred_element_type=jnp.float32)
     mixed = rounded(mixed_full.reshape(rows, heads_n * HEAD))
     saved = (normed, q4, k4, v4, weights_low, mixed_full, mixed)
@@ -381,7 +381,7 @@
     row_top = jnp.max(scores, axis=-1, keepdims=True)
     raw = jnp.exp(scores - row_top)
     row_total = jnp.sum(raw, axis=-1, keepdims=True)
-    weights = (raw / row_total).astype(jnp.bfloat16)
+    weights = (raw * (1.0 / row_total)).astype(jnp.bfloat16)
     weights_ref[...] = weights
     mix_ref[...] = lax.dot_general(
         weights, pixel_ref[...], (((1,), (1,)), ((), ())), preferred_element_type=jnp.float32

time: 679 us -> 679 us (level)
  no operation moved by 1% of the time
where the time goes in v13:
time: 679 us; the launch traced here: 671 us
  waiting for transfers between devices  318 us (47%)
  local copies, waits for them, and re-layouts  153 us (23%)
  matrix products  105 us (15%)
  other arithmetic  55.4 us (8%)
  Pallas kernels  21.1 us (3%)
  between operations  18.1 us (3%)
    reduce_scatter x1, waiting for transfers between devices, reduce_grads(): lax.psum_scatter(packed.reshape(count * total, PANEL), 'items', scatter_d...  143 us
    all_gather x1, waiting for transfers between devices, gather_weights(): lax.all_gather(packed, ALL, axis=0, tiled=True).reshape(count, total, PANEL)  127 us
    dot_general x40, matrix products, contract(): lax.dot_general(left, right, ((left_dims, right_dims), ((), ())), preferr...  85.1 us
    unnamed x242, local copies, waits for them, and re-layouts  49.9 us
    reduce_scatter x1, waiting for transfers between devices, reduce_grads(): mine = lax.psum_scatter(mine, 'heads', scatter_dimension=0, tiled=True)  47.5 us
    dot_general x17, local copies, waits for them, and re-layouts, contract(): lax.dot_general(left, right, ((left_dims, right_dims), ((), ())), preferr...  45.9 us
    slice x2, local copies, waits for them, and re-layouts, gather_weights(): piece = gathered[:, first:first + rows, :]  17.3 us
  transfers between devices with their start and end apart: 3, of which 3 were waited for; matrix products, arithmetic and copies ran while one was open for 4% of the time, Pallas kernels for 0%

profile of v13, /device:TPU:0, one launch (start us, length us, event | category | flops | bytes accessed | tf_op | source)
XLA Modules:
  0.0 671.0 jit_solution(992182872353029041)
XLA Ops:
  21.5 3.3 convert_reduce_fusion
  24.8 3.7 fusion.4
  28.5 4.2 fusion.5
  32.8 2.5 pad.46.pixel_ref
  36.1 127.5 %all-gather.2.cloned.1.call-done = bf16[89088,128]{1,0:T(8,128)(2,1)} async-done(((bf16[2784,128]{1,0:T(8,128)(2,1)}), bf16[89088,128]{1,0:T(8,128)(2,1)}) %all-gather.2.cloned.1.call-update) | async-done | bytes 22806544 | tf_op jit(solution)/shard_map/all_gather | solution.py:214
  164.5 2.4 fusion.141
  166.8 15.0 %fusion.140 = (bf16[32,256,128]{2,1,0:T(8,128)(2,1)}, bf16[32,256,128]{2,1,0:T(8,128)(2,1)}, bf16[32,256,128]{2,1,0:T(8,128)(2,1)}, bf16[32,256,128]{2,1,0:T(8,1...) fusion(bf16[32,2784,128]{2,1,0:T(8,128)(2,1)} %bitcast.710), kind=kLoop, calls=%fused_computation.321 | loop fusion | bytes 41943040 | tf_op jit(solution)/shard_map/slice | solution.py:217
  185.0 4.2 bitcast_convert_fusion.6
  191.9 3.9 copy.268
  195.8 3.9 copy.270
  199.7 2.4 copy-done
  202.1 10.6 %shard_map.331 = (bf16[512,6272]{1,0:T(8,128)(2,1)}, f32[512,384]{1,0:T(8,128)S(1)}) custom-call(bf16[512,384]{1,0:T(8,128)(2,1)S(1)} %pad.45.keyed_ref, bf16[384,6272]{1,0:T(8,128)(2,1)S(1)} %copy-done, f32[1,6272]{1,0:T(1,128)S(1)} %compare_convert_fusion.1.mask_ref), custom_call_target="tpu_custom_call" | custom-call | flops 4932501504 | bytes 12419072 | tf_op jit(solution)/shard_map/pallas_call | solution.py:400
  219.8 1.9 copy.266
  221.7 3.3 fusion.143
  227.8 2.9 fusion.52
  235.2 2.7 reshape.658
  237.9 3.9 copy.272
  241.8 3.9 copy.274
  245.7 3.9 copy.276
  249.6 3.9 copy.282
  253.6 3.2 copy.290
  256.7 3.9 copy.284
  260.7 4.3 fusion.58
  265.0 2.3 bitcast_convert_fusion.3
  267.3 2.3 bitcast_convert_fusion.4
  269.6 2.3 copy.428
  271.9 2.4 copy.429
  274.3 7.7 %fusion.145 = (f32[8,512]{1,0:T(8,128)S(1)}, f32[8,512,512]{1,2,0:T(8,128)}) fusion(bf16[512,8,128]{0,2,1:T(8,128)(2,1)} %bitcast.754, bf16[512,8,128]{0,2,1:T(8,128)(2,1)} %bitcast.756), kind=kOutput, calls=%fused_computation.326 | convolution fusion | flops 543162880 | bytes 10502144 | tf_op jit(solution)/shard_map/sub | solution.py:322
  282.0 4.7 multiply_convert_fusion.1
  286.7 2.1 bitcast_convert_fusion.2
  293.9 2.7 fusion.50
  296.6 3.3 fusion.30
  299.9 2.8 reshape_reshape.22
  302.7 4.2 fusion.39
  310.1 2.3 bitcast_convert_fusion.1
  312.4 2.3 copy.293
  314.7 2.3 fusion.51
  317.0 4.9 convolution_convert_fusion.7
  323.1 2.5 multiply_convert_fusion.2
  343.6 2.8 copy.391
  348.0 2.6 convolution_convert_fusion
  350.7 2.8 convert_bitcast_fusion.1
  359.8 1.9 multiply_reduce_fusion.1
  363.6 1.9 convert_bitcast_fusion.4
  366.9 3.3 fusion.23
  370.2 2.0 reshape_reshape.23
  372.2 2.5 convert_bitcast_fusion.2
  379.3 2.7 convolution_convert_fusion.4
  382.9 2.5 convert_bitcast_fusion.3
  386.4 2.3 bitcast_convert_fusion
  390.3 3.9 convolution_convert_fusion.5
  395.3 10.5 %shard_map.332 = f32[512,384]{1,0:T(8,128)S(1)} custom-call(bf16[512,384]{1,0:T(8,128)(2,1)S(1)} %get-tuple-element.95.grad_ref, bf16[384,6272]{1,0:T(8,128)(2,1)} %pad.46.pixel_ref, bf16[512,6272]{1,0:T(8,128)(2,1)} %get-tuple-element.25.weights_ref, f32[512,1]{1,0:T(8,128)S(1)} %copy.316.dot_ref), custom_call_target="tpu_custom_call" | custom-call | flops 4932501504 | bytes 12421120 | tf_op jit(solution)/shard_map/pallas_call | solution.py:439
  406.3 3.2 reshape.666
  409.4 2.5 convert_bitcast_fusion
  417.6 2.6 convolution_convert_fusion.6
  421.5 2.7 convolution_convert_fusion.1
  436.7 2.0 constant_dynamic-update-slice_fusion.17
  448.2 1.8 constant_dynamic-update-slice_fusion.11
  453.0 143.0 %reduce-scatter.3.cloned.1.call-done = bf16[11136,128]{1,0:T(8,128)(2,1)} async-done(((bf16[89088,128]{1,0:T(8,128)(2,1)}), bf16[11136,128]{1,0:T(8,128)(2,1)}) %reduce-scatter.3.cloned.1.call-update) | async-done | bytes 2850832 | tf_op jit(solution)/shard_map/reduce_scatter | solution.py:240
  596.1 4.1 copy.286
  600.2 4.3 fusion.49
  604.5 2.2 add_add_fusion.4
  606.7 47.5 %reduce-scatter.5.cloned.1.call-done = bf16[2784,128]{1,0:T(8,128)(2,1)} async-done(((bf16[11136,128]{1,0:T(8,128)(2,1)}), bf16[2784,128]{1,0:T(8,128)(2,1)}) %reduce-scatter.5.cloned.1.call-update) | async-done | bytes 712720 | tf_op jit(solution)/shard_map/reduce_scatter | solution.py:243
  657.5 1.9 slice_convert_fusion.2
  (375 shorter events, 121.3 us)
Async XLA Ops:
  7.2 9.7 %copy-start.92 = (f32[256,128]{1,0:T(8,128)S(1)}, f32[256,128]{1,0:T(8,128)}, u32[]{:S(2)}) copy-start(f32[256,128]{1,0:T(8,128)} %param.29) | copy-start | bytes 393220
  7.2 9.8 %copy-start.93 = (f32[256,128]{1,0:T(8,128)S(1)}, f32[256,128]{1,0:T(8,128)}, u32[]{:S(2)}) copy-start(f32[256,128]{1,0:T(8,128)} %param.33) | copy-start | bytes 393220
  7.2 9.9 %copy-start.94 = (f32[256,128]{1,0:T(8,128)S(1)}, f32[256,128]{1,0:T(8,128)}, u32[]{:S(2)}) copy-start(f32[256,128]{1,0:T(8,128)} %param.35) | copy-start | bytes 393220
  7.2 156.3 %all-gather.2.cloned.1.call-start = ((), (), s32[]{:S(2)}) async-start(), calls=%async_computation.2 | async-start | bytes 23519232 | tf_op jit(solution)/shard_map/all_gather | solution.py:214
  8.2 10.0 %copy-start.95 = (s32[1,16384]{1,0:T(1,128)S(1)}, s32[1,16384]{1,0:T(1,128)}, u32[]{:S(2)}) copy-start(s32[1,16384]{1,0:T(1,128)} %param.22) | copy-start | bytes 196612
  18.1 578.0 %reduce-scatter.3.cloned.1.call-start = ((), (), s32[]{:S(2)}) async-start(), calls=%async_computation.3 | async-start | bytes 25657344 | tf_op jit(solution)/shard_map/reduce_scatter | solution.py:240
  32.7 2.6 copy-start.3
  35.6 146.7 %copy-start.98 = (f32[512]{0:T(512)}, f32[512]{0:T(512)S(1)}, u32[]{:S(2)}) copy-start(f32[512]{0:T(512)S(1)} %broadcast_multiply_fusion.4) | copy-start | bytes 6148
  36.0 130.8 %copy-start.102 = (f32[512]{0:T(512)}, f32[512]{0:T(512)S(1)}, u32[]{:S(2)}) copy-start(f32[512]{0:T(512)S(1)} %fusion.31) | copy-start | bytes 6148
  36.1 146.2 %copy-start.100 = (f32[512]{0:T(512)}, f32[512]{0:T(512)S(1)}, u32[]{:S(2)}) copy-start(f32[512]{0:T(512)S(1)} %fusion.131) | copy-start | bytes 6148
  166.8 17.2 %copy-start.59 = (bf16[32,96,128]{2,1,0:T(8,128)(2,1)}, bf16[32,96,128]{2,1,0:T(8,128)(2,1)S(1)}, u32[]{:S(2)}) copy-start(bf16[32,96,128]{2,1,0:T(8,128)(2,1)S(1)} %get-tuple-element.60) | copy-start | bytes 2359300
  199.7 2.4 copy-start
  212.7 4.6 copy-start.36
  214.6 3.4 copy-start.51
  221.7 3.3 copy-start.80
  225.1 5.6 copy-start.12
  225.4 2.3 copy-start.69
  227.8 2.9 copy-start.67
  260.7 4.4 copy-start.75
  260.7 4.4 copy-start.76
  265.0 2.3 copy-start.74
  282.0 4.7 copy-start.45
  286.7 2.8 copy-start.1
  286.7 3.1 copy-start.70
  291.6 2.4 copy-start.68
  293.9 2.7 copy-start.24
  293.9 2.7 copy-start.47
  302.7 4.3 copy-start.10
  314.7 2.3 copy-start.19
  317.0 4.9 copy-start.2
  317.0 4.9 copy-start.46
  323.1 2.5 copy-start.43
  325.6 2.7 copy-start.27
  332.4 2.3 copy-start.7
  334.7 2.3 copy-start.6
  337.1 2.3 copy-start.5
  353.5 2.3 copy-start.72
  353.5 2.6 copy-start.86
  363.6 2.8 copy-start.25
  363.6 3.3 copy-start.105
  370.2 2.1 copy-start.82
  374.8 2.3 copy-start.13
  374.8 3.0 copy-start.66
  382.7 2.7 copy-start.14
  382.9 3.5 copy-start.64
  390.3 3.9 copy-start.60
  390.3 3.9 copy-start.104
  406.0 3.4 copy-start.50
  406.1 8.2 %copy-start.53 = (bf16[512,384]{0,1:T(8,128)(2,1)}, bf16[512,384]{0,1:T(8,128)(2,1)S(1)}, u32[]{:S(2)}) copy-start(bf16[512,384]{0,1:T(8,128)(2,1)S(1)} %pad.51.clone) | copy-start | bytes 1179652
  406.3 7.2 %copy-start.57 = (bf16[512,384]{0,1:T(8,128)(2,1)}, bf16[512,384]{0,1:T(8,128)(2,1)S(1)}, u32[]{:S(2)}) copy-start(bf16[512,384]{0,1:T(8,128)(2,1)S(1)} %pad.50.clone) | copy-start | bytes 1179652
  417.6 2.6 copy-start.32
  417.6 2.6 copy-start.101
  421.5 2.7 copy-start.81
  421.5 2.7 copy-start.85
  432.4 2.1 copy-start.65
  434.5 2.2 copy-start.21
  443.8 2.2 copy-start.29
  446.0 2.2 copy-start.20
  448.2 2.2 copy-start.31
  452.9 201.3 %reduce-scatter.5.cloned.1.call-start = ((), (), s32[]{:S(2)}) async-start(), calls=%async_computation.4 | async-start | bytes 3563520 | tf_op jit(solution)/shard_map/reduce_scatter | solution.py:243
  596.0 4.1 copy-start.11
  600.1 4.3 copy-start.15
  600.1 4.3 copy-start.16
  600.1 4.3 copy-start.33
  (45 other events, 67.2 us)
Sparse Core Ops, SparseCore 0:
  18.2 145.3 all-gather.1
  453.0 142.9 reduce-scatter.2
  598.4 55.7 reduce-scatter.4
